TPU v7x, 512 devices: a whole 4x8x8 slice. The times are simulated.
512 devices in a mesh: gx: 32 (over x_lo, y, core), gy: 16 (over z, x_hi).
Axes of the slice: x: 4 (x_hi: 2, x_lo: 2; x = x_hi * 2 + x_lo), y: 8, z: 8, core: 2. Of those that a mesh axis runs over, the one named last changes fastest.
Arguments:
- probe_signs: int32 [32, 64, 256, 128], P(None, 'gx', 'gy'), may hold values from 0 to 1
- diagonal: float32 [64, 256, 128], P('gx', 'gy'), may hold values from 0.25 to 4
Outputs:
- diagonal_blocks: float32 [3, 32, 32], replicated
- offdiag_blocks: float32 [3, 32, 32], replicated
- next_block: float32 [32, 64, 256, 128], P(None, 'gx', 'gy')
All inputs are finite; a program needn't handle non-finite values.
Results may differ from a plain program's by a relative error of at most 0.0006.
Values sent between devices are 32-bit elements; how exact they have to be, the bound alone decides.
No kernel may reach another device: no remote copies, remote signals or barrier semaphores. Data moves between devices by JAX's collectives and lax.ppermute only.
A program may use at most 64 MiB of HBM per device.

v0:
```python
import jax
import jax.numpy as jnp
from jax import lax
from jax.sharding import Mesh
from jax.sharding import PartitionSpec as P

ITERS = 3
GX_GY = ("gx_0", "gx_1", "gx_2", "gy_0", "gy_1")
GX = ("gx_0", "gx_1", "gx_2")
GY = ("gy_0", "gy_1")


def with_halo(block, sides, width):
    for axis, dim in sides:
        count = lax.axis_size(axis)
        forward = [(i, i + 1) for i in range(count - 1)]
        forward.append((count - 1, 0))
        backward = [(target, source) for source, target in forward]
        low = lax.ppermute(
            lax.slice_in_dim(block, block.shape[dim] - width, None, axis=dim), axis, forward
        )
        high = lax.ppermute(lax.slice_in_dim(block, 0, width, axis=dim), axis, backward)
        block = jnp.concatenate([low, block, high], axis=dim)
    return block


def by_axis(x, axes):
    for axis in axes:
        x = lax.psum(x, axis)
    return x


def stencil(vectors, diagonal):
    padded = with_halo(vectors, ((GX, 1), (GY, 2)), 1)
    beside = padded[:, 2:, 1:-1] + padded[:, :-2, 1:-1] + padded[:, 1:-1, 2:] + padded[:, 1:-1, :-2]
    beside = beside + jnp.roll(vectors, 1, 3) + jnp.roll(vectors, -1, 3)
    return (6.0 + diagonal)[None] * vectors - beside


def inner_block(left, right):
    return jnp.einsum("pxyz,qxyz->pq", left, right, precision=lax.Precision.HIGHEST)


def combine(vectors, matrix):
    return jnp.einsum("pxyz,pq->qxyz", vectors, matrix, precision=lax.Precision.HIGHEST)


def small_product(left, right):
    return jnp.dot(left, right, precision=lax.Precision.HIGHEST)


def inverse_lower(gram_matrix):
    lower_factor = jnp.linalg.cholesky(gram_matrix)
    identity_matrix = jnp.eye(gram_matrix.shape[0], dtype=gram_matrix.dtype)
    inverse = lax.linalg.triangular_solve(lower_factor, identity_matrix, left_side=True, lower=True)
    return (lower_factor, inverse)


def per_device(probe_signs, diagonal):
    total_cells = (
        probe_signs.shape[1]
        * lax.axis_size(GX)
        * probe_signs.shape[2]
        * lax.axis_size(GY)
        * probe_signs.shape[3]
    )
    scale_factor = 1.0 / jnp.sqrt(jnp.float32(total_cells))
    probes = (2.0 * probe_signs.astype(jnp.float32) - 1.0) * scale_factor
    have_start = False
    first_image = None
    first_projected = None
    first_gram = None
    probe_image = stencil(probes, diagonal)
    probe_matrix, cross_matrix, image_matrix = (
        by_axis(inner_block(probes, probes), GX_GY),
        by_axis(inner_block(probes, probe_image), GX_GY),
        by_axis(inner_block(probe_image, probe_image), GX_GY),
    )
    lower_factor, inverse = inverse_lower(probe_matrix)
    current = combine(probes, inverse.T)
    first_image = combine(probe_image, inverse.T)
    first_projected = small_product(small_product(inverse, cross_matrix), inverse.T)
    first_gram = small_product(small_product(inverse, image_matrix), inverse.T) - small_product(
        first_projected.T, first_projected
    )
    have_start = True
    previous = None
    coupling = None
    alphas = []
    betas = []
    for iteration in range(ITERS):
        if iteration == 0 and have_start:
            image = first_image
            projected = first_projected
            remain = image - combine(current, projected)
            remain_gram = first_gram
        else:
            image = stencil(current, diagonal)
            image = image - combine(previous, coupling)
            projected, image_gram = (
                by_axis(inner_block(current, image), GX_GY),
                by_axis(inner_block(image, image), GX_GY),
            )
            remain = image - combine(current, projected)
            remain_gram = image_gram - small_product(projected.T, projected)
        lower_factor, inverse = inverse_lower(remain_gram)
        alphas.append(projected)
        betas.append(lower_factor.T)
        previous = current
        coupling = lower_factor
        current = combine(remain, inverse.T)
    return (jnp.stack(alphas), jnp.stack(betas), current)


def solution(mesh):
    split = Mesh(mesh.devices.reshape(2, 8, 2, 8, 2), ("gx_0", "gx_1", "gx_2", "gy_0", "gy_1"))
    placed = (P(None, GX, GY, None), P(GX, GY, None))
    return jax.shard_map(
        per_device,
        mesh=split,
        in_specs=placed,
        out_specs=(P(), P(), P(None, GX, GY, None)),
        check_vma=False,
    )
```

profile of v0, /device:TPU:6, one launch (start us, length us, event | category | flops | bytes accessed | tf_op | source)
XLA Modules:
  0.0 362.1 jit_solution(11180302722896008968)
XLA Ops:
  0.6 1.1 fusion.18
  1.8 1.9 collective-permute-start.1
  3.7 5.8 %collective-permute-start = (f32[32,1,16,128]{3,2,1,0:T(8,128)S(1)}, f32[32,1,16,128]{3,2,1,0:T(8,128)S(1)}, u32[]{:S(2)}, u32[]{:S(2)}) collective-permute-start(f32[32,1,16,128]{3,2,1,0:T(8,128)S(1)} %get-tuple-element.66), channel_id=1, source_target_pairs={{16,0},{32,16},{48,32},{64,48},{80,64},{96,80},{112,96},{128,112},... | collective-permute-start | bytes 786440 | tf_op jit(solution)/shard_map/ppermute | solution.py:22
  9.9 1.7 collective-permute-done.1
  11.6 1.8 collective-permute-done
  13.5 3.4 collective-permute-start.2
  16.9 4.9 %collective-permute-start.3 = (f32[32,4,1,128]{3,2,1,0:T(1,128)S(1)}, f32[32,4,1,128]{3,2,1,0:T(1,128)S(1)}, u32[]{:S(2)}, u32[]{:S(2)}) collective-permute-start(f32[32,4,1,128]{3,2,1,0:T(1,128)S(1)} %get-tuple-element.48), channel_id=1, source_target_pairs={{0,1},{1,2},{2,3},{3,4},{4,5},{5,6},{6,7},{7,8},{8,9},{9,10},{10,1... | collective-permute-start | bytes 196616 | tf_op jit(solution)/shard_map/ppermute | solution.py:19
  21.9 0.8 convolution_bitcast_fusion.9
  22.7 9.0 %collective-permute-done.3 = f32[32,4,1,128]{3,2,1,0:T(1,128)S(1)} collective-permute-done((f32[32,4,1,128]{3,2,1,0:T(1,128)S(1)}, f32[32,4,1,128]{3,2,1,0:T(1,128)S(1)}, u32[]{:S(2)}, u32[]{:S(2)}) %collective-permute-start.3) | collective-permute-done | bytes 65568 | tf_op jit(solution)/shard_map/ppermute | solution.py:19
  32.2 0.8 convolution_bitcast_fusion.7
  33.0 1.1 convolution_bitcast_fusion.8
  34.2 8.0 %all-reduce.14 = (f32[32,32]{0,1:T(8,128)S(1)}, f32[32,32]{1,0:T(8,128)S(1)}, f32[32,32]{1,0:T(8,128)S(1)}) all-reduce(f32[32,32]{0,1:T(8,128)S(1)} %convolution_bitcast_fusion.9, f32[32,32]{1,0:T(8,128)S(1)} %convolution_bitcast_fusion.7, ...), channel_id=1, replica_groups=mesh['gx_0'=2,'gx_1'=8,'gx_2'=2,'gy_0'=8,'gy_1'=2] {'gx_0'}, use_global_device_ids=true, to_apply=%region_0.1 | all-reduce | flops 3072 | bytes 24576 | tf_op jit(solution)/shard_map/psum | solution.py:29
  42.1 28.9 %all-reduce.5 = (f32[32,32]{0,1:T(8,128)S(1)}, f32[32,32]{1,0:T(8,128)S(1)}, f32[32,32]{1,0:T(8,128)S(1)}) all-reduce(f32[32,32]{0,1:T(8,128)S(1)} %get-tuple-element.40, f32[32,32]{1,0:T(8,128)S(1)} %get-tuple-element.41, f32[32,32]{1,0:T(8,128)S(1)} %get-tuple-element.42), channel_id=1, replica_groups=mesh['gx_0'=2,'gx_1'=8,'gx_2'=2,'gy_0'=8,'gy_1'=2] {'gx_1'}, use_global_device_ids=true, to_apply=%region_1.2 | all-reduce | flops 3072 | bytes 24576 | tf_op jit(solution)/shard_map/psum | solution.py:29
  71.0 3.6 all-reduce.11
  74.6 29.6 %all-reduce.2 = (f32[32,32]{0,1:T(8,128)S(1)}, f32[32,32]{1,0:T(8,128)S(1)}, f32[32,32]{1,0:T(8,128)S(1)}) all-reduce(f32[32,32]{0,1:T(8,128)S(1)} %get-tuple-element.33, f32[32,32]{1,0:T(8,128)S(1)} %get-tuple-element.34, f32[32,32]{1,0:T(8,128)S(1)} %get-tuple-element.35), channel_id=1, replica_groups=mesh['gx_0'=2,'gx_1'=8,'gx_2'=2,'gy_0'=8,'gy_1'=2] {'gy_0'}, use_global_device_ids=true, to_apply=%region_3.4 | all-reduce | flops 3072 | bytes 24576 | tf_op jit(solution)/shard_map/psum | solution.py:29
  104.2 12.6 %all-reduce.8 = (f32[32,32]{0,1:T(8,128)S(1)}, f32[32,32]{1,0:T(8,128)S(1)}, f32[32,32]{1,0:T(8,128)S(1)}) all-reduce(f32[32,32]{0,1:T(8,128)S(1)} %get-tuple-element.12, f32[32,32]{1,0:T(8,128)S(1)} %get-tuple-element.13, f32[32,32]{1,0:T(8,128)S(1)} %get-tuple-element.14), channel_id=1, replica_groups=mesh['gx_0'=2,'gx_1'=8,'gx_2'=2,'gy_0'=8,'gy_1'=2] {'gy_1'}, use_global_device_ids=true, to_apply=%region_4.5 | all-reduce | flops 3072 | bytes 24576 | tf_op jit(solution)/shard_map/psum | solution.py:29
  116.9 2.9 cholesky.74
  119.8 0.6 compare_reduce_fusion.3
  120.5 0.7 fusion.32
  121.1 2.4 custom-call.8
  123.8 0.9 fusion.23
  124.7 0.9 fusion.19
  126.5 2.9 cholesky.85
  129.4 0.6 compare_reduce_fusion.2
  130.1 0.7 fusion.49
  130.7 2.4 custom-call.9
  134.7 1.9 collective-permute-start.5
  136.6 5.8 %collective-permute-start.4 = (f32[32,1,16,128]{3,0,2,1:T(8,128)S(1)}, f32[32,1,16,128]{3,0,2,1:T(8,128)S(1)}, u32[]{:S(2)}, u32[]{:S(2)}) collective-permute-start(f32[32,1,16,128]{3,0,2,1:T(8,128)S(1)} %get-tuple-element.60), channel_id=1, source_target_pairs={{16,0},{32,16},{48,32},{64,48},{80,64},{96,80},{112,96},{128,112},... | collective-permute-start | bytes 786440 | tf_op jit(solution)/shard_map/ppermute | solution.py:22
  142.6 1.9 collective-permute-done.5
  144.5 1.8 collective-permute-done.4
  146.2 1.9 collective-permute-start.6
  148.2 6.5 %collective-permute-start.7 = (f32[32,4,1,128]{3,0,2,1:T(8,128)S(1)}, f32[32,4,1,128]{3,0,2,1:T(8,128)S(1)}, u32[]{:S(2)}, u32[]{:S(2)}) collective-permute-start(f32[32,4,1,128]{3,0,2,1:T(8,128)S(1)} %get-tuple-element.46), channel_id=1, source_target_pairs={{0,1},{1,2},{2,3},{3,4},{4,5},{5,6},{6,7},{7,8},{8,9},{9,10},{10,1... | collective-permute-start | bytes 196616 | tf_op jit(solution)/shard_map/ppermute | solution.py:19
  154.9 2.3 collective-permute-done.7
  157.2 1.6 convolution_subtract_fusion.3
  159.9 7.1 %all-reduce.13 = (f32[32,32]{0,1:T(8,128)S(1)}, f32[32,32]{1,0:T(8,128)S(1)}) all-reduce(f32[32,32]{0,1:T(8,128)S(1)} %convolution_bitcast_fusion.4, f32[32,32]{1,0:T(8,128)S(1)} %convolution_bitcast_fusion.5), channel_id=1, replica_groups=mesh['gx_0'=2,'gx_1'=8,'gx_2'=2,'gy_0'=8,'gy_1'=2] {'gx_0'}, use_global_device_ids=true, to_apply=%region_22.25 | all-reduce | flops 2048 | bytes 16384 | tf_op jit(solution)/shard_map/psum | solution.py:29
  166.9 27.2 %all-reduce.4 = (f32[32,32]{0,1:T(8,128)S(1)}, f32[32,32]{1,0:T(8,128)S(1)}) all-reduce(f32[32,32]{0,1:T(8,128)S(1)} %get-tuple-element.38, f32[32,32]{1,0:T(8,128)S(1)} %get-tuple-element.39), channel_id=1, replica_groups=mesh['gx_0'=2,'gx_1'=8,'gx_2'=2,'gy_0'=8,'gy_1'=2] {'gx_1'}, use_global_device_ids=true, to_apply=%region_23.26 | all-reduce | flops 2048 | bytes 16384 | tf_op jit(solution)/shard_map/psum | solution.py:29
  194.1 3.4 all-reduce.10
  197.5 29.1 %all-reduce.1 = (f32[32,32]{0,1:T(8,128)S(1)}, f32[32,32]{1,0:T(8,128)S(1)}) all-reduce(f32[32,32]{0,1:T(8,128)S(1)} %get-tuple-element.31, f32[32,32]{1,0:T(8,128)S(1)} %get-tuple-element.32), channel_id=1, replica_groups=mesh['gx_0'=2,'gx_1'=8,'gx_2'=2,'gy_0'=8,'gy_1'=2] {'gy_0'}, use_global_device_ids=true, to_apply=%region_25.28 | all-reduce | flops 2048 | bytes 16384 | tf_op jit(solution)/shard_map/psum | solution.py:29
  226.6 12.4 %all-reduce.7 = (f32[32,32]{0,1:T(8,128)S(1)}, f32[32,32]{1,0:T(8,128)S(1)}) all-reduce(f32[32,32]{0,1:T(8,128)S(1)} %get-tuple-element.10, f32[32,32]{1,0:T(8,128)S(1)} %get-tuple-element.11), channel_id=1, replica_groups=mesh['gx_0'=2,'gx_1'=8,'gx_2'=2,'gy_0'=8,'gy_1'=2] {'gy_1'}, use_global_device_ids=true, to_apply=%region_26.29 | all-reduce | flops 2048 | bytes 16384 | tf_op jit(solution)/shard_map/psum | solution.py:29
  240.0 2.9 cholesky.96
  243.0 0.6 compare_reduce_fusion.1
  243.6 0.7 fusion.50
  244.3 2.4 custom-call.10
  247.6 1.9 collective-permute-start.9
  249.5 5.8 %collective-permute-start.8 = (f32[32,1,16,128]{3,0,2,1:T(8,128)S(1)}, f32[32,1,16,128]{3,0,2,1:T(8,128)S(1)}, u32[]{:S(2)}, u32[]{:S(2)}) collective-permute-start(f32[32,1,16,128]{3,0,2,1:T(8,128)S(1)} %get-tuple-element.54), channel_id=1, source_target_pairs={{16,0},{32,16},{48,32},{64,48},{80,64},{96,80},{112,96},{128,112},... | collective-permute-start | bytes 786440 | tf_op jit(solution)/shard_map/ppermute | solution.py:22
  255.5 1.9 collective-permute-done.9
  257.4 1.8 collective-permute-done.8
  259.1 2.0 collective-permute-start.10
  261.1 6.3 %collective-permute-start.11 = (f32[32,4,1,128]{3,0,2,1:T(8,128)S(1)}, f32[32,4,1,128]{3,0,2,1:T(8,128)S(1)}, u32[]{:S(2)}, u32[]{:S(2)}) collective-permute-start(f32[32,4,1,128]{3,0,2,1:T(8,128)S(1)} %get-tuple-element.44), channel_id=1, source_target_pairs={{0,1},{1,2},{2,3},{3,4},{4,5},{5,6},{6,7},{7,8},{8,9},{9,10},{10,1... | collective-permute-start | bytes 196616 | tf_op jit(solution)/shard_map/ppermute | solution.py:19
  267.7 1.6 collective-permute-done.11
  269.3 1.6 convolution_subtract_fusion.1
  272.0 7.6 %all-reduce.12 = (f32[32,32]{1,0:T(8,128)S(1)}, f32[32,32]{0,1:T(8,128)S(1)}) all-reduce(f32[32,32]{1,0:T(8,128)S(1)} %convolution_bitcast_fusion.2, f32[32,32]{0,1:T(8,128)S(1)} %convolution_bitcast_fusion.1), channel_id=1, replica_groups=mesh['gx_0'=2,'gx_1'=8,'gx_2'=2,'gy_0'=8,'gy_1'=2] {'gx_0'}, use_global_device_ids=true, to_apply=%region_27.30 | all-reduce | flops 2048 | bytes 16384 | tf_op jit(solution)/shard_map/psum | solution.py:29
  279.6 27.1 %all-reduce.3 = (f32[32,32]{1,0:T(8,128)S(1)}, f32[32,32]{0,1:T(8,128)S(1)}) all-reduce(f32[32,32]{1,0:T(8,128)S(1)} %get-tuple-element.36, f32[32,32]{0,1:T(8,128)S(1)} %get-tuple-element.37), channel_id=1, replica_groups=mesh['gx_0'=2,'gx_1'=8,'gx_2'=2,'gy_0'=8,'gy_1'=2] {'gx_1'}, use_global_device_ids=true, to_apply=%region_28.31 | all-reduce | flops 2048 | bytes 16384 | tf_op jit(solution)/shard_map/psum | solution.py:29
  306.7 3.4 all-reduce.9
  310.1 28.6 %all-reduce = (f32[32,32]{1,0:T(8,128)S(1)}, f32[32,32]{0,1:T(8,128)S(1)}) all-reduce(f32[32,32]{1,0:T(8,128)S(1)} %get-tuple-element.29, f32[32,32]{0,1:T(8,128)S(1)} %get-tuple-element.30), channel_id=1, replica_groups=mesh['gx_0'=2,'gx_1'=8,'gx_2'=2,'gy_0'=8,'gy_1'=2] {'gy_0'}, use_global_device_ids=true, to_apply=%region_30.33 | all-reduce | flops 2048 | bytes 16384 | tf_op jit(solution)/shard_map/psum | solution.py:29
  338.8 12.5 %all-reduce.6 = (f32[32,32]{1,0:T(8,128)S(1)}, f32[32,32]{0,1:T(8,128)S(1)}) all-reduce(f32[32,32]{1,0:T(8,128)S(1)} %get-tuple-element.8, f32[32,32]{0,1:T(8,128)S(1)} %get-tuple-element.9), channel_id=1, replica_groups=mesh['gx_0'=2,'gx_1'=8,'gx_2'=2,'gy_0'=8,'gy_1'=2] {'gy_1'}, use_global_device_ids=true, to_apply=%region_31.34 | all-reduce | flops 2048 | bytes 16384 | tf_op jit(solution)/shard_map/psum | solution.py:29
  351.2 0.6 convolution_subtract_fusion
  352.2 2.9 cholesky.107
  355.1 0.6 compare_reduce_fusion
  355.8 0.7 select_bitcast_fusion
  356.4 2.4 custom-call.11
  359.7 1.1 copy.22
  360.8 0.7 copy.21
  361.5 0.6 pad_maximum_fusion.33
  (54 shorter events, 9.9 us)
Async XLA Ops:
  1.8 9.8 %collective-permute-start.1 = (f32[32,1,16,128]{3,2,1,0:T(8,128)S(1)}, f32[32,1,16,128]{3,2,1,0:T(8,128)S(1)}, u32[]{:S(2)}, u32[]{:S(2)}) collective-permute-start(f32[32,1,16,128]{3,2,1,0:T(8,128)S(1)} %get-tuple-element.65), channel_id=1, source_target_pairs={{0,16},{16,32},{32,48},{48,64},{64,80},{80,96},{96,112},{112,128},... | collective-permute-start | bytes 786440 | tf_op jit(solution)/shard_map/ppermute | solution.py:19
  3.7 6.0 %copy-start.1 = (f32[2,16,128]{2,1,0:T(8,128)S(1)}, f32[2,16,128]{2,1,0:T(8,128)}, u32[]{:S(2)}) copy-start(f32[2,16,128]{2,1,0:T(8,128)} %param.6) | copy-start | bytes 49156
  3.7 9.6 %collective-permute-start = (f32[32,1,16,128]{3,2,1,0:T(8,128)S(1)}, f32[32,1,16,128]{3,2,1,0:T(8,128)S(1)}, u32[]{:S(2)}, u32[]{:S(2)}) collective-permute-start(f32[32,1,16,128]{3,2,1,0:T(8,128)S(1)} %get-tuple-element.66), channel_id=1, source_target_pairs={{16,0},{32,16},{48,32},{64,48},{80,64},{96,80},{112,96},{128,112},... | collective-permute-start | bytes 786440 | tf_op jit(solution)/shard_map/ppermute | solution.py:22
  13.5 18.2 %copy-start = (s32[32,2,16,128]{3,2,1,0:T(8,128)S(1)}, s32[32,2,16,128]{3,2,1,0:T(8,128)}, u32[]{:S(2)}) copy-start(s32[32,2,16,128]{3,2,1,0:T(8,128)} %param.5) | copy-start | bytes 1572868
  13.5 9.2 %collective-permute-start.2 = (f32[32,4,1,128]{3,2,1,0:T(1,128)S(1)}, f32[32,4,1,128]{3,2,1,0:T(1,128)S(1)}, u32[]{:S(2)}, u32[]{:S(2)}) collective-permute-start(f32[32,4,1,128]{3,2,1,0:T(1,128)S(1)} %get-tuple-element.47), channel_id=1, source_target_pairs={{1,0},{2,1},{3,2},{4,3},{5,4},{6,5},{7,6},{8,7},{9,8},{10,9},{11,1... | collective-permute-start | bytes 196616 | tf_op jit(solution)/shard_map/ppermute | solution.py:22
  16.9 14.7 %collective-permute-start.3 = (f32[32,4,1,128]{3,2,1,0:T(1,128)S(1)}, f32[32,4,1,128]{3,2,1,0:T(1,128)S(1)}, u32[]{:S(2)}, u32[]{:S(2)}) collective-permute-start(f32[32,4,1,128]{3,2,1,0:T(1,128)S(1)} %get-tuple-element.48), channel_id=1, source_target_pairs={{0,1},{1,2},{2,3},{3,4},{4,5},{5,6},{6,7},{7,8},{8,9},{9,10},{10,1... | collective-permute-start | bytes 196616 | tf_op jit(solution)/shard_map/ppermute | solution.py:19
  134.7 9.8 %collective-permute-start.5 = (f32[32,1,16,128]{3,0,2,1:T(8,128)S(1)}, f32[32,1,16,128]{3,0,2,1:T(8,128)S(1)}, u32[]{:S(2)}, u32[]{:S(2)}) collective-permute-start(f32[32,1,16,128]{3,0,2,1:T(8,128)S(1)} %get-tuple-element.59), channel_id=1, source_target_pairs={{0,16},{16,32},{32,48},{48,64},{64,80},{80,96},{96,112},{112,128},... | collective-permute-start | bytes 786440 | tf_op jit(solution)/shard_map/ppermute | solution.py:19
  136.6 9.6 %collective-permute-start.4 = (f32[32,1,16,128]{3,0,2,1:T(8,128)S(1)}, f32[32,1,16,128]{3,0,2,1:T(8,128)S(1)}, u32[]{:S(2)}, u32[]{:S(2)}) collective-permute-start(f32[32,1,16,128]{3,0,2,1:T(8,128)S(1)} %get-tuple-element.60), channel_id=1, source_target_pairs={{16,0},{32,16},{48,32},{64,48},{80,64},{96,80},{112,96},{128,112},... | collective-permute-start | bytes 786440 | tf_op jit(solution)/shard_map/ppermute | solution.py:22
  146.2 8.7 %collective-permute-start.6 = (f32[32,4,1,128]{3,0,2,1:T(8,128)S(1)}, f32[32,4,1,128]{3,0,2,1:T(8,128)S(1)}, u32[]{:S(2)}, u32[]{:S(2)}) collective-permute-start(f32[32,4,1,128]{3,0,2,1:T(8,128)S(1)} %get-tuple-element.45), channel_id=1, source_target_pairs={{1,0},{2,1},{3,2},{4,3},{5,4},{6,5},{7,6},{8,7},{9,8},{10,9},{11,1... | collective-permute-start | bytes 196616 | tf_op jit(solution)/shard_map/ppermute | solution.py:22
  148.2 9.0 %collective-permute-start.7 = (f32[32,4,1,128]{3,0,2,1:T(8,128)S(1)}, f32[32,4,1,128]{3,0,2,1:T(8,128)S(1)}, u32[]{:S(2)}, u32[]{:S(2)}) collective-permute-start(f32[32,4,1,128]{3,0,2,1:T(8,128)S(1)} %get-tuple-element.46), channel_id=1, source_target_pairs={{0,1},{1,2},{2,3},{3,4},{4,5},{5,6},{6,7},{7,8},{8,9},{9,10},{10,1... | collective-permute-start | bytes 196616 | tf_op jit(solution)/shard_map/ppermute | solution.py:19
  247.6 9.8 %collective-permute-start.9 = (f32[32,1,16,128]{3,0,2,1:T(8,128)S(1)}, f32[32,1,16,128]{3,0,2,1:T(8,128)S(1)}, u32[]{:S(2)}, u32[]{:S(2)}) collective-permute-start(f32[32,1,16,128]{3,0,2,1:T(8,128)S(1)} %get-tuple-element.53), channel_id=1, source_target_pairs={{0,16},{16,32},{32,48},{48,64},{64,80},{80,96},{96,112},{112,128},... | collective-permute-start | bytes 786440 | tf_op jit(solution)/shard_map/ppermute | solution.py:19
  249.5 9.6 %collective-permute-start.8 = (f32[32,1,16,128]{3,0,2,1:T(8,128)S(1)}, f32[32,1,16,128]{3,0,2,1:T(8,128)S(1)}, u32[]{:S(2)}, u32[]{:S(2)}) collective-permute-start(f32[32,1,16,128]{3,0,2,1:T(8,128)S(1)} %get-tuple-element.54), channel_id=1, source_target_pairs={{16,0},{32,16},{48,32},{64,48},{80,64},{96,80},{112,96},{128,112},... | collective-permute-start | bytes 786440 | tf_op jit(solution)/shard_map/ppermute | solution.py:22
  259.1 8.6 %collective-permute-start.10 = (f32[32,4,1,128]{3,0,2,1:T(8,128)S(1)}, f32[32,4,1,128]{3,0,2,1:T(8,128)S(1)}, u32[]{:S(2)}, u32[]{:S(2)}) collective-permute-start(f32[32,4,1,128]{3,0,2,1:T(8,128)S(1)} %get-tuple-element.43), channel_id=1, source_target_pairs={{1,0},{2,1},{3,2},{4,3},{5,4},{6,5},{7,6},{8,7},{9,8},{10,9},{11,1... | collective-permute-start | bytes 196616 | tf_op jit(solution)/shard_map/ppermute | solution.py:22
  261.1 8.2 %collective-permute-start.11 = (f32[32,4,1,128]{3,0,2,1:T(8,128)S(1)}, f32[32,4,1,128]{3,0,2,1:T(8,128)S(1)}, u32[]{:S(2)}, u32[]{:S(2)}) collective-permute-start(f32[32,4,1,128]{3,0,2,1:T(8,128)S(1)} %get-tuple-element.44), channel_id=1, source_target_pairs={{0,1},{1,2},{2,3},{3,4},{4,5},{5,6},{6,7},{7,8},{8,9},{9,10},{10,1... | collective-permute-start | bytes 196616 | tf_op jit(solution)/shard_map/ppermute | solution.py:19
where the time goes:
time: 363 us; the launch traced here: 362 us
  blocking collectives  241 us (66%)
  starting transfers between devices  48.1 us (13%)
  other arithmetic  29.1 us (8%)
  waiting for transfers between devices  23.7 us (7%)
  matrix products  15.6 us (4%)
    psum x15, blocking collectives, by_axis(): x = lax.psum(x, axis)  241 us
    ppermute x6, starting transfers between devices, with_halo(): lax.ppermute(lax.slice_in_dim(block, 0, width, axis=dim), axis, backward)  24.6 us
    ppermute x6, starting transfers between devices, with_halo(): lax.ppermute(lax.slice_in_dim(block, block.shape[dim] - width, None, axis...  23.5 us
    ppermute x6, waiting for transfers between devices, with_halo(): lax.ppermute(lax.slice_in_dim(block, block.shape[dim] - width, None, axis...  18.3 us
    another operation x12, other arithmetic, inverse_lower(): lower_factor = jnp.linalg.cholesky(gram_matrix)  14.4 us
    another operation x6, other arithmetic, inverse_lower(): lax.linalg.triangular_solve(lower_factor, identity_matrix, left_side=True...  11 us
    dot_general x10, matrix products, combine(): jnp.einsum('pxyz,pq->qxyz', vectors, matrix, precision=lax.Precision.HIGH...  8.48 us
  transfers between devices with their start and end apart: 12, of which 10 were waited for; matrix products, arithmetic and copies ran while one was open for 1% of the time, Pallas kernels for 0%

commit v1 on v0

v1 whole, which is shorter than its diff:
```python
import functools

import jax
import jax.numpy as jnp
from jax import lax
from jax.experimental import pallas as pl
from jax.experimental.pallas import tpu as pltpu
from jax.sharding import Mesh
from jax.sharding import PartitionSpec as P

GX = ("gx_0", "gx_1", "gx_2")
GY = ("gy_0", "gy_1")
NEAR = ("gx_0", "gx_2", "gy_1")
FAR = ("gx_1", "gy_0")

PROBES = 32
LANES = 128
ROWS = 16
PLANES = 2
CELLS = PLANES * ROWS
SHIFT = 7.75
B0 = 7.0
B1 = 10.0
PANEL = 8
F32 = jnp.float32
BF16 = jnp.bfloat16
INTERPRET = False

Y_ROWS = 2 * 3 * PROBES
X_BLOCKS = 20 + 18
X_ROWS = X_BLOCKS * PROBES


def vmem_specs(count):
    return [pl.BlockSpec(memory_space=pltpu.VMEM) for _ in range(count)]


def shaped(*shape, dtype=F32):
    return jax.ShapeDtypeStruct(shape, dtype)


def row_of(index):
    return pl.ds(index * PROBES, PROBES)


def prepare_kernel(signs_ref, diag_ref, own_ref, up_ref, down_ref):
    for cell in range(CELLS):
        plane, row = divmod(cell, ROWS)
        bits = signs_ref[pl.ds(cell, PROBES, stride=CELLS), :]
        probes = (2 * bits - 1).astype(F32)
        own_ref[row_of(cell), :] = probes
        if row < 3:
            down_ref[row_of(plane * 3 + row), :] = probes
        if row >= ROWS - 3:
            up_ref[row_of(plane * 3 + row - (ROWS - 3)), :] = probes
    for plane in range(PLANES):
        base = plane * ROWS
        down_ref[Y_ROWS + 2 * plane : Y_ROWS + 2 * plane + 2, :] = diag_ref[base : base + 2, :]
        up_ref[Y_ROWS + 2 * plane : Y_ROWS + 2 * plane + 2, :] = diag_ref[base + ROWS - 2 : base + ROWS, :]
    down_ref[Y_ROWS + 4 : Y_ROWS + 8, :] = jnp.zeros((4, LANES), F32)
    up_ref[Y_ROWS + 4 : Y_ROWS + 8, :] = jnp.zeros((4, LANES), F32)


def prepare(signs, diagonal):
    return pl.pallas_call(
        prepare_kernel,
        out_shape=(shaped(CELLS * PROBES, LANES), shaped(Y_ROWS + 8, LANES), shaped(Y_ROWS + 8, LANES)),
        in_specs=vmem_specs(2),
        out_specs=tuple(vmem_specs(3)),
        interpret=INTERPRET,
        name="prepare",
    )(signs, diagonal)


def pack_kernel(own_ref, diag_ref, low_ref, high_ref, plus_ref, minus_ref):
    def cell_of(plane, row):
        if row < 0:
            return low_ref[row_of(plane * 3 + row + 3), :]
        if row >= ROWS:
            return high_ref[row_of(plane * 3 + row - ROWS), :]
        return own_ref[row_of(plane * ROWS + row), :]

    def diag_of(plane, row):
        if row < 0:
            start = Y_ROWS + 2 * plane + row + 2
            return low_ref[start : start + 1, :]
        if row >= ROWS:
            start = Y_ROWS + 2 * plane + row - ROWS
            return high_ref[start : start + 1, :]
        return diag_ref[plane * ROWS + row : plane * ROWS + row + 1, :]

    for ref, near in ((plus_ref, 1), (minus_ref, 0)):
        far = 1 - near
        block = 0
        for row in range(-2, ROWS + 2):
            ref[row_of(block), :] = cell_of(near, row)
            block += 1
        for row in range(-1, ROWS + 1):
            ref[row_of(block), :] = cell_of(far, row)
            block += 1
        line = X_ROWS
        for row in range(-1, ROWS + 1):
            ref[line : line + 1, :] = diag_of(near, row)
            line += 1
        for row in range(ROWS):
            ref[line : line + 1, :] = diag_of(far, row)
            line += 1
        ref[line : line + 6, :] = jnp.zeros((6, LANES), F32)


def pack(own, diagonal, low, high):
    return pl.pallas_call(
        pack_kernel,
        out_shape=(shaped(X_ROWS + 40, LANES), shaped(X_ROWS + 40, LANES)),
        in_specs=vmem_specs(4),
        out_specs=tuple(vmem_specs(2)),
        interpret=INTERPRET,
        name="pack",
    )(own, diagonal, low, high)


def nt_dot(left, right, precision=None):
    return lax.dot_general(
        left, right, (((1,), (1,)), ((), ())), precision=precision, preferred_element_type=F32
    )


def basis_kernel(
    own_ref, diag_ref, low_ref, high_ref, left_ref, right_ref, left2_ref, right2_ref,
    high_out, low_out, gram_ref, first_ref, second_ref,
):
    def distance(plane):
        return -plane if plane < 0 else max(plane - (PLANES - 1), 0)

    def k0(plane, row):
        away = distance(plane)
        if away == 0:
            if row < 0:
                return low_ref[row_of(plane * 3 + row + 3), :]
            if row >= ROWS:
                return high_ref[row_of(plane * 3 + row - ROWS), :]
            return own_ref[row_of(plane * ROWS + row), :]
        side, side2 = (left_ref, left2_ref) if plane < 0 else (right_ref, right2_ref)
        if away == 1:
            return side[row_of(row + 2), :]
        if away == 2:
            return side[row_of(20 + row + 1), :]
        return side2[row_of(row), :]

    def factor(plane, row):
        away = distance(plane)
        if away == 0:
            if row < 0:
                start = Y_ROWS + 2 * plane + row + 2
                line = low_ref[start : start + 1, :]
            elif row >= ROWS:
                start = Y_ROWS + 2 * plane + row - ROWS
                line = high_ref[start : start + 1, :]
            else:
                line = diag_ref[plane * ROWS + row : plane * ROWS + row + 1, :]
        else:
            side = left_ref if plane < 0 else right_ref
            start = X_ROWS + (row + 1 if away == 1 else 18 + row)
            line = side[start : start + 1, :]
        return line + (6.0 - SHIFT)

    def cells(width):
        found = []
        for plane in range(-width, PLANES + width):
            extra = width - distance(plane)
            for row in range(-extra, ROWS + extra):
                found.append((plane, row))
        return found

    first_slot = {key: slot for slot, key in enumerate(cells(2))}
    second_slot = {key: slot for slot, key in enumerate(cells(1))}

    def k1(plane, row):
        return first_ref[row_of(first_slot[(plane, row)]), :]

    def k2(plane, row):
        return second_ref[row_of(second_slot[(plane, row)]), :]

    def apply(field, plane, row):
        center = field(plane, row)
        beside = field(plane - 1, row) + field(plane + 1, row)
        beside = beside + (field(plane, row - 1) + field(plane, row + 1))
        beside = beside + (pltpu.roll(center, 1, 1) + pltpu.roll(center, LANES - 1, 1))
        return factor(plane, row) * center - beside

    def keep(order, plane, row, value):
        columns = pl.ds((plane * ROWS + row) * LANES, LANES)
        upper = value.astype(BF16)
        high_out[row_of(order), columns] = upper
        if order == 0:
            low_out[row_of(order), columns] = jnp.zeros_like(upper)
        else:
            low_out[row_of(order), columns] = (value - upper.astype(F32)).astype(BF16)

    for plane, row in cells(0):
        keep(0, plane, row, k0(plane, row))
    for plane, row in cells(2):
        value = apply(k0, plane, row)
        first_ref[row_of(first_slot[(plane, row)]), :] = value
        if distance(plane) == 0 and 0 <= row < ROWS:
            keep(1, plane, row, value)
    for plane, row in cells(1):
        value = apply(k1, plane, row) - B0 * k0(plane, row)
        second_ref[row_of(second_slot[(plane, row)]), :] = value
        if distance(plane) == 0 and 0 <= row < ROWS:
            keep(2, plane, row, value)
    for plane, row in cells(0):
        keep(3, plane, row, apply(k2, plane, row) - B1 * k1(plane, row))
    upper = high_out[...]
    lower = low_out[...]
    top = nt_dot(upper[:PROBES], upper) + nt_dot(upper[:PROBES], lower)
    bottom = nt_dot(upper[3 * PROBES :], upper) + nt_dot(upper[3 * PROBES :], lower)
    gram_ref[:PROBES, :] = top
    gram_ref[PROBES:, :] = bottom + nt_dot(lower[3 * PROBES :], upper)


def basis(*operands):
    width = CELLS * LANES
    return pl.pallas_call(
        basis_kernel,
        out_shape=(
            shaped(4 * PROBES, width, dtype=BF16),
            shaped(4 * PROBES, width, dtype=BF16),
            shaped(2 * PROBES, LANES),
        ),
        in_specs=vmem_specs(len(operands)),
        out_specs=tuple(vmem_specs(3)),
        scratch_shapes=[pltpu.VMEM((108 * PROBES, LANES), F32), pltpu.VMEM((68 * PROBES, LANES), F32)],
        interpret=INTERPRET,
        name="basis",
    )(*operands)


def eliminate(system, block):
    groups = PROBES // 8
    lane = lax.broadcasted_iota(jnp.int32, (8, LANES), 1)
    sub = lax.broadcasted_iota(jnp.int32, (8, LANES), 0)
    start = block * PROBES
    inside = (lane >= start) & (lane < start + PROBES)
    pivoted = [system[8 * g : 8 * g + 8, :] for g in range(groups)]
    solved = [
        jnp.where(inside, jnp.where(lane - start == sub + 8 * g, 1.0, 0.0), pivoted[g]) for g in range(groups)
    ]
    scales = [None] * PROBES
    for panel in range(0, PROBES, PANEL):
        first_group = panel // 8
        spread = {}
        for k in range(panel, panel + PANEL):
            for g in range(first_group, groups):
                column = pivoted[g][:, start + k : start + k + 1]
                spread[k, g] = jnp.broadcast_to(column, (8, LANES))
        for k in range(panel, panel + PANEL):
            group, line = divmod(k, 8)

            def pivot_row(value):
                return jnp.broadcast_to(value[line : line + 1, :], (8, LANES))

            pivot = pivot_row(spread[k, group])
            inverse = 1.0 / pivot
            scales[k] = lax.rsqrt(pivot)
            multiplier = {}
            for g in range(group, groups):
                value = spread[k, g] * inverse
                if g == group:
                    value = jnp.where(sub > line, value, 0.0)
                multiplier[g] = value
            for other in range(k + 1, panel + PANEL):
                row = pivot_row(spread[other, group])
                for g in range(group, groups):
                    spread[other, g] = spread[other, g] - multiplier[g] * row
            row = pivot_row(pivoted[group])
            solved_row = pivot_row(solved[group])
            for g in range(group, groups):
                pivoted[g] = pivoted[g] - multiplier[g] * row
                solved[g] = solved[g] - multiplier[g] * solved_row
    upper = []
    for g in range(groups):
        scale = scales[8 * g]
        for line in range(1, 8):
            scale = jnp.where(sub == line, scales[8 * g + line], scale)
        solved[g] = solved[g] * scale
        upper.append(jnp.where(inside & (lane - start >= sub + 8 * g), pivoted[g] * scale, 0.0))
    return jnp.concatenate(solved, 0), jnp.concatenate(upper, 0)


def finish_kernel(gram_ref, high_ref, low_ref, alpha_ref, beta_ref, next_ref):
    exact = lax.Precision.HIGHEST
    lane = lax.broadcasted_iota(jnp.int32, (PROBES, LANES), 1)
    block_of = lane // PROBES
    first = gram_ref[:PROBES, :]
    last = gram_ref[PROBES:, :]

    def moved(value, blocks):
        return pltpu.roll(value, (blocks * PROBES) % LANES, 1)

    second = moved(first, -1) + jnp.where(block_of == 1, B0, B1) * moved(first, 1)
    second = jnp.where(block_of == 3, moved(last, 2), jnp.where(block_of == 0, 0.0, second))
    third = moved(last, 1) + jnp.where(block_of == 2, B1 * moved(second, 1) - B0 * first, 0.0)
    third = jnp.where(block_of < 2, 0.0, third)
    systems = [first, second, third, jnp.where(block_of < 3, 0.0, last)]
    solved = []
    uppers = []
    for block in range(4):
        value, upper = eliminate(systems[block], block)
        solved.append(value)
        uppers.append(upper)
        if block < 3:
            tail = value[:, (block + 1) * PROBES :]
            update = lax.dot_general(
                tail, value, (((0,), (0,)), ((), ())), precision=exact, preferred_element_type=F32
            )
            for later in range(block + 1, 4):
                offset = (later - block - 1) * PROBES
                change = update[offset : offset + PROBES, :]
                change = jnp.where((block_of <= block) | (block_of >= later), change, 0.0)
                systems[later] = systems[later] - change
    weights = solved[3]
    upper = weights.astype(BF16)
    lower = (weights - upper.astype(F32)).astype(BF16)
    high = high_ref[...]
    result = jnp.dot(upper, high, preferred_element_type=F32)
    result = result + jnp.dot(upper, low_ref[...], preferred_element_type=F32)
    result = result + jnp.dot(lower, high, preferred_element_type=F32)
    for cell in range(CELLS):
        next_ref[pl.ds(cell, PROBES, stride=CELLS), :] = result[:, cell * LANES : (cell + 1) * LANES]
    row32 = lax.broadcasted_iota(jnp.int32, (PROBES, PROBES), 0)
    lane32 = lax.broadcasted_iota(jnp.int32, (PROBES, PROBES), 1)
    beta = None
    for block in range(3):
        inverse = jnp.where(block_of == block, solved[block], 0.0)
        alpha = nt_dot(moved(solved[block], -1), inverse, exact)
        if block > 0:
            alpha = alpha - jnp.dot(
                beta, nt_dot(solved[block - 1], inverse, exact), precision=exact, preferred_element_type=F32
            )
        alpha_ref[block] = alpha + jnp.where(row32 == lane32, SHIFT, 0.0)
        beta = nt_dot(moved(uppers[block + 1], -1), inverse, exact)
        beta_ref[block] = jnp.where(row32 <= lane32, beta, 0.0)


def finish(gram, high, low):
    return pl.pallas_call(
        finish_kernel,
        out_shape=(
            shaped(3, PROBES, PROBES),
            shaped(3, PROBES, PROBES),
            shaped(PROBES * CELLS, LANES),
        ),
        in_specs=vmem_specs(3),
        out_specs=tuple(vmem_specs(3)),
        interpret=INTERPRET,
        name="finish",
    )(gram, high, low)


def shifted(x, axes, steps):
    count = lax.axis_size(axes)
    return lax.ppermute(x, axes, [(i, (i + steps) % count) for i in range(count)])


def exchanged(x, axes):
    return lax.all_to_all(x, axes, 0, 0, tiled=True)


def gathered(x, axes):
    return exchanged(jnp.broadcast_to(x[None], (lax.axis_size(axes),) + x.shape), axes)


def reduced(x):
    near = lax.axis_size(NEAR)
    part = exchanged(x.reshape(near, x.shape[0] // near, x.shape[1]), NEAR).sum(0)
    part = gathered(part, FAR).sum(0)
    return gathered(part, NEAR).reshape(x.shape)


def per_device(probe_signs, diagonal):
    signs = probe_signs.reshape(PROBES * CELLS, LANES)
    diag = diagonal.reshape(CELLS, LANES)
    own, up, down = prepare(signs, diag)
    low = shifted(up, GY, 1)
    high = shifted(down, GY, -1)
    half = ROWS * PROBES
    left2 = shifted(own[half:], GX, 2)
    right2 = shifted(own[:half], GX, -2)
    plus, minus = pack(own, diag, low, high)
    left = shifted(plus, GX, 1)
    right = shifted(minus, GX, -1)
    upper, lower, gram = basis(own, diag, low, high, left, right, left2, right2)
    alphas, betas, following = finish(reduced(gram), upper, lower)
    return (alphas, betas, following.reshape(PROBES, PLANES, ROWS, LANES))


def solution(mesh):
    split = Mesh(mesh.devices.reshape(2, 8, 2, 8, 2), ("gx_0", "gx_1", "gx_2", "gy_0", "gy_1"))
    placed = (P(None, GX, GY, None), P(GX, GY, None))
    return jax.shard_map(
        per_device,
        mesh=split,
        in_specs=placed,
        out_specs=(P(), P(), P(None, GX, GY, None)),
        check_vma=False,
    )
```

time: 363 us -> 107 us (0.29)
  the two profiles are of different devices: /device:TPU:6 before, /device:TPU:1 now
where the time goes in v1:
time: 107 us
  blocking collectives  47 us (44%)
  starting transfers between devices  28.6 us (27%)
  Pallas kernels  17.6 us (16%)
  waiting for transfers between devices  10.1 us (9%)
  local copies, waits for them, and re-layouts  2.44 us (2%)
    all_to_all x3, blocking collectives, exchanged(): return lax.all_to_all(x, axes, 0, 0, tiled=True)  47 us
    ppermute x6, starting transfers between devices, shifted(): lax.ppermute(x, axes, [(i, (i + steps) % count) for i in range(count)])  28.6 us
    ppermute x6, waiting for transfers between devices, shifted(): lax.ppermute(x, axes, [(i, (i + steps) % count) for i in range(count)])  10.1 us
    pallas_call x1, Pallas kernels, finish(): pl.pallas_call(finish_kernel, out_shape=(shaped(3, PROBES, PROBES), shape...  7.5 us
    pallas_call x1, Pallas kernels, basis(): pl.pallas_call(basis_kernel, out_shape=(shaped(4 * PROBES, width, dtype=B...  5.63 us
    unnamed x14, local copies, waits for them, and re-layouts  2.38 us
    pallas_call x1, Pallas kernels, pack(): pl.pallas_call(pack_kernel, out_shape=(shaped(X_ROWS + 40, LANES), shaped...  2.23 us
    pallas_call x1, Pallas kernels, prepare(): pl.pallas_call(prepare_kernel, out_shape=(shaped(CELLS * PROBES, LANES),...  2.2 us
  transfers between devices with their start and end apart: 6, of which 4 were waited for; matrix products, arithmetic and copies ran while one was open for 0% of the time, Pallas kernels for 0%

profile of v1, /device:TPU:1, one launch (start us, length us, event | category | flops | bytes accessed | tf_op | source)
XLA Modules:
  0.0 106.6 jit_solution(12338166082414746958)
XLA Ops:
  0.6 2.2 %prepare.1 = (f32[1024,128]{1,0:T(8,128)}, f32[200,128]{1,0:T(8,128)}, f32[200,128]{1,0:T(8,128)}) custom-call(s32[1024,128]{1,0:T(8,128)} %bitcast.5, f32[32,128]{1,0:T(8,128)} %bitcast.6), custom_call_target="tpu_custom_call" | custom-call | tf_op jit(solution)/shard_map/prepare/pallas_call | solution.py:65
  2.8 0.0 copy-start
  2.8 5.6 %collective-permute-start = (f32[200,128]{1,0:T(8,128)}, f32[200,128]{1,0:T(8,128)S(1)}, u32[]{:S(2)}, u32[]{:S(2)}) collective-permute-start(f32[200,128]{1,0:T(8,128)} %get-tuple-element.15), channel_id=1, source_target_pairs={{0,1},{1,2},{2,3},{3,4},{4,5},{5,6},{6,7},{7,8},{8,9},{9,10},{10,1... | collective-permute-start | bytes 307208 | tf_op jit(solution)/shard_map/ppermute | solution.py:363
  8.4 10.4 %collective-permute-start.1 = (f32[200,128]{1,0:T(8,128)}, f32[200,128]{1,0:T(8,128)S(1)}, u32[]{:S(2)}, u32[]{:S(2)}) collective-permute-start(f32[200,128]{1,0:T(8,128)} %get-tuple-element.16), channel_id=1, source_target_pairs={{0,15},{1,0},{2,1},{3,2},{4,3},{5,4},{6,5},{7,6},{8,7},{9,8},{10,9... | collective-permute-start | bytes 307208 | tf_op jit(solution)/shard_map/ppermute | solution.py:363
  18.8 0.9 collective-permute-done.low_ref
  19.7 0.0 copy-start.3
  19.7 1.1 %collective-permute-done.1.high_ref = f32[200,128]{1,0:T(8,128)S(1)} collective-permute-done((f32[200,128]{1,0:T(8,128)}, f32[200,128]{1,0:T(8,128)S(1)}, u32[]{:S(2)}, u32[]{:S(2)}) %collective-permute-start.1) | collective-permute-done | bytes 102432 | tf_op jit(solution)/shard_map/ppermute | solution.py:363
  20.8 0.0 copy-start.4
  20.8 0.0 copy-done.3
  20.8 0.6 copy-done.4
  21.4 2.2 %pack.1 = (f32[1256,128]{1,0:T(8,128)}, f32[1256,128]{1,0:T(8,128)}) custom-call(f32[1024,128]{1,0:T(8,128)} %get-tuple-element.14.own_ref, f32[32,128]{1,0:T(8,128)} %bitcast.7, f32[200,128]{1,0:T(8,128)} %copy-done.3, f32[200,128]{1,0:T(8,128)} %copy-done.4), custom_call_target="tpu_custom_call" | custom-call | tf_op jit(solution)/shard_map/pack/pallas_call | solution.py:112
  23.7 4.6 %collective-permute-start.2 = (f32[1256,128]{1,0:T(8,128)}, f32[1256,128]{1,0:T(8,128)S(1)}, u32[]{:S(2)}, u32[]{:S(2)}) collective-permute-start(f32[1256,128]{1,0:T(8,128)} %get-tuple-element.17), channel_id=1, source_target_pairs={{0,16},{16,32},{32,48},{48,64},{64,80},{80,96},{96,112},{112,128},... | collective-permute-start | bytes 1929224 | tf_op jit(solution)/shard_map/ppermute | solution.py:363
  28.3 1.9 %collective-permute-start.3 = (f32[1256,128]{1,0:T(8,128)}, f32[1256,128]{1,0:T(8,128)S(1)}, u32[]{:S(2)}, u32[]{:S(2)}) collective-permute-start(f32[1256,128]{1,0:T(8,128)} %get-tuple-element.18), channel_id=1, source_target_pairs={{0,496},{16,0},{32,16},{48,32},{64,48},{80,64},{96,80},{112,96},{1... | collective-permute-start | bytes 1929224 | tf_op jit(solution)/shard_map/ppermute | solution.py:363
  30.2 0.0 copy-done
  30.3 4.2 %collective-permute-start.5 = (f32[512,128]{1,0:T(8,128)S(1)}, f32[512,128]{1,0:T(8,128)S(1)}, u32[]{:S(2)}, u32[]{:S(2)}) collective-permute-start(f32[512,128]{1,0:T(8,128)S(1)} %get-tuple-element.25), channel_id=1, source_target_pairs={{0,480},{16,496},{32,0},{48,16},{64,32},{80,48},{96,64},{112,80},{... | collective-permute-start | bytes 786440 | tf_op jit(solution)/shard_map/ppermute | solution.py:363
  34.5 1.9 %collective-permute-start.4 = (f32[512,128]{1,0:T(8,128)S(1)}, f32[512,128]{1,0:T(8,128)S(1)}, u32[]{:S(2)}, u32[]{:S(2)}) collective-permute-start(f32[512,128]{1,0:T(8,128)S(1)} %get-tuple-element.26), channel_id=1, source_target_pairs={{0,32},{16,48},{32,64},{48,80},{64,96},{80,112},{96,128},{112,144}... | collective-permute-start | bytes 786440 | tf_op jit(solution)/shard_map/ppermute | solution.py:363
  36.4 4.2 %collective-permute-done.5.right2_ref = f32[512,128]{1,0:T(8,128)S(1)} collective-permute-done((f32[512,128]{1,0:T(8,128)S(1)}, f32[512,128]{1,0:T(8,128)S(1)}, u32[]{:S(2)}, u32[]{:S(2)}) %collective-permute-start.5) | collective-permute-done | bytes 262176 | tf_op jit(solution)/shard_map/ppermute | solution.py:363
  40.6 0.0 copy-start.5
  40.6 4.0 %collective-permute-done.4.left2_ref = f32[512,128]{1,0:T(8,128)S(1)} collective-permute-done((f32[512,128]{1,0:T(8,128)S(1)}, f32[512,128]{1,0:T(8,128)S(1)}, u32[]{:S(2)}, u32[]{:S(2)}) %collective-permute-start.4) | collective-permute-done | bytes 262176 | tf_op jit(solution)/shard_map/ppermute | solution.py:363
  44.6 0.0 copy-start.6
  44.6 0.0 collective-permute-done.2.left_ref
  44.6 0.0 copy-start.1
  44.6 0.0 collective-permute-done.3.right_ref
  44.6 0.0 copy-done.5
  44.6 0.7 copy-done.6
  45.3 0.2 copy-done.1
  45.5 0.0 copy-start.2
  45.5 0.8 copy-done.2
  46.3 5.6 %basis.1 = (bf16[128,4096]{1,0:T(8,128)(2,1)}, bf16[128,4096]{1,0:T(8,128)(2,1)}, f32[64,128]{1,0:T(8,128)}) custom-call(f32[1024,128]{1,0:T(8,128)} %get-tuple-element.14.own_ref, f32[32,128]{1,0:T(8,128)} %bitcast.8, f32[200,128]{1,0:T(8,128)} %copy-done.3, f32[200,128]{1,0:T(8,128)} %copy-done.4, f32[1256,128]{1,0:T(8,128)} %copy-done.1, ...), custom_call_target="tpu_custom_call" | custom-call | tf_op jit(solution)/shard_map/basis/pallas_call | solution.py:224
  51.9 10.8 %all_to_all.15 = f32[8,8,128]{2,1,0:T(8,128)S(1)} all-to-all(f32[8,8,128]{2,1,0:T(8,128)} %bitcast.10), channel_id=1, replica_groups=mesh['gx_0'=2,'gx_1'=8,'gx_2'=2,'gy_0'=8,'gy_1'=2] {'gx_0','gx_2','gy_1'}, dimensions={0} | all-to-all | bytes 65536 | tf_op jit(solution)/shard_map/all_to_all | solution.py:367
  62.8 25.4 %all_to_all.16 = f32[64,8,128]{2,1,0:T(8,128)S(1)} all-to-all(f32[64,8,128]{2,1,0:T(8,128)S(1)} %broadcast_in_dim.4), channel_id=1, replica_groups=mesh['gx_0'=2,'gx_1'=8,'gx_2'=2,'gy_0'=8,'gy_1'=2] {'gx_1','gy_0'}, dimensions={0} | all-to-all | bytes 524288 | tf_op jit(solution)/shard_map/all_to_all | solution.py:367
  88.2 0.1 reduce_sum.19
  88.3 10.8 %all_to_all.17 = f32[8,8,128]{2,1,0:T(8,128)} all-to-all(f32[8,8,128]{2,1,0:T(8,128)S(1)} %broadcast_in_dim.5), channel_id=1, replica_groups=mesh['gx_0'=2,'gx_1'=8,'gx_2'=2,'gy_0'=8,'gy_1'=2] {'gx_0','gx_2','gy_1'}, dimensions={0} | all-to-all | bytes 65536 | tf_op jit(solution)/shard_map/all_to_all | solution.py:367
  99.1 7.5 %finish.1 = (f32[3,32,32]{2,1,0:T(8,128)}, f32[3,32,32]{2,1,0:T(8,128)}, f32[1024,128]{1,0:T(8,128)}) custom-call(f32[64,128]{1,0:T(8,128)} %bitcast.9, bf16[128,4096]{1,0:T(8,128)(2,1)} %get-tuple-element.20.high_ref, bf16[128,4096]{1,0:T(8,128)(2,1)} %get-tuple-element.21.low_ref), custom_call_target="tpu_custom_call" | custom-call | tf_op jit(solution)/shard_map/finish/pallas_call | solution.py:347
  (4 shorter events, 0.1 us)
Async XLA Ops:
  2.8 27.4 %copy-start = (f32[1024,128]{1,0:T(8,128)S(1)}, f32[1024,128]{1,0:T(8,128)}, u32[]{:S(2)}) copy-start(f32[1024,128]{1,0:T(8,128)} %get-tuple-element.14.own_ref) | copy-start | bytes 1572868
  2.8 16.9 %collective-permute-start = (f32[200,128]{1,0:T(8,128)}, f32[200,128]{1,0:T(8,128)S(1)}, u32[]{:S(2)}, u32[]{:S(2)}) collective-permute-start(f32[200,128]{1,0:T(8,128)} %get-tuple-element.15), channel_id=1, source_target_pairs={{0,1},{1,2},{2,3},{3,4},{4,5},{5,6},{6,7},{7,8},{8,9},{9,10},{10,1... | collective-permute-start | bytes 307208 | tf_op jit(solution)/shard_map/ppermute | solution.py:363
  8.4 12.4 %collective-permute-start.1 = (f32[200,128]{1,0:T(8,128)}, f32[200,128]{1,0:T(8,128)S(1)}, u32[]{:S(2)}, u32[]{:S(2)}) collective-permute-start(f32[200,128]{1,0:T(8,128)} %get-tuple-element.16), channel_id=1, source_target_pairs={{0,15},{1,0},{2,1},{3,2},{4,3},{5,4},{6,5},{7,6},{8,7},{9,8},{10,9... | collective-permute-start | bytes 307208 | tf_op jit(solution)/shard_map/ppermute | solution.py:363
  19.7 1.1 %copy-start.3 = (f32[200,128]{1,0:T(8,128)}, f32[200,128]{1,0:T(8,128)S(1)}, u32[]{:S(2)}) copy-start(f32[200,128]{1,0:T(8,128)S(1)} %collective-permute-done.low_ref) | copy-start | bytes 307204
  20.8 0.6 copy-start.4
  23.7 20.9 %collective-permute-start.2 = (f32[1256,128]{1,0:T(8,128)}, f32[1256,128]{1,0:T(8,128)S(1)}, u32[]{:S(2)}, u32[]{:S(2)}) collective-permute-start(f32[1256,128]{1,0:T(8,128)} %get-tuple-element.17), channel_id=1, source_target_pairs={{0,16},{16,32},{32,48},{48,64},{64,80},{80,96},{96,112},{112,128},... | collective-permute-start | bytes 1929224 | tf_op jit(solution)/shard_map/ppermute | solution.py:363
  28.3 16.3 %collective-permute-start.3 = (f32[1256,128]{1,0:T(8,128)}, f32[1256,128]{1,0:T(8,128)S(1)}, u32[]{:S(2)}, u32[]{:S(2)}) collective-permute-start(f32[1256,128]{1,0:T(8,128)} %get-tuple-element.18), channel_id=1, source_target_pairs={{0,496},{16,0},{32,16},{48,32},{64,48},{80,64},{96,80},{112,96},{1... | collective-permute-start | bytes 1929224 | tf_op jit(solution)/shard_map/ppermute | solution.py:363
  30.3 10.3 %collective-permute-start.5 = (f32[512,128]{1,0:T(8,128)S(1)}, f32[512,128]{1,0:T(8,128)S(1)}, u32[]{:S(2)}, u32[]{:S(2)}) collective-permute-start(f32[512,128]{1,0:T(8,128)S(1)} %get-tuple-element.25), channel_id=1, source_target_pairs={{0,480},{16,496},{32,0},{48,16},{64,32},{80,48},{96,64},{112,80},{... | collective-permute-start | bytes 786440 | tf_op jit(solution)/shard_map/ppermute | solution.py:363
  34.5 10.1 %collective-permute-start.4 = (f32[512,128]{1,0:T(8,128)S(1)}, f32[512,128]{1,0:T(8,128)S(1)}, u32[]{:S(2)}, u32[]{:S(2)}) collective-permute-start(f32[512,128]{1,0:T(8,128)S(1)} %get-tuple-element.26), channel_id=1, source_target_pairs={{0,32},{16,48},{32,64},{48,80},{64,96},{80,112},{96,128},{112,144}... | collective-permute-start | bytes 786440 | tf_op jit(solution)/shard_map/ppermute | solution.py:363
  40.6 4.0 %copy-start.5 = (f32[512,128]{1,0:T(8,128)}, f32[512,128]{1,0:T(8,128)S(1)}, u32[]{:S(2)}) copy-start(f32[512,128]{1,0:T(8,128)S(1)} %collective-permute-done.5.right2_ref) | copy-start | bytes 786436
  44.6 0.7 copy-start.6
  44.6 0.9 copy-start.1
  45.5 0.8 copy-start.2

commit v2 on v1

--- a/solution.py
+++ b/solution.py
@@ -1,5 +1,3 @@
-import functools
-
 import jax
 import jax.numpy as jnp
 from jax import lax
@@ -7,6 +5,7 @@
 from jax.experimental.pallas import tpu as pltpu
 from jax.sharding import Mesh
 from jax.sharding import PartitionSpec as P
+
 
 GX = ("gx_0", "gx_1", "gx_2")
 GY = ("gy_0", "gy_1")
@@ -25,6 +24,7 @@
 F32 = jnp.float32
 BF16 = jnp.bfloat16
 INTERPRET = False
+VMEM_LIMIT = 16 * 2**20
 
 Y_ROWS = 2 * 3 * PROBES
 X_BLOCKS = 20 + 18
@@ -36,7 +36,11 @@
 
 
 def shaped(*shape, dtype=F32):
-    return jax.ShapeDtypeStruct(shape, dtype)
+    return pltpu.VMEM(shape, dtype)
+
+
+def held(*arrays):
+    return tuple(pltpu.with_memory_space_constraint(x, pltpu.VMEM) for x in arrays)
 
 
 def row_of(index):
@@ -67,6 +71,7 @@
         out_shape=(shaped(CELLS * PROBES, LANES), shaped(Y_ROWS + 8, LANES), shaped(Y_ROWS + 8, LANES)),
         in_specs=vmem_specs(2),
         out_specs=tuple(vmem_specs(3)),
+        compiler_params=pltpu.CompilerParams(vmem_limit_bytes=VMEM_LIMIT),
         interpret=INTERPRET,
         name="prepare",
     )(signs, diagonal)
@@ -114,9 +119,10 @@
         out_shape=(shaped(X_ROWS + 40, LANES), shaped(X_ROWS + 40, LANES)),
         in_specs=vmem_specs(4),
         out_specs=tuple(vmem_specs(2)),
+        compiler_params=pltpu.CompilerParams(vmem_limit_bytes=VMEM_LIMIT),
         interpret=INTERPRET,
         name="pack",
-    )(own, diagonal, low, high)
+    )(*held(own), diagonal, *held(low, high))
 
 
 def nt_dot(left, right, precision=None):
@@ -231,9 +237,10 @@
         in_specs=vmem_specs(len(operands)),
         out_specs=tuple(vmem_specs(3)),
         scratch_shapes=[pltpu.VMEM((108 * PROBES, LANES), F32), pltpu.VMEM((68 * PROBES, LANES), F32)],
+        compiler_params=pltpu.CompilerParams(vmem_limit_bytes=VMEM_LIMIT),
         interpret=INTERPRET,
         name="basis",
-    )(*operands)
+    )(*held(*operands))
 
 
 def eliminate(system, block):
@@ -347,15 +354,16 @@
     return pl.pallas_call(
         finish_kernel,
         out_shape=(
-            shaped(3, PROBES, PROBES),
-            shaped(3, PROBES, PROBES),
-            shaped(PROBES * CELLS, LANES),
+            jax.ShapeDtypeStruct((3, PROBES, PROBES), F32),
+            jax.ShapeDtypeStruct((3, PROBES, PROBES), F32),
+            jax.ShapeDtypeStruct((PROBES * CELLS, LANES), F32),
         ),
         in_specs=vmem_specs(3),
         out_specs=tuple(vmem_specs(3)),
+        compiler_params=pltpu.CompilerParams(vmem_limit_bytes=VMEM_LIMIT),
         interpret=INTERPRET,
         name="finish",
-    )(gram, high, low)
+    )(*held(gram, high, low))
 
 
 def shifted(x, axes, steps):
@@ -382,9 +390,9 @@
     signs = probe_signs.reshape(PROBES * CELLS, LANES)
     diag = diagonal.reshape(CELLS, LANES)
     own, up, down = prepare(signs, diag)
+    half = ROWS * PROBES
     low = shifted(up, GY, 1)
     high = shifted(down, GY, -1)
-    half = ROWS * PROBES
     left2 = shifted(own[half:], GX, 2)
     right2 = shifted(own[:half], GX, -2)
     plus, minus = pack(own, diag, low, high)

time: 107 us -> 97.3 us (0.909)
  Pallas kernels: 17.6 us -> 9.84 us
    pallas_call x1, Pallas kernels: 5.63 us -> 3.44 us  [basis(): pl.pallas_call(basis_kernel, out_shape=(shaped(4 * PROBES, width, dtype=B...]
    pallas_call x1, Pallas kernels: 2.23 us -> 0.1 us  [pack(): pl.pallas_call(pack_kernel, out_shape=(shaped(X_ROWS + 40, LANES), shaped...]
    pallas_call x1, Pallas kernels: 2.2 us -> 0.36 us  [prepare(): pl.pallas_call(prepare_kernel, out_shape=(shaped(CELLS * PROBES, LANES),...]
    pallas_call x1, Pallas kernels: 7.5 us -> 5.94 us  [finish(): pl.pallas_call(finish_kernel, out_shape=(jax.ShapeDtypeStruct((3, PROBES,...]
    unnamed x14 -> x6, local copies, waits for them, and re-layouts: 2.38 us -> 1.76 us
where the time goes in v2:
time: 97.3 us; the launch traced here: 96.8 us
  blocking collectives  46 us (47%)
  starting transfers between devices  28.5 us (29%)
  Pallas kernels  9.84 us (10%)
  waiting for transfers between devices  9.83 us (10%)
  local copies, waits for them, and re-layouts  1.82 us (2%)
    all_to_all x3, blocking collectives, exchanged(): return lax.all_to_all(x, axes, 0, 0, tiled=True)  46 us
    ppermute x6, starting transfers between devices, shifted(): lax.ppermute(x, axes, [(i, (i + steps) % count) for i in range(count)])  28.5 us
    ppermute x6, waiting for transfers between devices, shifted(): lax.ppermute(x, axes, [(i, (i + steps) % count) for i in range(count)])  9.83 us
    pallas_call x1, Pallas kernels, finish(): pl.pallas_call(finish_kernel, out_shape=(jax.ShapeDtypeStruct((3, PROBES,...  5.94 us
    pallas_call x1, Pallas kernels, basis(): pl.pallas_call(basis_kernel, out_shape=(shaped(4 * PROBES, width, dtype=B...  3.44 us
  transfers between devices with their start and end apart: 6, of which 4 were waited for; matrix products, arithmetic and copies ran while one was open for 0% of the time, Pallas kernels for 0%

profile of v2, /device:TPU:1, one launch (start us, length us, event | category | flops | bytes accessed | tf_op | source)
XLA Modules:
  0.0 96.8 jit_solution(7448414215002040832)
XLA Ops:
  0.6 0.0 copy-start
  0.6 1.0 %copy-done = s32[32,2,16,128]{3,2,1,0:T(8,128)S(1)} copy-done((s32[32,2,16,128]{3,2,1,0:T(8,128)S(1)}, s32[32,2,16,128]{3,2,1,0:T(8,128)}, u32[]{:S(2)}) %copy-start) | copy-done | bytes 524312
  1.7 0.0 copy-start.1
  1.7 0.7 copy-done.1
  2.4 0.4 prepare.1
  2.7 5.5 %collective-permute-start = (f32[200,128]{1,0:T(8,128)S(1)}, f32[200,128]{1,0:T(8,128)S(1)}, u32[]{:S(2)}, u32[]{:S(2)}) collective-permute-start(f32[200,128]{1,0:T(8,128)S(1)} %get-tuple-element.15), channel_id=1, source_target_pairs={{0,1},{1,2},{2,3},{3,4},{4,5},{5,6},{6,7},{7,8},{8,9},{9,10},{10,1... | collective-permute-start | bytes 307208 | tf_op jit(solution)/shard_map/ppermute | solution.py:371
  8.2 10.4 %collective-permute-start.1 = (f32[200,128]{1,0:T(8,128)S(1)}, f32[200,128]{1,0:T(8,128)S(1)}, u32[]{:S(2)}, u32[]{:S(2)}) collective-permute-start(f32[200,128]{1,0:T(8,128)S(1)} %get-tuple-element.16), channel_id=1, source_target_pairs={{0,15},{1,0},{2,1},{3,2},{4,3},{5,4},{6,5},{7,6},{8,7},{9,8},{10,9... | collective-permute-start | bytes 307208 | tf_op jit(solution)/shard_map/ppermute | solution.py:371
  18.6 0.6 collective-permute-done.low_ref
  19.3 1.0 %collective-permute-done.1.high_ref = f32[200,128]{1,0:T(8,128)S(1)} collective-permute-done((f32[200,128]{1,0:T(8,128)S(1)}, f32[200,128]{1,0:T(8,128)S(1)}, u32[]{:S(2)}, u32[]{:S(2)}) %collective-permute-start.1) | collective-permute-done | bytes 102432 | tf_op jit(solution)/shard_map/ppermute | solution.py:371
  20.3 0.1 pack.1
  20.4 4.6 %collective-permute-start.2 = (f32[1256,128]{1,0:T(8,128)S(1)}, f32[1256,128]{1,0:T(8,128)S(1)}, u32[]{:S(2)}, u32[]{:S(2)}) collective-permute-start(f32[1256,128]{1,0:T(8,128)S(1)} %get-tuple-element.17), channel_id=1, source_target_pairs={{0,16},{16,32},{32,48},{48,64},{64,80},{80,96},{96,112},{112,128},... | collective-permute-start | bytes 1929224 | tf_op jit(solution)/shard_map/ppermute | solution.py:371
  25.0 0.0 copy-start.2
  25.0 1.9 %collective-permute-start.3 = (f32[1256,128]{1,0:T(8,128)S(1)}, f32[1256,128]{1,0:T(8,128)S(1)}, u32[]{:S(2)}, u32[]{:S(2)}) collective-permute-start(f32[1256,128]{1,0:T(8,128)S(1)} %get-tuple-element.18), channel_id=1, source_target_pairs={{0,496},{16,0},{32,16},{48,32},{64,48},{80,64},{96,80},{112,96},{1... | collective-permute-start | bytes 1929224 | tf_op jit(solution)/shard_map/ppermute | solution.py:371
  27.0 4.2 %collective-permute-start.5 = (f32[512,128]{1,0:T(8,128)S(1)}, f32[512,128]{1,0:T(8,128)S(1)}, u32[]{:S(2)}, u32[]{:S(2)}) collective-permute-start(f32[512,128]{1,0:T(8,128)S(1)} %get-tuple-element.25), channel_id=1, source_target_pairs={{0,480},{16,496},{32,0},{48,16},{64,32},{80,48},{96,64},{112,80},{... | collective-permute-start | bytes 786440 | tf_op jit(solution)/shard_map/ppermute | solution.py:371
  31.2 1.9 %collective-permute-start.4 = (f32[512,128]{1,0:T(8,128)S(1)}, f32[512,128]{1,0:T(8,128)S(1)}, u32[]{:S(2)}, u32[]{:S(2)}) collective-permute-start(f32[512,128]{1,0:T(8,128)S(1)} %get-tuple-element.26), channel_id=1, source_target_pairs={{0,32},{16,48},{32,64},{48,80},{64,96},{80,112},{96,128},{112,144}... | collective-permute-start | bytes 786440 | tf_op jit(solution)/shard_map/ppermute | solution.py:371
  33.1 4.2 %collective-permute-done.5.right2_ref = f32[512,128]{1,0:T(8,128)S(1)} collective-permute-done((f32[512,128]{1,0:T(8,128)S(1)}, f32[512,128]{1,0:T(8,128)S(1)}, u32[]{:S(2)}, u32[]{:S(2)}) %collective-permute-start.5) | collective-permute-done | bytes 262176 | tf_op jit(solution)/shard_map/ppermute | solution.py:371
  37.3 4.0 %collective-permute-done.4.left2_ref = f32[512,128]{1,0:T(8,128)S(1)} collective-permute-done((f32[512,128]{1,0:T(8,128)S(1)}, f32[512,128]{1,0:T(8,128)S(1)}, u32[]{:S(2)}, u32[]{:S(2)}) %collective-permute-start.4) | collective-permute-done | bytes 262176 | tf_op jit(solution)/shard_map/ppermute | solution.py:371
  41.3 0.0 collective-permute-done.2.left_ref
  41.3 0.0 collective-permute-done.3.right_ref
  41.3 0.0 copy-done.2
  41.3 3.4 %basis.1 = (bf16[128,4096]{1,0:T(8,128)(2,1)S(1)}, bf16[128,4096]{1,0:T(8,128)(2,1)S(1)}, f32[64,128]{1,0:T(8,128)S(1)}) custom-call(f32[1024,128]{1,0:T(8,128)S(1)} %get-tuple-element.14.own_ref, f32[32,128]{1,0:T(8,128)S(1)} %bitcast.8, f32[200,128]{1,0:T(8,128)S(1)} %collective-permute-done.low_ref, f32[200,128]{1,0:T(8,128)S(1)} %collective-permute-done.1.high_ref, ...), custom_call_target="tpu_custom_call" | custom-call | tf_op jit(solution)/shard_map/basis/pallas_call | solution.py:230
  44.8 9.9 %all_to_all.15 = f32[8,8,128]{2,1,0:T(8,128)S(1)} all-to-all(f32[8,8,128]{2,1,0:T(8,128)S(1)} %bitcast.10), channel_id=1, replica_groups=mesh['gx_0'=2,'gx_1'=8,'gx_2'=2,'gy_0'=8,'gy_1'=2] {'gx_0','gx_2','gy_1'}, dimensions={0} | all-to-all | bytes 65536 | tf_op jit(solution)/shard_map/all_to_all | solution.py:375
  54.7 25.9 %all_to_all.16 = f32[64,8,128]{2,1,0:T(8,128)S(1)} all-to-all(f32[64,8,128]{2,1,0:T(8,128)S(1)} %broadcast_in_dim.4), channel_id=1, replica_groups=mesh['gx_0'=2,'gx_1'=8,'gx_2'=2,'gy_0'=8,'gy_1'=2] {'gx_1','gy_0'}, dimensions={0} | all-to-all | bytes 524288 | tf_op jit(solution)/shard_map/all_to_all | solution.py:375
  80.6 0.1 reduce_sum.19
  80.7 10.1 %all_to_all.17 = f32[8,8,128]{2,1,0:T(8,128)S(1)} all-to-all(f32[8,8,128]{2,1,0:T(8,128)S(1)} %broadcast_in_dim.5), channel_id=1, replica_groups=mesh['gx_0'=2,'gx_1'=8,'gx_2'=2,'gy_0'=8,'gy_1'=2] {'gx_0','gx_2','gy_1'}, dimensions={0} | all-to-all | bytes 65536 | tf_op jit(solution)/shard_map/all_to_all | solution.py:375
  90.8 5.9 %finish.1 = (f32[3,32,32]{2,1,0:T(8,128)}, f32[3,32,32]{2,1,0:T(8,128)}, f32[1024,128]{1,0:T(8,128)}) custom-call(f32[64,128]{1,0:T(8,128)S(1)} %bitcast.9, bf16[128,4096]{1,0:T(8,128)(2,1)S(1)} %get-tuple-element.20.high_ref, bf16[128,4096]{1,0:T(8,128)(2,1)S(1)} %get-tuple-element.21.low_ref), custom_call_target="tpu_custom_call" | custom-call | tf_op jit(solution)/shard_map/finish/pallas_call | solution.py:354
  (4 shorter events, 0.1 us)
Async XLA Ops:
  0.6 1.0 %copy-start = (s32[32,2,16,128]{3,2,1,0:T(8,128)S(1)}, s32[32,2,16,128]{3,2,1,0:T(8,128)}, u32[]{:S(2)}) copy-start(s32[32,2,16,128]{3,2,1,0:T(8,128)} %param.2) | copy-start | bytes 1572868
  1.7 0.7 copy-start.1
  2.7 16.5 %collective-permute-start = (f32[200,128]{1,0:T(8,128)S(1)}, f32[200,128]{1,0:T(8,128)S(1)}, u32[]{:S(2)}, u32[]{:S(2)}) collective-permute-start(f32[200,128]{1,0:T(8,128)S(1)} %get-tuple-element.15), channel_id=1, source_target_pairs={{0,1},{1,2},{2,3},{3,4},{4,5},{5,6},{6,7},{7,8},{8,9},{9,10},{10,1... | collective-permute-start | bytes 307208 | tf_op jit(solution)/shard_map/ppermute | solution.py:371
  8.2 12.1 %collective-permute-start.1 = (f32[200,128]{1,0:T(8,128)S(1)}, f32[200,128]{1,0:T(8,128)S(1)}, u32[]{:S(2)}, u32[]{:S(2)}) collective-permute-start(f32[200,128]{1,0:T(8,128)S(1)} %get-tuple-element.16), channel_id=1, source_target_pairs={{0,15},{1,0},{2,1},{3,2},{4,3},{5,4},{6,5},{7,6},{8,7},{9,8},{10,9... | collective-permute-start | bytes 307208 | tf_op jit(solution)/shard_map/ppermute | solution.py:371
  20.4 20.9 %collective-permute-start.2 = (f32[1256,128]{1,0:T(8,128)S(1)}, f32[1256,128]{1,0:T(8,128)S(1)}, u32[]{:S(2)}, u32[]{:S(2)}) collective-permute-start(f32[1256,128]{1,0:T(8,128)S(1)} %get-tuple-element.17), channel_id=1, source_target_pairs={{0,16},{16,32},{32,48},{48,64},{64,80},{80,96},{96,112},{112,128},... | collective-permute-start | bytes 1929224 | tf_op jit(solution)/shard_map/ppermute | solution.py:371
  25.0 16.3 %copy-start.2 = (f32[2,16,128]{2,1,0:T(8,128)S(1)}, f32[2,16,128]{2,1,0:T(8,128)}, u32[]{:S(2)}) copy-start(f32[2,16,128]{2,1,0:T(8,128)} %param.3) | copy-start | bytes 49156
  25.0 16.3 %collective-permute-start.3 = (f32[1256,128]{1,0:T(8,128)S(1)}, f32[1256,128]{1,0:T(8,128)S(1)}, u32[]{:S(2)}, u32[]{:S(2)}) collective-permute-start(f32[1256,128]{1,0:T(8,128)S(1)} %get-tuple-element.18), channel_id=1, source_target_pairs={{0,496},{16,0},{32,16},{48,32},{64,48},{80,64},{96,80},{112,96},{1... | collective-permute-start | bytes 1929224 | tf_op jit(solution)/shard_map/ppermute | solution.py:371
  27.0 10.3 %collective-permute-start.5 = (f32[512,128]{1,0:T(8,128)S(1)}, f32[512,128]{1,0:T(8,128)S(1)}, u32[]{:S(2)}, u32[]{:S(2)}) collective-permute-start(f32[512,128]{1,0:T(8,128)S(1)} %get-tuple-element.25), channel_id=1, source_target_pairs={{0,480},{16,496},{32,0},{48,16},{64,32},{80,48},{96,64},{112,80},{... | collective-permute-start | bytes 786440 | tf_op jit(solution)/shard_map/ppermute | solution.py:371
  31.2 10.1 %collective-permute-start.4 = (f32[512,128]{1,0:T(8,128)S(1)}, f32[512,128]{1,0:T(8,128)S(1)}, u32[]{:S(2)}, u32[]{:S(2)}) collective-permute-start(f32[512,128]{1,0:T(8,128)S(1)} %get-tuple-element.26), channel_id=1, source_target_pairs={{0,32},{16,48},{32,64},{48,80},{64,96},{80,112},{96,128},{112,144}... | collective-permute-start | bytes 786440 | tf_op jit(solution)/shard_map/ppermute | solution.py:371

commit v3 on v2

--- a/solution.py
+++ b/solution.py
@@ -11,6 +11,7 @@
 GY = ("gy_0", "gy_1")
 NEAR = ("gx_0", "gx_2", "gy_1")
 FAR = ("gx_1", "gy_0")
+CORE = "gx_2"
 
 PROBES = 32
 LANES = 128
@@ -26,9 +27,10 @@
 INTERPRET = False
 VMEM_LIMIT = 16 * 2**20
 
-Y_ROWS = 2 * 3 * PROBES
-X_BLOCKS = 20 + 18
-X_ROWS = X_BLOCKS * PROBES
+OWN_ROWS = CELLS * PROBES + CELLS
+EDGE_ROWS = 2 * 3 * PROBES + 8
+CORNER_ROWS = 6 * PROBES + 8
+CROSS_ROWS = ROWS * PROBES + CORNER_ROWS
 
 
 def vmem_specs(count):
@@ -47,82 +49,79 @@
     return pl.ds(index * PROBES, PROBES)
 
 
-def prepare_kernel(signs_ref, diag_ref, own_ref, up_ref, down_ref):
+def prepare_kernel(mirror_ref, signs_ref, diag_ref, own_ref, far_ref, high_ref, low_ref):
+    flip_plane = mirror_ref[0]
+    flip_row = mirror_ref[1] * (ROWS - 1)
     for cell in range(CELLS):
         plane, row = divmod(cell, ROWS)
-        bits = signs_ref[pl.ds(cell, PROBES, stride=CELLS), :]
+        source = (flip_plane ^ plane) * ROWS + (flip_row ^ row)
+        bits = signs_ref[pl.ds(source, PROBES, stride=CELLS), :]
         probes = (2 * bits - 1).astype(F32)
+        line = diag_ref[pl.ds(source, 1), :]
         own_ref[row_of(cell), :] = probes
-        if row < 3:
-            down_ref[row_of(plane * 3 + row), :] = probes
-        if row >= ROWS - 3:
-            up_ref[row_of(plane * 3 + row - (ROWS - 3)), :] = probes
-    for plane in range(PLANES):
-        base = plane * ROWS
-        down_ref[Y_ROWS + 2 * plane : Y_ROWS + 2 * plane + 2, :] = diag_ref[base : base + 2, :]
-        up_ref[Y_ROWS + 2 * plane : Y_ROWS + 2 * plane + 2, :] = diag_ref[base + ROWS - 2 : base + ROWS, :]
-    down_ref[Y_ROWS + 4 : Y_ROWS + 8, :] = jnp.zeros((4, LANES), F32)
-    up_ref[Y_ROWS + 4 : Y_ROWS + 8, :] = jnp.zeros((4, LANES), F32)
-
-
-def prepare(signs, diagonal):
+        own_ref[CELLS * PROBES + cell : CELLS * PROBES + cell + 1, :] = line
+        if plane == 1:
+            far_ref[row_of(row), :] = probes
+        for ref, step in ((low_ref, row), (high_ref, ROWS - 1 - row)):
+            if step < 3:
+                ref[row_of(plane * 3 + step), :] = probes
+            if step < 2:
+                start = 6 * PROBES + plane * 2 + step
+                ref[start : start + 1, :] = line
+    for ref in (low_ref, high_ref):
+        ref[6 * PROBES + 4 :, :] = jnp.zeros((4, LANES), F32)
+
+
+def prepare(mirror, signs, diagonal):
     return pl.pallas_call(
         prepare_kernel,
-        out_shape=(shaped(CELLS * PROBES, LANES), shaped(Y_ROWS + 8, LANES), shaped(Y_ROWS + 8, LANES)),
-        in_specs=vmem_specs(2),
-        out_specs=tuple(vmem_specs(3)),
+        out_shape=(
+            shaped(OWN_ROWS, LANES),
+            shaped(ROWS * PROBES, LANES),
+            shaped(EDGE_ROWS, LANES),
+            shaped(EDGE_ROWS, LANES),
+        ),
+        in_specs=[pl.BlockSpec(memory_space=pltpu.SMEM)] + vmem_specs(2),
+        out_specs=tuple(vmem_specs(4)),
         compiler_params=pltpu.CompilerParams(vmem_limit_bytes=VMEM_LIMIT),
         interpret=INTERPRET,
         name="prepare",
-    )(signs, diagonal)
-
-
-def pack_kernel(own_ref, diag_ref, low_ref, high_ref, plus_ref, minus_ref):
-    def cell_of(plane, row):
+    )(mirror, signs, diagonal)
+
+
+def pack_kernel(high_ref, low_ref, near_ref, corner_ref, cross_ref):
+    def edge(plane, row):
         if row < 0:
-            return low_ref[row_of(plane * 3 + row + 3), :]
-        if row >= ROWS:
-            return high_ref[row_of(plane * 3 + row - ROWS), :]
-        return own_ref[row_of(plane * ROWS + row), :]
-
-    def diag_of(plane, row):
-        if row < 0:
-            start = Y_ROWS + 2 * plane + row + 2
-            return low_ref[start : start + 1, :]
-        if row >= ROWS:
-            start = Y_ROWS + 2 * plane + row - ROWS
-            return high_ref[start : start + 1, :]
-        return diag_ref[plane * ROWS + row : plane * ROWS + row + 1, :]
-
-    for ref, near in ((plus_ref, 1), (minus_ref, 0)):
-        far = 1 - near
-        block = 0
-        for row in range(-2, ROWS + 2):
-            ref[row_of(block), :] = cell_of(near, row)
-            block += 1
-        for row in range(-1, ROWS + 1):
-            ref[row_of(block), :] = cell_of(far, row)
-            block += 1
-        line = X_ROWS
-        for row in range(-1, ROWS + 1):
-            ref[line : line + 1, :] = diag_of(near, row)
-            line += 1
-        for row in range(ROWS):
-            ref[line : line + 1, :] = diag_of(far, row)
-            line += 1
-        ref[line : line + 6, :] = jnp.zeros((6, LANES), F32)
-
-
-def pack(own, diagonal, low, high):
+            return low_ref[row_of(plane * 3 - row - 1), :]
+        return high_ref[row_of(plane * 3 + row - ROWS), :]
+
+    def edge_line(plane, row):
+        ref = low_ref if row < 0 else high_ref
+        start = 6 * PROBES + plane * 2
+        return ref[start : start + 1, :]
+
+    for row in range(ROWS):
+        cross_ref[row_of(row), :] = near_ref[row_of(row), :]
+    for ref, plane, first in ((corner_ref, 0, 0), (cross_ref, 1, ROWS)):
+        for place, row in enumerate((-2, -1, ROWS, ROWS + 1)):
+            ref[row_of(first + place), :] = edge(plane, row)
+        for place, row in enumerate((-1, ROWS)):
+            ref[row_of(first + 4 + place), :] = edge(1 - plane, row)
+            start = (first + 6) * PROBES + place
+            ref[start : start + 1, :] = edge_line(plane, row)
+        ref[(first + 6) * PROBES + 2 :, :] = jnp.zeros((6, LANES), F32)
+
+
+def pack(high, low, near):
     return pl.pallas_call(
         pack_kernel,
-        out_shape=(shaped(X_ROWS + 40, LANES), shaped(X_ROWS + 40, LANES)),
-        in_specs=vmem_specs(4),
+        out_shape=(shaped(CORNER_ROWS, LANES), shaped(CROSS_ROWS, LANES)),
+        in_specs=vmem_specs(3),
         out_specs=tuple(vmem_specs(2)),
         compiler_params=pltpu.CompilerParams(vmem_limit_bytes=VMEM_LIMIT),
         interpret=INTERPRET,
         name="pack",
-    )(*held(own), diagonal, *held(low, high))
+    )(*held(high, low, near))
 
 
 def nt_dot(left, right, precision=None):
@@ -132,7 +131,7 @@
 
 
 def basis_kernel(
-    own_ref, diag_ref, low_ref, high_ref, left_ref, right_ref, left2_ref, right2_ref,
+    own_ref, high_ref, low_ref, near_ref, beside_ref, far_ref, corner_ref, cross_ref,
     high_out, low_out, gram_ref, first_ref, second_ref,
 ):
     def distance(plane):
@@ -142,33 +141,38 @@
         away = distance(plane)
         if away == 0:
             if row < 0:
-                return low_ref[row_of(plane * 3 + row + 3), :]
+                return low_ref[row_of(plane * 3 - row - 1), :]
             if row >= ROWS:
                 return high_ref[row_of(plane * 3 + row - ROWS), :]
             return own_ref[row_of(plane * ROWS + row), :]
-        side, side2 = (left_ref, left2_ref) if plane < 0 else (right_ref, right2_ref)
-        if away == 1:
-            return side[row_of(row + 2), :]
-        if away == 2:
-            return side[row_of(20 + row + 1), :]
-        return side2[row_of(row), :]
+        if away == 3:
+            return (far_ref if plane < 0 else cross_ref)[row_of(row), :]
+        if 0 <= row < ROWS:
+            if plane < 0:
+                return near_ref[row_of((away - 1) * ROWS + row), :]
+            return beside_ref[row_of((2 - away) * ROWS + row), :]
+        ref, first = (corner_ref, 0) if plane < 0 else (cross_ref, ROWS)
+        places = (-2, -1, ROWS, ROWS + 1) if away == 1 else (-1, ROWS)
+        return ref[row_of(first + 4 * (away - 1) + places.index(row)), :]
 
     def factor(plane, row):
         away = distance(plane)
         if away == 0:
             if row < 0:
-                start = Y_ROWS + 2 * plane + row + 2
-                line = low_ref[start : start + 1, :]
+                ref, start = low_ref, 6 * PROBES + plane * 2 - row - 1
             elif row >= ROWS:
-                start = Y_ROWS + 2 * plane + row - ROWS
-                line = high_ref[start : start + 1, :]
+                ref, start = high_ref, 6 * PROBES + plane * 2 + row - ROWS
             else:
-                line = diag_ref[plane * ROWS + row : plane * ROWS + row + 1, :]
+                ref, start = own_ref, CELLS * PROBES + plane * ROWS + row
+        elif 0 <= row < ROWS:
+            if plane < 0:
+                ref, start = near_ref, CELLS * PROBES + (away - 1) * ROWS + row
+            else:
+                ref, start = beside_ref, CELLS * PROBES + (2 - away) * ROWS + row
         else:
-            side = left_ref if plane < 0 else right_ref
-            start = X_ROWS + (row + 1 if away == 1 else 18 + row)
-            line = side[start : start + 1, :]
-        return line + (6.0 - SHIFT)
+            ref, first = (corner_ref, 0) if plane < 0 else (cross_ref, ROWS)
+            start = (first + 6) * PROBES + (0 if row < 0 else 1)
+        return ref[start : start + 1, :] + (6.0 - SHIFT)
 
     def cells(width):
         found = []
@@ -295,7 +299,7 @@
     return jnp.concatenate(solved, 0), jnp.concatenate(upper, 0)
 
 
-def finish_kernel(gram_ref, high_ref, low_ref, alpha_ref, beta_ref, next_ref):
+def finish_kernel(mirror_ref, gram_ref, high_ref, low_ref, alpha_ref, beta_ref, next_ref):
     exact = lax.Precision.HIGHEST
     lane = lax.broadcasted_iota(jnp.int32, (PROBES, LANES), 1)
     block_of = lane // PROBES
@@ -333,8 +337,12 @@
     result = jnp.dot(upper, high, preferred_element_type=F32)
     result = result + jnp.dot(upper, low_ref[...], preferred_element_type=F32)
     result = result + jnp.dot(lower, high, preferred_element_type=F32)
+    flip_plane = mirror_ref[0]
+    flip_row = mirror_ref[1] * (ROWS - 1)
     for cell in range(CELLS):
-        next_ref[pl.ds(cell, PROBES, stride=CELLS), :] = result[:, cell * LANES : (cell + 1) * LANES]
+        plane, row = divmod(cell, ROWS)
+        target = (flip_plane ^ plane) * ROWS + (flip_row ^ row)
+        next_ref[pl.ds(target, PROBES, stride=CELLS), :] = result[:, cell * LANES : (cell + 1) * LANES]
     row32 = lax.broadcasted_iota(jnp.int32, (PROBES, PROBES), 0)
     lane32 = lax.broadcasted_iota(jnp.int32, (PROBES, PROBES), 1)
     beta = None
@@ -350,7 +358,7 @@
         beta_ref[block] = jnp.where(row32 <= lane32, beta, 0.0)
 
 
-def finish(gram, high, low):
+def finish(mirror, gram, high, low):
     return pl.pallas_call(
         finish_kernel,
         out_shape=(
@@ -358,17 +366,33 @@
             jax.ShapeDtypeStruct((3, PROBES, PROBES), F32),
             jax.ShapeDtypeStruct((PROBES * CELLS, LANES), F32),
         ),
-        in_specs=vmem_specs(3),
+        in_specs=[pl.BlockSpec(memory_space=pltpu.SMEM)] + vmem_specs(3),
         out_specs=tuple(vmem_specs(3)),
         compiler_params=pltpu.CompilerParams(vmem_limit_bytes=VMEM_LIMIT),
         interpret=INTERPRET,
         name="finish",
-    )(*held(gram, high, low))
-
-
-def shifted(x, axes, steps):
-    count = lax.axis_size(axes)
-    return lax.ppermute(x, axes, [(i, (i + steps) % count) for i in range(count)])
+    )(mirror, *held(gram, high, low))
+
+
+def off_chip(x):
+    count = lax.axis_size(GX)
+    return lax.ppermute(x, GX, [(i, (i - 1 if i % 2 == 0 else i + 1) % count) for i in range(count)])
+
+
+def same_core(x):
+    count = lax.axis_size(GX)
+    return lax.ppermute(x, GX, [(i, (i + 2 if i % 2 == 0 else i - 2) % count) for i in range(count)])
+
+
+def on_chip(x):
+    count = lax.axis_size(CORE)
+    return lax.ppermute(x, CORE, [(i, count - 1 - i) for i in range(count)])
+
+
+def row_pair(x, offset):
+    count = lax.axis_size(GY)
+    step = lambda i: i + 1 if i % 2 == offset else i - 1
+    return lax.ppermute(x, GY, [(i, step(i) % count) for i in range(count)])
 
 
 def exchanged(x, axes):
@@ -389,17 +413,18 @@
 def per_device(probe_signs, diagonal):
     signs = probe_signs.reshape(PROBES * CELLS, LANES)
     diag = diagonal.reshape(CELLS, LANES)
-    own, up, down = prepare(signs, diag)
-    half = ROWS * PROBES
-    low = shifted(up, GY, 1)
-    high = shifted(down, GY, -1)
-    left2 = shifted(own[half:], GX, 2)
-    right2 = shifted(own[:half], GX, -2)
-    plus, minus = pack(own, diag, low, high)
-    left = shifted(plus, GX, 1)
-    right = shifted(minus, GX, -1)
-    upper, lower, gram = basis(own, diag, low, high, left, right, left2, right2)
-    alphas, betas, following = finish(reduced(gram), upper, lower)
+    mirror = jnp.stack([lax.axis_index(CORE), lax.axis_index("gy_1")]).astype(jnp.int32)
+    own, outer, top, bottom = prepare(mirror, signs, diag)
+    near = off_chip(own)
+    high = row_pair(top, 0)
+    low = row_pair(bottom, 1)
+    far = same_core(outer)
+    beside = on_chip(own)
+    corner_message, cross_message = pack(high, low, near)
+    corner = off_chip(corner_message)
+    cross = on_chip(cross_message)
+    upper, lower, gram = basis(own, high, low, near, beside, far, corner, cross)
+    alphas, betas, following = finish(mirror, reduced(gram), upper, lower)
     return (alphas, betas, following.reshape(PROBES, PLANES, ROWS, LANES))
 
 

time: 97.3 us -> 94.5 us (0.971)
  blocking collectives: 46 us -> 40.8 us
  starting transfers between devices: 28.5 us -> 32.1 us
  waiting for transfers between devices: 9.83 us -> 7.29 us
  Pallas kernels: 9.84 us -> 11.2 us
    all_to_all x3, blocking collectives: 46 us -> 40.8 us  [exchanged(): return lax.all_to_all(x, axes, 0, 0, tiled=True)]
    ppermute x6 -> x7, starting transfers between devices: 28.5 us -> 32.1 us  [the longest x2 13.7 us: row_pair(): return lax.ppermute(x, GY, [(i, step(i) % count) for i in range(count)])]
    ppermute x6 -> x7, waiting for transfers between devices: 9.83 us -> 7.29 us  [the longest x2 2.94 us: row_pair(): return lax.ppermute(x, GY, [(i, step(i) % count) for i in range(count)])]
  transfers between devices with their start and end apart: 6 -> 7, of which waited for: 4 -> 3; matrix products, arithmetic and copies ran while one was open for 0% -> 0% of each run, Pallas kernels for 0% -> 0%
where the time goes in v3:
time: 94.5 us; the launch traced here: 94 us
  blocking collectives  40.8 us (43%)
  starting transfers between devices  32.1 us (34%)
  Pallas kernels  11.2 us (12%)
  waiting for transfers between devices  7.29 us (8%)
  local copies, waits for them, and re-layouts  1.7 us (2%)
    all_to_all x3, blocking collectives, exchanged(): return lax.all_to_all(x, axes, 0, 0, tiled=True)  40.8 us
    ppermute x2, starting transfers between devices, row_pair(): return lax.ppermute(x, GY, [(i, step(i) % count) for i in range(count)])  13.7 us
    ppermute x2, starting transfers between devices, on_chip(): return lax.ppermute(x, CORE, [(i, count - 1 - i) for i in range(count)])  8.86 us
    pallas_call x1, Pallas kernels, finish(): pl.pallas_call(finish_kernel, out_shape=(jax.ShapeDtypeStruct((3, PROBES,...  6.68 us
    ppermute x2, starting transfers between devices, off_chip(): lax.ppermute(x, GX, [(i, (i - 1 if i % 2 == 0 else i + 1) % count) for i...  6.5 us
    pallas_call x1, Pallas kernels, basis(): pl.pallas_call(basis_kernel, out_shape=(shaped(4 * PROBES, width, dtype=B...  3.34 us
    ppermute x1, starting transfers between devices, same_core(): lax.ppermute(x, GX, [(i, (i + 2 if i % 2 == 0 else i - 2) % count) for i...  2.98 us
    ppermute x2, waiting for transfers between devices, row_pair(): return lax.ppermute(x, GY, [(i, step(i) % count) for i in range(count)])  2.94 us
  transfers between devices with their start and end apart: 7, of which 3 were waited for; matrix products, arithmetic and copies ran while one was open for 0% of the time, Pallas kernels for 0%

profile of v3, /device:TPU:1, one launch (start us, length us, event | category | flops | bytes accessed | tf_op | source)
XLA Modules:
  0.0 94.0 jit_solution(11201598822205328852)
XLA Ops:
  0.6 0.0 copy-start.1
  0.6 0.1 pad_add_fusion.mirror_ref
  0.7 0.6 copy-done.1
  1.3 0.0 copy-start
  1.4 1.0 %copy-done = s32[32,2,16,128]{3,2,1,0:T(8,128)S(1)} copy-done((s32[32,2,16,128]{3,2,1,0:T(8,128)S(1)}, s32[32,2,16,128]{3,2,1,0:T(8,128)}, u32[]{:S(2)}) %copy-start) | copy-done | bytes 524312
  2.4 1.1 %prepare.1 = (f32[1056,128]{1,0:T(8,128)S(1)}, f32[512,128]{1,0:T(8,128)S(1)}, f32[200,128]{1,0:T(8,128)S(1)}, f32[200,128]{1,0:T(8,128)S(1)}) custom-call(s32[2]{0:T(128)S(1)} %pad_add_fusion.mirror_ref, s32[1024,128]{1,0:T(8,128)S(1)} %bitcast.7, f32[32,128]{1,0:T(8,128)S(1)} %bitcast.10), custom_call_target="tpu_custom_call" | custom-call | tf_op jit(solution)/shard_map/prepare/pallas_call | solution.py:76
  3.5 4.6 %collective-permute-start.2 = (f32[1056,128]{1,0:T(8,128)S(1)}, f32[1056,128]{1,0:T(8,128)S(1)}, u32[]{:S(2)}, u32[]{:S(2)}) collective-permute-start(f32[1056,128]{1,0:T(8,128)S(1)} %get-tuple-element.15.own_ref), channel_id=1, source_target_pairs={{0,496},{16,32},{32,16},{48,64},{64,48},{80,96},{96,80},{112,128},... | collective-permute-start | bytes 1622024 | tf_op jit(solution)/shard_map/ppermute | solution.py:379
  8.1 6.1 %collective-permute-start.3 = (f32[1056,128]{1,0:T(8,128)S(1)}, f32[1056,128]{1,0:T(8,128)S(1)}, u32[]{:S(2)}, u32[]{:S(2)}) collective-permute-start(f32[1056,128]{1,0:T(8,128)S(1)} %get-tuple-element.15.own_ref), channel_id=1, source_target_pairs={{0,16},{16,0},{1,17},{17,1},{2,18},{18,2},{3,19},{19,3},{4,20},{20... | collective-permute-start | bytes 1622024 | tf_op jit(solution)/shard_map/ppermute | solution.py:389
  14.2 2.8 %collective-permute-start = (f32[200,128]{1,0:T(8,128)S(1)}, f32[200,128]{1,0:T(8,128)S(1)}, u32[]{:S(2)}, u32[]{:S(2)}) collective-permute-start(f32[200,128]{1,0:T(8,128)S(1)} %get-tuple-element.16), channel_id=1, source_target_pairs={{0,1},{1,0},{2,3},{3,2},{4,5},{5,4},{6,7},{7,6},{8,9},{9,8},{10,11... | collective-permute-start | bytes 307208 | tf_op jit(solution)/shard_map/ppermute | solution.py:395
  17.0 10.9 %collective-permute-start.1 = (f32[200,128]{1,0:T(8,128)S(1)}, f32[200,128]{1,0:T(8,128)S(1)}, u32[]{:S(2)}, u32[]{:S(2)}) collective-permute-start(f32[200,128]{1,0:T(8,128)S(1)} %get-tuple-element.17), channel_id=1, source_target_pairs={{0,15},{1,2},{2,1},{3,4},{4,3},{5,6},{6,5},{7,8},{8,7},{9,10},{10,... | collective-permute-start | bytes 307208 | tf_op jit(solution)/shard_map/ppermute | solution.py:395
  27.9 0.0 collective-permute-done.high_ref
  28.0 2.9 %collective-permute-done.1.low_ref = f32[200,128]{1,0:T(8,128)S(1)} collective-permute-done((f32[200,128]{1,0:T(8,128)S(1)}, f32[200,128]{1,0:T(8,128)S(1)}, u32[]{:S(2)}, u32[]{:S(2)}) %collective-permute-start.1) | collective-permute-done | bytes 102432 | tf_op jit(solution)/shard_map/ppermute | solution.py:395
  30.9 0.0 collective-permute-done.2.near_ref
  30.9 2.8 %collective-permute-start.6 = (f32[712,128]{1,0:T(8,128)S(1)}, f32[712,128]{1,0:T(8,128)S(1)}, u32[]{:S(2)}, u32[]{:S(2)}) collective-permute-start(f32[712,128]{1,0:T(8,128)S(1)} %get-tuple-element.20), channel_id=1, source_target_pairs={{0,16},{16,0},{1,17},{17,1},{2,18},{18,2},{3,19},{19,3},{4,20},{20... | collective-permute-start | bytes 1093640 | tf_op jit(solution)/shard_map/ppermute | solution.py:389
  33.7 3.0 %collective-permute-start.4 = (f32[512,128]{1,0:T(8,128)S(1)}, f32[512,128]{1,0:T(8,128)S(1)}, u32[]{:S(2)}, u32[]{:S(2)}) collective-permute-start(f32[512,128]{1,0:T(8,128)S(1)} %get-tuple-element.18), channel_id=1, source_target_pairs={{0,32},{16,496},{32,64},{48,16},{64,96},{80,48},{96,128},{112,80},... | collective-permute-start | bytes 786440 | tf_op jit(solution)/shard_map/ppermute | solution.py:384
  36.7 1.9 %collective-permute-start.5 = (f32[200,128]{1,0:T(8,128)S(1)}, f32[200,128]{1,0:T(8,128)S(1)}, u32[]{:S(2)}, u32[]{:S(2)}) collective-permute-start(f32[200,128]{1,0:T(8,128)S(1)} %get-tuple-element.19), channel_id=1, source_target_pairs={{0,496},{16,32},{32,16},{48,64},{64,48},{80,96},{96,80},{112,128},... | collective-permute-start | bytes 307208 | tf_op jit(solution)/shard_map/ppermute | solution.py:379
  38.6 2.5 %collective-permute-done.4.far_ref = f32[512,128]{1,0:T(8,128)S(1)} collective-permute-done((f32[512,128]{1,0:T(8,128)S(1)}, f32[512,128]{1,0:T(8,128)S(1)}, u32[]{:S(2)}, u32[]{:S(2)}) %collective-permute-start.4) | collective-permute-done | bytes 262176 | tf_op jit(solution)/shard_map/ppermute | solution.py:384
  41.1 0.0 collective-permute-done.3.beside_ref
  41.1 1.8 %collective-permute-done.5.corner_ref = f32[200,128]{1,0:T(8,128)S(1)} collective-permute-done((f32[200,128]{1,0:T(8,128)S(1)}, f32[200,128]{1,0:T(8,128)S(1)}, u32[]{:S(2)}, u32[]{:S(2)}) %collective-permute-start.5) | collective-permute-done | bytes 102432 | tf_op jit(solution)/shard_map/ppermute | solution.py:379
  43.0 0.0 collective-permute-done.6.cross_ref
  43.0 3.3 %basis.1 = (bf16[128,4096]{1,0:T(8,128)(2,1)S(1)}, bf16[128,4096]{1,0:T(8,128)(2,1)S(1)}, f32[64,128]{1,0:T(8,128)S(1)}) custom-call(f32[1056,128]{1,0:T(8,128)S(1)} %get-tuple-element.15.own_ref, f32[200,128]{1,0:T(8,128)S(1)} %collective-permute-done.high_ref, f32[200,128]{1,0:T(8,128)S(1)} %collective-permute-done.1.low_ref, ...), custom_call_target="tpu_custom_call" | custom-call | tf_op jit(solution)/shard_map/basis/pallas_call | solution.py:234
  46.3 9.5 %all_to_all.15 = f32[8,8,128]{2,1,0:T(8,128)S(1)} all-to-all(f32[8,8,128]{2,1,0:T(8,128)S(1)} %bitcast.9), channel_id=1, replica_groups=mesh['gx_0'=2,'gx_1'=8,'gx_2'=2,'gy_0'=8,'gy_1'=2] {'gx_0','gx_2','gy_1'}, dimensions={0} | all-to-all | bytes 65536 | tf_op jit(solution)/shard_map/all_to_all | solution.py:399
  55.9 21.2 %all_to_all.16 = f32[64,8,128]{2,1,0:T(8,128)S(1)} all-to-all(f32[64,8,128]{2,1,0:T(8,128)S(1)} %broadcast_in_dim.4), channel_id=1, replica_groups=mesh['gx_0'=2,'gx_1'=8,'gx_2'=2,'gy_0'=8,'gy_1'=2] {'gx_1','gy_0'}, dimensions={0} | all-to-all | bytes 524288 | tf_op jit(solution)/shard_map/all_to_all | solution.py:399
  77.1 0.1 reduce_sum.19
  77.2 10.1 %all_to_all.17 = f32[8,8,128]{2,1,0:T(8,128)S(1)} all-to-all(f32[8,8,128]{2,1,0:T(8,128)S(1)} %broadcast_in_dim.5), channel_id=1, replica_groups=mesh['gx_0'=2,'gx_1'=8,'gx_2'=2,'gy_0'=8,'gy_1'=2] {'gx_0','gx_2','gy_1'}, dimensions={0} | all-to-all | bytes 65536 | tf_op jit(solution)/shard_map/all_to_all | solution.py:399
  87.3 6.7 %finish.1 = (f32[3,32,32]{2,1,0:T(8,128)}, f32[3,32,32]{2,1,0:T(8,128)}, f32[1024,128]{1,0:T(8,128)}) custom-call(s32[2]{0:T(128)S(1)} %pad_add_fusion.mirror_ref, f32[64,128]{1,0:T(8,128)S(1)} %bitcast.8, bf16[128,4096]{1,0:T(8,128)(2,1)S(1)} %get-tuple-element.22.high_ref, bf16[128,4096]{1,0:T(8,128)(2,1)S(1)} %get-tuple-element.23.low_ref), custom_call_target="tpu_custom_call" | custom-call | tf_op jit(solution)/shard_map/finish/pallas_call | solution.py:362
  (4 shorter events, 0.1 us)
Async XLA Ops:
  0.6 0.7 copy-start.1
  1.3 1.0 %copy-start = (s32[32,2,16,128]{3,2,1,0:T(8,128)S(1)}, s32[32,2,16,128]{3,2,1,0:T(8,128)}, u32[]{:S(2)}) copy-start(s32[32,2,16,128]{3,2,1,0:T(8,128)} %param.2) | copy-start | bytes 1572868
  3.5 27.4 %collective-permute-start.2 = (f32[1056,128]{1,0:T(8,128)S(1)}, f32[1056,128]{1,0:T(8,128)S(1)}, u32[]{:S(2)}, u32[]{:S(2)}) collective-permute-start(f32[1056,128]{1,0:T(8,128)S(1)} %get-tuple-element.15.own_ref), channel_id=1, source_target_pairs={{0,496},{16,32},{32,16},{48,64},{64,48},{80,96},{96,80},{112,128},... | collective-permute-start | bytes 1622024 | tf_op jit(solution)/shard_map/ppermute | solution.py:379
  8.1 33.0 %collective-permute-start.3 = (f32[1056,128]{1,0:T(8,128)S(1)}, f32[1056,128]{1,0:T(8,128)S(1)}, u32[]{:S(2)}, u32[]{:S(2)}) collective-permute-start(f32[1056,128]{1,0:T(8,128)S(1)} %get-tuple-element.15.own_ref), channel_id=1, source_target_pairs={{0,16},{16,0},{1,17},{17,1},{2,18},{18,2},{3,19},{19,3},{4,20},{20... | collective-permute-start | bytes 1622024 | tf_op jit(solution)/shard_map/ppermute | solution.py:389
  14.2 13.8 %collective-permute-start = (f32[200,128]{1,0:T(8,128)S(1)}, f32[200,128]{1,0:T(8,128)S(1)}, u32[]{:S(2)}, u32[]{:S(2)}) collective-permute-start(f32[200,128]{1,0:T(8,128)S(1)} %get-tuple-element.16), channel_id=1, source_target_pairs={{0,1},{1,0},{2,3},{3,2},{4,5},{5,4},{6,7},{7,6},{8,9},{9,8},{10,11... | collective-permute-start | bytes 307208 | tf_op jit(solution)/shard_map/ppermute | solution.py:395
  17.0 13.9 %collective-permute-start.1 = (f32[200,128]{1,0:T(8,128)S(1)}, f32[200,128]{1,0:T(8,128)S(1)}, u32[]{:S(2)}, u32[]{:S(2)}) collective-permute-start(f32[200,128]{1,0:T(8,128)S(1)} %get-tuple-element.17), channel_id=1, source_target_pairs={{0,15},{1,2},{2,1},{3,4},{4,3},{5,6},{6,5},{7,8},{8,7},{9,10},{10,... | collective-permute-start | bytes 307208 | tf_op jit(solution)/shard_map/ppermute | solution.py:395
  30.9 12.1 %collective-permute-start.6 = (f32[712,128]{1,0:T(8,128)S(1)}, f32[712,128]{1,0:T(8,128)S(1)}, u32[]{:S(2)}, u32[]{:S(2)}) collective-permute-start(f32[712,128]{1,0:T(8,128)S(1)} %get-tuple-element.20), channel_id=1, source_target_pairs={{0,16},{16,0},{1,17},{17,1},{2,18},{18,2},{3,19},{19,3},{4,20},{20... | collective-permute-start | bytes 1093640 | tf_op jit(solution)/shard_map/ppermute | solution.py:389
  33.7 7.4 %collective-permute-start.4 = (f32[512,128]{1,0:T(8,128)S(1)}, f32[512,128]{1,0:T(8,128)S(1)}, u32[]{:S(2)}, u32[]{:S(2)}) collective-permute-start(f32[512,128]{1,0:T(8,128)S(1)} %get-tuple-element.18), channel_id=1, source_target_pairs={{0,32},{16,496},{32,64},{48,16},{64,96},{80,48},{96,128},{112,80},... | collective-permute-start | bytes 786440 | tf_op jit(solution)/shard_map/ppermute | solution.py:384
  36.7 6.3 %collective-permute-start.5 = (f32[200,128]{1,0:T(8,128)S(1)}, f32[200,128]{1,0:T(8,128)S(1)}, u32[]{:S(2)}, u32[]{:S(2)}) collective-permute-start(f32[200,128]{1,0:T(8,128)S(1)} %get-tuple-element.19), channel_id=1, source_target_pairs={{0,496},{16,32},{32,16},{48,64},{64,48},{80,96},{96,80},{112,128},... | collective-permute-start | bytes 307208 | tf_op jit(solution)/shard_map/ppermute | solution.py:379

commit v4 on v3

--- a/solution.py
+++ b/solution.py
@@ -21,7 +21,7 @@
 SHIFT = 7.75
 B0 = 7.0
 B1 = 10.0
-PANEL = 8
+PANEL = 16
 F32 = jnp.float32
 BF16 = jnp.bfloat16
 INTERPRET = False
@@ -49,30 +49,56 @@
     return pl.ds(index * PROBES, PROBES)
 
 
-def prepare_kernel(mirror_ref, signs_ref, diag_ref, own_ref, far_ref, high_ref, low_ref):
+def prepare_kernel(
+    mirror_ref, signs_hbm, diag_hbm, own_ref, far_ref, high_ref, low_ref, signs_ref, diag_ref, arrived
+):
+    rows = 8 * CELLS
+    copies = []
+    for group in range(PROBES // 8):
+        part = pl.ds(group * rows, rows)
+        copies.append(pltpu.make_async_copy(signs_hbm.at[part, :], signs_ref.at[part, :], arrived.at[group]))
+    lines = pltpu.make_async_copy(diag_hbm, diag_ref, arrived.at[PROBES // 8])
+    lines.start()
+    for copy in copies:
+        copy.start()
     flip_plane = mirror_ref[0]
     flip_row = mirror_ref[1] * (ROWS - 1)
+
+    def source_of(cell):
+        plane, row = divmod(cell, ROWS)
+        return (flip_plane ^ plane) * ROWS + (flip_row ^ row)
+
+    lines.wait()
     for cell in range(CELLS):
         plane, row = divmod(cell, ROWS)
-        source = (flip_plane ^ plane) * ROWS + (flip_row ^ row)
-        bits = signs_ref[pl.ds(source, PROBES, stride=CELLS), :]
-        probes = (2 * bits - 1).astype(F32)
-        line = diag_ref[pl.ds(source, 1), :]
-        own_ref[row_of(cell), :] = probes
+        line = diag_ref[pl.ds(source_of(cell), 1), :]
         own_ref[CELLS * PROBES + cell : CELLS * PROBES + cell + 1, :] = line
-        if plane == 1:
-            far_ref[row_of(row), :] = probes
         for ref, step in ((low_ref, row), (high_ref, ROWS - 1 - row)):
-            if step < 3:
-                ref[row_of(plane * 3 + step), :] = probes
             if step < 2:
                 start = 6 * PROBES + plane * 2 + step
                 ref[start : start + 1, :] = line
     for ref in (low_ref, high_ref):
         ref[6 * PROBES + 4 :, :] = jnp.zeros((4, LANES), F32)
+    for group in range(PROBES // 8):
+        copies[group].wait()
+        for cell in range(CELLS):
+            plane, row = divmod(cell, ROWS)
+            bits = signs_ref[pl.ds(group * rows + source_of(cell), 8, stride=CELLS), :]
+            probes = (2 * bits - 1).astype(F32)
+
+            def put(ref, index):
+                ref[pl.ds(index * PROBES + group * 8, 8), :] = probes
+
+            put(own_ref, cell)
+            if plane == 1:
+                put(far_ref, row)
+            for ref, step in ((low_ref, row), (high_ref, ROWS - 1 - row)):
+                if step < 3:
+                    put(ref, plane * 3 + step)
 
 
 def prepare(mirror, signs, diagonal):
+    hbm = pl.BlockSpec(memory_space=pltpu.HBM)
     return pl.pallas_call(
         prepare_kernel,
         out_shape=(
@@ -81,12 +107,17 @@
             shaped(EDGE_ROWS, LANES),
             shaped(EDGE_ROWS, LANES),
         ),
-        in_specs=[pl.BlockSpec(memory_space=pltpu.SMEM)] + vmem_specs(2),
+        in_specs=[pl.BlockSpec(memory_space=pltpu.SMEM), hbm, hbm],
         out_specs=tuple(vmem_specs(4)),
+        scratch_shapes=[
+            pltpu.VMEM((PROBES * CELLS, LANES), jnp.int32),
+            pltpu.VMEM((CELLS, LANES), F32),
+            pltpu.SemaphoreType.DMA((PROBES // 8 + 1,)),
+        ],
         compiler_params=pltpu.CompilerParams(vmem_limit_bytes=VMEM_LIMIT),
         interpret=INTERPRET,
         name="prepare",
-    )(mirror, signs, diagonal)
+    )(mirror, *(pltpu.with_memory_space_constraint(x, pltpu.HBM) for x in (signs, diagonal)))
 
 
 def pack_kernel(high_ref, low_ref, near_ref, corner_ref, cross_ref):
@@ -132,7 +163,7 @@
 
 def basis_kernel(
     own_ref, high_ref, low_ref, near_ref, beside_ref, far_ref, corner_ref, cross_ref,
-    high_out, low_out, gram_ref, first_ref, second_ref,
+    split_out, gram_ref, first_ref, second_ref,
 ):
     def distance(plane):
         return -plane if plane < 0 else max(plane - (PLANES - 1), 0)
@@ -201,11 +232,11 @@
     def keep(order, plane, row, value):
         columns = pl.ds((plane * ROWS + row) * LANES, LANES)
         upper = value.astype(BF16)
-        high_out[row_of(order), columns] = upper
+        split_out[row_of(order), columns] = upper
         if order == 0:
-            low_out[row_of(order), columns] = jnp.zeros_like(upper)
+            split_out[row_of(4), columns] = jnp.zeros_like(upper)
         else:
-            low_out[row_of(order), columns] = (value - upper.astype(F32)).astype(BF16)
+            split_out[row_of(order + 4), columns] = (value - upper.astype(F32)).astype(BF16)
 
     for plane, row in cells(0):
         keep(0, plane, row, k0(plane, row))
@@ -221,25 +252,21 @@
             keep(2, plane, row, value)
     for plane, row in cells(0):
         keep(3, plane, row, apply(k2, plane, row) - B1 * k1(plane, row))
-    upper = high_out[...]
-    lower = low_out[...]
-    top = nt_dot(upper[:PROBES], upper) + nt_dot(upper[:PROBES], lower)
-    bottom = nt_dot(upper[3 * PROBES :], upper) + nt_dot(upper[3 * PROBES :], lower)
-    gram_ref[:PROBES, :] = top
-    gram_ref[PROBES:, :] = bottom + nt_dot(lower[3 * PROBES :], upper)
+    split = split_out[...]
+    left = jnp.concatenate([split[:PROBES], split[3 * PROBES : 4 * PROBES], split[7 * PROBES :]], 0)
+    product = nt_dot(left, split)
+    product = product[:, :LANES] + product[:, LANES:]
+    gram_ref[:PROBES, :] = product[:PROBES]
+    gram_ref[PROBES:, :] = product[PROBES : 2 * PROBES] + product[2 * PROBES :]
 
 
 def basis(*operands):
     width = CELLS * LANES
     return pl.pallas_call(
         basis_kernel,
-        out_shape=(
-            shaped(4 * PROBES, width, dtype=BF16),
-            shaped(4 * PROBES, width, dtype=BF16),
-            shaped(2 * PROBES, LANES),
-        ),
+        out_shape=(shaped(8 * PROBES, width, dtype=BF16), shaped(2 * PROBES, LANES)),
         in_specs=vmem_specs(len(operands)),
-        out_specs=tuple(vmem_specs(3)),
+        out_specs=tuple(vmem_specs(2)),
         scratch_shapes=[pltpu.VMEM((108 * PROBES, LANES), F32), pltpu.VMEM((68 * PROBES, LANES), F32)],
         compiler_params=pltpu.CompilerParams(vmem_limit_bytes=VMEM_LIMIT),
         interpret=INTERPRET,
@@ -299,7 +326,21 @@
     return jnp.concatenate(solved, 0), jnp.concatenate(upper, 0)
 
 
-def finish_kernel(mirror_ref, gram_ref, high_ref, low_ref, alpha_ref, beta_ref, next_ref):
+def parts_of(value):
+    upper = value.astype(BF16)
+    rest = value - upper.astype(F32)
+    middle = rest.astype(BF16)
+    return upper, middle, (rest - middle.astype(F32)).astype(BF16)
+
+
+def square(value):
+    upper, middle, lower = parts_of(value)
+    left = jnp.concatenate([upper, upper, middle, middle, upper, lower], 0)
+    right = jnp.concatenate([upper, middle, upper, middle, lower, upper], 0)
+    return lax.dot_general(left, right, (((0,), (0,)), ((), ())), preferred_element_type=F32)
+
+
+def finish_kernel(mirror_ref, gram_ref, split_ref, alpha_ref, beta_ref, next_ref):
     exact = lax.Precision.HIGHEST
     lane = lax.broadcasted_iota(jnp.int32, (PROBES, LANES), 1)
     block_of = lane // PROBES
@@ -321,22 +362,17 @@
         solved.append(value)
         uppers.append(upper)
         if block < 3:
-            tail = value[:, (block + 1) * PROBES :]
-            update = lax.dot_general(
-                tail, value, (((0,), (0,)), ((), ())), precision=exact, preferred_element_type=F32
-            )
+            update = square(value)
             for later in range(block + 1, 4):
-                offset = (later - block - 1) * PROBES
-                change = update[offset : offset + PROBES, :]
+                change = update[later * PROBES : (later + 1) * PROBES, :]
                 change = jnp.where((block_of <= block) | (block_of >= later), change, 0.0)
                 systems[later] = systems[later] - change
-    weights = solved[3]
-    upper = weights.astype(BF16)
-    lower = (weights - upper.astype(F32)).astype(BF16)
-    high = high_ref[...]
-    result = jnp.dot(upper, high, preferred_element_type=F32)
-    result = result + jnp.dot(upper, low_ref[...], preferred_element_type=F32)
-    result = result + jnp.dot(lower, high, preferred_element_type=F32)
+    upper, lower, _ = parts_of(solved[3])
+    weights = jnp.concatenate(
+        [jnp.concatenate([upper, upper], 1), jnp.concatenate([lower, jnp.zeros_like(lower)], 1)], 0
+    )
+    result = jnp.dot(weights, split_ref[...], preferred_element_type=F32)
+    result = result[:PROBES] + result[PROBES:]
     flip_plane = mirror_ref[0]
     flip_row = mirror_ref[1] * (ROWS - 1)
     for cell in range(CELLS):
@@ -358,7 +394,7 @@
         beta_ref[block] = jnp.where(row32 <= lane32, beta, 0.0)
 
 
-def finish(mirror, gram, high, low):
+def finish(mirror, gram, split):
     return pl.pallas_call(
         finish_kernel,
         out_shape=(
@@ -366,12 +402,12 @@
             jax.ShapeDtypeStruct((3, PROBES, PROBES), F32),
             jax.ShapeDtypeStruct((PROBES * CELLS, LANES), F32),
         ),
-        in_specs=[pl.BlockSpec(memory_space=pltpu.SMEM)] + vmem_specs(3),
+        in_specs=[pl.BlockSpec(memory_space=pltpu.SMEM)] + vmem_specs(2),
         out_specs=tuple(vmem_specs(3)),
         compiler_params=pltpu.CompilerParams(vmem_limit_bytes=VMEM_LIMIT),
         interpret=INTERPRET,
         name="finish",
-    )(mirror, *held(gram, high, low))
+    )(mirror, *held(gram, split))
 
 
 def off_chip(x):
@@ -423,8 +459,8 @@
     corner_message, cross_message = pack(high, low, near)
     corner = off_chip(corner_message)
     cross = on_chip(cross_message)
-    upper, lower, gram = basis(own, high, low, near, beside, far, corner, cross)
-    alphas, betas, following = finish(mirror, reduced(gram), upper, lower)
+    split, gram = basis(own, high, low, near, beside, far, corner, cross)
+    alphas, betas, following = finish(mirror, reduced(gram), split)
     return (alphas, betas, following.reshape(PROBES, PLANES, ROWS, LANES))
 
 

time: 94.5 us -> 91.9 us (0.972)
  local copies, waits for them, and re-layouts: 1.7 us -> 0.03 us
    unnamed x4 -> x0, local copies, waits for them, and re-layouts: 1.67 us -> none
    pallas_call x1, Pallas kernels: 6.68 us -> 5.67 us  [finish(): pl.pallas_call(finish_kernel, out_shape=(jax.ShapeDtypeStruct((3, PROBES,...]
    pallas_call x1, Pallas kernels: 1.11 us -> 2.07 us  [prepare(): pl.pallas_call(prepare_kernel, out_shape=(shaped(OWN_ROWS, LANES), shaped...]
where the time goes in v4:
time: 91.9 us; the launch traced here: 91.4 us
  blocking collectives  40.8 us (44%)
  starting transfers between devices  32.1 us (35%)
  Pallas kernels  10.3 us (11%)
  waiting for transfers between devices  7.29 us (8%)
    all_to_all x3, blocking collectives, exchanged(): return lax.all_to_all(x, axes, 0, 0, tiled=True)  40.8 us
    ppermute x2, starting transfers between devices, row_pair(): return lax.ppermute(x, GY, [(i, step(i) % count) for i in range(count)])  13.7 us
    ppermute x2, starting transfers between devices, on_chip(): return lax.ppermute(x, CORE, [(i, count - 1 - i) for i in range(count)])  8.86 us
    ppermute x2, starting transfers between devices, off_chip(): lax.ppermute(x, GX, [(i, (i - 1 if i % 2 == 0 else i + 1) % count) for i...  6.5 us
    pallas_call x1, Pallas kernels, finish(): pl.pallas_call(finish_kernel, out_shape=(jax.ShapeDtypeStruct((3, PROBES,...  5.67 us
    ppermute x1, starting transfers between devices, same_core(): lax.ppermute(x, GX, [(i, (i + 2 if i % 2 == 0 else i - 2) % count) for i...  2.98 us
    ppermute x2, waiting for transfers between devices, row_pair(): return lax.ppermute(x, GY, [(i, step(i) % count) for i in range(count)])  2.94 us
    pallas_call x1, Pallas kernels, basis(): pl.pallas_call(basis_kernel, out_shape=(shaped(8 * PROBES, width, dtype=B...  2.54 us
  transfers between devices with their start and end apart: 7, of which 3 were waited for; matrix products, arithmetic and copies ran while one was open for 0% of the time, Pallas kernels for 0%

profile of v4, /device:TPU:1, one launch (start us, length us, event | category | flops | bytes accessed | tf_op | source)
XLA Modules:
  0.0 91.4 jit_solution(15893963674382859953)
XLA Ops:
  0.6 0.1 pad_add_fusion.mirror_ref
  0.7 2.1 %prepare.1 = (f32[1056,128]{1,0:T(8,128)S(1)}, f32[512,128]{1,0:T(8,128)S(1)}, f32[200,128]{1,0:T(8,128)S(1)}, f32[200,128]{1,0:T(8,128)S(1)}) custom-call(s32[2]{0:T(128)S(1)} %pad_add_fusion.mirror_ref, s32[1024,128]{1,0:T(8,128)} %bitcast.9, f32[32,128]{1,0:T(8,128)} %bitcast.10), custom_call_target="tpu_custom_call" | custom-call | tf_op jit(solution)/shard_map/prepare/pallas_call | solution.py:102
  2.8 4.6 %collective-permute-start.2 = (f32[1056,128]{1,0:T(8,128)S(1)}, f32[1056,128]{1,0:T(8,128)S(1)}, u32[]{:S(2)}, u32[]{:S(2)}) collective-permute-start(f32[1056,128]{1,0:T(8,128)S(1)} %get-tuple-element.14.own_ref), channel_id=1, source_target_pairs={{0,496},{16,32},{32,16},{48,64},{64,48},{80,96},{96,80},{112,128},... | collective-permute-start | bytes 1622024 | tf_op jit(solution)/shard_map/ppermute | solution.py:415
  7.4 6.1 %collective-permute-start.3 = (f32[1056,128]{1,0:T(8,128)S(1)}, f32[1056,128]{1,0:T(8,128)S(1)}, u32[]{:S(2)}, u32[]{:S(2)}) collective-permute-start(f32[1056,128]{1,0:T(8,128)S(1)} %get-tuple-element.14.own_ref), channel_id=1, source_target_pairs={{0,16},{16,0},{1,17},{17,1},{2,18},{18,2},{3,19},{19,3},{4,20},{20... | collective-permute-start | bytes 1622024 | tf_op jit(solution)/shard_map/ppermute | solution.py:425
  13.5 2.8 %collective-permute-start = (f32[200,128]{1,0:T(8,128)S(1)}, f32[200,128]{1,0:T(8,128)S(1)}, u32[]{:S(2)}, u32[]{:S(2)}) collective-permute-start(f32[200,128]{1,0:T(8,128)S(1)} %get-tuple-element.15), channel_id=1, source_target_pairs={{0,1},{1,0},{2,3},{3,2},{4,5},{5,4},{6,7},{7,6},{8,9},{9,8},{10,11... | collective-permute-start | bytes 307208 | tf_op jit(solution)/shard_map/ppermute | solution.py:431
  16.3 10.9 %collective-permute-start.1 = (f32[200,128]{1,0:T(8,128)S(1)}, f32[200,128]{1,0:T(8,128)S(1)}, u32[]{:S(2)}, u32[]{:S(2)}) collective-permute-start(f32[200,128]{1,0:T(8,128)S(1)} %get-tuple-element.16), channel_id=1, source_target_pairs={{0,15},{1,2},{2,1},{3,4},{4,3},{5,6},{6,5},{7,8},{8,7},{9,10},{10,... | collective-permute-start | bytes 307208 | tf_op jit(solution)/shard_map/ppermute | solution.py:431
  27.2 0.0 collective-permute-done.high_ref
  27.2 2.9 %collective-permute-done.1.low_ref = f32[200,128]{1,0:T(8,128)S(1)} collective-permute-done((f32[200,128]{1,0:T(8,128)S(1)}, f32[200,128]{1,0:T(8,128)S(1)}, u32[]{:S(2)}, u32[]{:S(2)}) %collective-permute-start.1) | collective-permute-done | bytes 102432 | tf_op jit(solution)/shard_map/ppermute | solution.py:431
  30.2 0.0 collective-permute-done.2.near_ref
  30.2 2.8 %collective-permute-start.6 = (f32[712,128]{1,0:T(8,128)S(1)}, f32[712,128]{1,0:T(8,128)S(1)}, u32[]{:S(2)}, u32[]{:S(2)}) collective-permute-start(f32[712,128]{1,0:T(8,128)S(1)} %get-tuple-element.19), channel_id=1, source_target_pairs={{0,16},{16,0},{1,17},{17,1},{2,18},{18,2},{3,19},{19,3},{4,20},{20... | collective-permute-start | bytes 1093640 | tf_op jit(solution)/shard_map/ppermute | solution.py:425
  33.0 3.0 %collective-permute-start.4 = (f32[512,128]{1,0:T(8,128)S(1)}, f32[512,128]{1,0:T(8,128)S(1)}, u32[]{:S(2)}, u32[]{:S(2)}) collective-permute-start(f32[512,128]{1,0:T(8,128)S(1)} %get-tuple-element.17), channel_id=1, source_target_pairs={{0,32},{16,496},{32,64},{48,16},{64,96},{80,48},{96,128},{112,80},... | collective-permute-start | bytes 786440 | tf_op jit(solution)/shard_map/ppermute | solution.py:420
  36.0 1.9 %collective-permute-start.5 = (f32[200,128]{1,0:T(8,128)S(1)}, f32[200,128]{1,0:T(8,128)S(1)}, u32[]{:S(2)}, u32[]{:S(2)}) collective-permute-start(f32[200,128]{1,0:T(8,128)S(1)} %get-tuple-element.18), channel_id=1, source_target_pairs={{0,496},{16,32},{32,16},{48,64},{64,48},{80,96},{96,80},{112,128},... | collective-permute-start | bytes 307208 | tf_op jit(solution)/shard_map/ppermute | solution.py:415
  37.9 2.5 %collective-permute-done.4.far_ref = f32[512,128]{1,0:T(8,128)S(1)} collective-permute-done((f32[512,128]{1,0:T(8,128)S(1)}, f32[512,128]{1,0:T(8,128)S(1)}, u32[]{:S(2)}, u32[]{:S(2)}) %collective-permute-start.4) | collective-permute-done | bytes 262176 | tf_op jit(solution)/shard_map/ppermute | solution.py:420
  40.4 0.0 collective-permute-done.3.beside_ref
  40.4 1.8 %collective-permute-done.5.corner_ref = f32[200,128]{1,0:T(8,128)S(1)} collective-permute-done((f32[200,128]{1,0:T(8,128)S(1)}, f32[200,128]{1,0:T(8,128)S(1)}, u32[]{:S(2)}, u32[]{:S(2)}) %collective-permute-start.5) | collective-permute-done | bytes 102432 | tf_op jit(solution)/shard_map/ppermute | solution.py:415
  42.3 0.0 collective-permute-done.6.cross_ref
  42.3 2.5 %basis.1 = (bf16[256,4096]{1,0:T(8,128)(2,1)S(1)}, f32[64,128]{1,0:T(8,128)S(1)}) custom-call(f32[1056,128]{1,0:T(8,128)S(1)} %get-tuple-element.14.own_ref, f32[200,128]{1,0:T(8,128)S(1)} %collective-permute-done.high_ref, f32[200,128]{1,0:T(8,128)S(1)} %collective-permute-done.1.low_ref, f32[1056,128]{1,0:T(8,128)S(1)} %collective-permute-done.2.near_ref, ...), custom_call_target="tpu_custom_call" | custom-call | tf_op jit(solution)/shard_map/basis/pallas_call | solution.py:265
  44.8 9.5 %all_to_all.15 = f32[8,8,128]{2,1,0:T(8,128)S(1)} all-to-all(f32[8,8,128]{2,1,0:T(8,128)S(1)} %bitcast.8), channel_id=1, replica_groups=mesh['gx_0'=2,'gx_1'=8,'gx_2'=2,'gy_0'=8,'gy_1'=2] {'gx_0','gx_2','gy_1'}, dimensions={0} | all-to-all | bytes 65536 | tf_op jit(solution)/shard_map/all_to_all | solution.py:435
  54.4 21.2 %all_to_all.16 = f32[64,8,128]{2,1,0:T(8,128)S(1)} all-to-all(f32[64,8,128]{2,1,0:T(8,128)S(1)} %broadcast_in_dim.4), channel_id=1, replica_groups=mesh['gx_0'=2,'gx_1'=8,'gx_2'=2,'gy_0'=8,'gy_1'=2] {'gx_1','gy_0'}, dimensions={0} | all-to-all | bytes 524288 | tf_op jit(solution)/shard_map/all_to_all | solution.py:435
  75.6 0.1 reduce_sum.19
  75.7 10.1 %all_to_all.17 = f32[8,8,128]{2,1,0:T(8,128)S(1)} all-to-all(f32[8,8,128]{2,1,0:T(8,128)S(1)} %broadcast_in_dim.5), channel_id=1, replica_groups=mesh['gx_0'=2,'gx_1'=8,'gx_2'=2,'gy_0'=8,'gy_1'=2] {'gx_0','gx_2','gy_1'}, dimensions={0} | all-to-all | bytes 65536 | tf_op jit(solution)/shard_map/all_to_all | solution.py:435
  85.8 5.7 %finish.1 = (f32[3,32,32]{2,1,0:T(8,128)}, f32[3,32,32]{2,1,0:T(8,128)}, f32[1024,128]{1,0:T(8,128)}) custom-call(s32[2]{0:T(128)S(1)} %pad_add_fusion.mirror_ref, f32[64,128]{1,0:T(8,128)S(1)} %bitcast.7, bf16[256,4096]{1,0:T(8,128)(2,1)S(1)} %get-tuple-element.21.split_ref), custom_call_target="tpu_custom_call" | custom-call | tf_op jit(solution)/shard_map/finish/pallas_call | solution.py:398
  (4 shorter events, 0.1 us)
Async XLA Ops:
  2.8 27.4 %collective-permute-start.2 = (f32[1056,128]{1,0:T(8,128)S(1)}, f32[1056,128]{1,0:T(8,128)S(1)}, u32[]{:S(2)}, u32[]{:S(2)}) collective-permute-start(f32[1056,128]{1,0:T(8,128)S(1)} %get-tuple-element.14.own_ref), channel_id=1, source_target_pairs={{0,496},{16,32},{32,16},{48,64},{64,48},{80,96},{96,80},{112,128},... | collective-permute-start | bytes 1622024 | tf_op jit(solution)/shard_map/ppermute | solution.py:415
  7.4 33.0 %collective-permute-start.3 = (f32[1056,128]{1,0:T(8,128)S(1)}, f32[1056,128]{1,0:T(8,128)S(1)}, u32[]{:S(2)}, u32[]{:S(2)}) collective-permute-start(f32[1056,128]{1,0:T(8,128)S(1)} %get-tuple-element.14.own_ref), channel_id=1, source_target_pairs={{0,16},{16,0},{1,17},{17,1},{2,18},{18,2},{3,19},{19,3},{4,20},{20... | collective-permute-start | bytes 1622024 | tf_op jit(solution)/shard_map/ppermute | solution.py:425
  13.5 13.8 %collective-permute-start = (f32[200,128]{1,0:T(8,128)S(1)}, f32[200,128]{1,0:T(8,128)S(1)}, u32[]{:S(2)}, u32[]{:S(2)}) collective-permute-start(f32[200,128]{1,0:T(8,128)S(1)} %get-tuple-element.15), channel_id=1, source_target_pairs={{0,1},{1,0},{2,3},{3,2},{4,5},{5,4},{6,7},{7,6},{8,9},{9,8},{10,11... | collective-permute-start | bytes 307208 | tf_op jit(solution)/shard_map/ppermute | solution.py:431
  16.3 13.9 %collective-permute-start.1 = (f32[200,128]{1,0:T(8,128)S(1)}, f32[200,128]{1,0:T(8,128)S(1)}, u32[]{:S(2)}, u32[]{:S(2)}) collective-permute-start(f32[200,128]{1,0:T(8,128)S(1)} %get-tuple-element.16), channel_id=1, source_target_pairs={{0,15},{1,2},{2,1},{3,4},{4,3},{5,6},{6,5},{7,8},{8,7},{9,10},{10,... | collective-permute-start | bytes 307208 | tf_op jit(solution)/shard_map/ppermute | solution.py:431
  30.2 12.1 %collective-permute-start.6 = (f32[712,128]{1,0:T(8,128)S(1)}, f32[712,128]{1,0:T(8,128)S(1)}, u32[]{:S(2)}, u32[]{:S(2)}) collective-permute-start(f32[712,128]{1,0:T(8,128)S(1)} %get-tuple-element.19), channel_id=1, source_target_pairs={{0,16},{16,0},{1,17},{17,1},{2,18},{18,2},{3,19},{19,3},{4,20},{20... | collective-permute-start | bytes 1093640 | tf_op jit(solution)/shard_map/ppermute | solution.py:425
  33.0 7.4 %collective-permute-start.4 = (f32[512,128]{1,0:T(8,128)S(1)}, f32[512,128]{1,0:T(8,128)S(1)}, u32[]{:S(2)}, u32[]{:S(2)}) collective-permute-start(f32[512,128]{1,0:T(8,128)S(1)} %get-tuple-element.17), channel_id=1, source_target_pairs={{0,32},{16,496},{32,64},{48,16},{64,96},{80,48},{96,128},{112,80},... | collective-permute-start | bytes 786440 | tf_op jit(solution)/shard_map/ppermute | solution.py:420
  36.0 6.3 %collective-permute-start.5 = (f32[200,128]{1,0:T(8,128)S(1)}, f32[200,128]{1,0:T(8,128)S(1)}, u32[]{:S(2)}, u32[]{:S(2)}) collective-permute-start(f32[200,128]{1,0:T(8,128)S(1)} %get-tuple-element.18), channel_id=1, source_target_pairs={{0,496},{16,32},{32,16},{48,64},{64,48},{80,96},{96,80},{112,128},... | collective-permute-start | bytes 307208 | tf_op jit(solution)/shard_map/ppermute | solution.py:415

commit v5 on v4

--- a/solution.py
+++ b/solution.py
@@ -12,6 +12,7 @@
 NEAR = ("gx_0", "gx_2", "gy_1")
 FAR = ("gx_1", "gy_0")
 CORE = "gx_2"
+PAIR = "gy_1"
 
 PROBES = 32
 LANES = 128
@@ -21,7 +22,7 @@
 SHIFT = 7.75
 B0 = 7.0
 B1 = 10.0
-PANEL = 16
+PANEL = 8
 F32 = jnp.float32
 BF16 = jnp.bfloat16
 INTERPRET = False
@@ -49,8 +50,18 @@
     return pl.ds(index * PROBES, PROBES)
 
 
+def mirrored():
+    core = lax.axis_index(CORE)
+    pair = lax.axis_index(PAIR)
+
+    def position(plane, row):
+        return (plane + core * (1 - 2 * plane)) * ROWS + row + pair * (ROWS - 1 - 2 * row)
+
+    return position
+
+
 def prepare_kernel(
-    mirror_ref, signs_hbm, diag_hbm, own_ref, far_ref, high_ref, low_ref, signs_ref, diag_ref, arrived
+    signs_hbm, diag_hbm, own_ref, far_ref, high_ref, low_ref, signs_ref, diag_ref, arrived
 ):
     rows = 8 * CELLS
     copies = []
@@ -61,17 +72,12 @@
     lines.start()
     for copy in copies:
         copy.start()
-    flip_plane = mirror_ref[0]
-    flip_row = mirror_ref[1] * (ROWS - 1)
-
-    def source_of(cell):
-        plane, row = divmod(cell, ROWS)
-        return (flip_plane ^ plane) * ROWS + (flip_row ^ row)
+    position = mirrored()
 
     lines.wait()
     for cell in range(CELLS):
         plane, row = divmod(cell, ROWS)
-        line = diag_ref[pl.ds(source_of(cell), 1), :]
+        line = diag_ref[pl.ds(position(plane, row), 1), :]
         own_ref[CELLS * PROBES + cell : CELLS * PROBES + cell + 1, :] = line
         for ref, step in ((low_ref, row), (high_ref, ROWS - 1 - row)):
             if step < 2:
@@ -83,7 +89,7 @@
         copies[group].wait()
         for cell in range(CELLS):
             plane, row = divmod(cell, ROWS)
-            bits = signs_ref[pl.ds(group * rows + source_of(cell), 8, stride=CELLS), :]
+            bits = signs_ref[pl.ds(group * rows + position(plane, row), 8, stride=CELLS), :]
             probes = (2 * bits - 1).astype(F32)
 
             def put(ref, index):
@@ -97,7 +103,7 @@
                     put(ref, plane * 3 + step)
 
 
-def prepare(mirror, signs, diagonal):
+def prepare(signs, diagonal):
     hbm = pl.BlockSpec(memory_space=pltpu.HBM)
     return pl.pallas_call(
         prepare_kernel,
@@ -107,7 +113,7 @@
             shaped(EDGE_ROWS, LANES),
             shaped(EDGE_ROWS, LANES),
         ),
-        in_specs=[pl.BlockSpec(memory_space=pltpu.SMEM), hbm, hbm],
+        in_specs=[hbm, hbm],
         out_specs=tuple(vmem_specs(4)),
         scratch_shapes=[
             pltpu.VMEM((PROBES * CELLS, LANES), jnp.int32),
@@ -117,7 +123,7 @@
         compiler_params=pltpu.CompilerParams(vmem_limit_bytes=VMEM_LIMIT),
         interpret=INTERPRET,
         name="prepare",
-    )(mirror, *(pltpu.with_memory_space_constraint(x, pltpu.HBM) for x in (signs, diagonal)))
+    )(*(pltpu.with_memory_space_constraint(x, pltpu.HBM) for x in (signs, diagonal)))
 
 
 def pack_kernel(high_ref, low_ref, near_ref, corner_ref, cross_ref):
@@ -155,10 +161,8 @@
     )(*held(high, low, near))
 
 
-def nt_dot(left, right, precision=None):
-    return lax.dot_general(
-        left, right, (((1,), (1,)), ((), ())), precision=precision, preferred_element_type=F32
-    )
+def nt_dot(left, right):
+    return lax.dot_general(left, right, (((1,), (1,)), ((), ())), preferred_element_type=F32)
 
 
 def basis_kernel(
@@ -285,13 +289,17 @@
         jnp.where(inside, jnp.where(lane - start == sub + 8 * g, 1.0, 0.0), pivoted[g]) for g in range(groups)
     ]
     scales = [None] * PROBES
-    for panel in range(0, PROBES, PANEL):
-        first_group = panel // 8
-        spread = {}
-        for k in range(panel, panel + PANEL):
-            for g in range(first_group, groups):
+    spread = {}
+
+    def spread_panel(panel):
+        for k in range(panel, min(panel + PANEL, PROBES)):
+            for g in range(max(panel - PANEL, 0) // 8, groups):
                 column = pivoted[g][:, start + k : start + k + 1]
                 spread[k, g] = jnp.broadcast_to(column, (8, LANES))
+
+    spread_panel(0)
+    for panel in range(0, PROBES, PANEL):
+        spread_panel(panel + PANEL)
         for k in range(panel, panel + PANEL):
             group, line = divmod(k, 8)
 
@@ -307,12 +315,12 @@
                 if g == group:
                     value = jnp.where(sub > line, value, 0.0)
                 multiplier[g] = value
-            for other in range(k + 1, panel + PANEL):
-                row = pivot_row(spread[other, group])
-                for g in range(group, groups):
-                    spread[other, g] = spread[other, g] - multiplier[g] * row
             row = pivot_row(pivoted[group])
             solved_row = pivot_row(solved[group])
+            for other in range(k + 1, min(panel + 2 * PANEL, PROBES)):
+                weight = pivot_row(spread[other, group])
+                for g in range(group, groups):
+                    spread[other, g] = spread[other, g] - multiplier[g] * weight
             for g in range(group, groups):
                 pivoted[g] = pivoted[g] - multiplier[g] * row
                 solved[g] = solved[g] - multiplier[g] * solved_row
@@ -340,8 +348,15 @@
     return lax.dot_general(left, right, (((0,), (0,)), ((), ())), preferred_element_type=F32)
 
 
-def finish_kernel(mirror_ref, gram_ref, split_ref, alpha_ref, beta_ref, next_ref):
-    exact = lax.Precision.HIGHEST
+def wide_dot(left, right):
+    left_upper, left_lower, _ = parts_of(left)
+    right_upper, right_lower, _ = parts_of(right)
+    both = jnp.concatenate([left_upper, left_lower], 1)
+    result = nt_dot(both, jnp.concatenate([right_upper, right_upper], 1))
+    return result + nt_dot(both, jnp.concatenate([right_lower, right_lower], 1))
+
+
+def finish_kernel(gram_ref, split_ref, alpha_ref, beta_ref, next_hbm, next_ref, left):
     lane = lax.broadcasted_iota(jnp.int32, (PROBES, LANES), 1)
     block_of = lane // PROBES
     first = gram_ref[:PROBES, :]
@@ -355,59 +370,75 @@
     third = moved(last, 1) + jnp.where(block_of == 2, B1 * moved(second, 1) - B0 * first, 0.0)
     third = jnp.where(block_of < 2, 0.0, third)
     systems = [first, second, third, jnp.where(block_of < 3, 0.0, last)]
+    row32 = lax.broadcasted_iota(jnp.int32, (PROBES, PROBES), 0)
+    lane32 = lax.broadcasted_iota(jnp.int32, (PROBES, PROBES), 1)
     solved = []
-    uppers = []
+    beta = None
     for block in range(4):
-        value, upper = eliminate(systems[block], block)
+        value, triangle = eliminate(systems[block], block)
         solved.append(value)
-        uppers.append(upper)
         if block < 3:
             update = square(value)
             for later in range(block + 1, 4):
                 change = update[later * PROBES : (later + 1) * PROBES, :]
                 change = jnp.where((block_of <= block) | (block_of >= later), change, 0.0)
                 systems[later] = systems[later] - change
+        if block > 0:
+            beta = wide_dot(moved(triangle, -1), inverse)
+            beta_ref[block - 1] = jnp.where(row32 <= lane32, beta, 0.0)
+        if block < 3:
+            inverse = jnp.where(block_of == block, value, 0.0)
+            alpha = wide_dot(moved(value, -1), inverse)
+            if block > 0:
+                coupled = wide_dot(solved[block - 1], inverse)
+                alpha = alpha - jnp.dot(
+                    beta, coupled, precision=lax.Precision.HIGHEST, preferred_element_type=F32
+                )
+            alpha_ref[block] = alpha + jnp.where(row32 == lane32, SHIFT, 0.0)
     upper, lower, _ = parts_of(solved[3])
     weights = jnp.concatenate(
         [jnp.concatenate([upper, upper], 1), jnp.concatenate([lower, jnp.zeros_like(lower)], 1)], 0
     )
-    result = jnp.dot(weights, split_ref[...], preferred_element_type=F32)
-    result = result[:PROBES] + result[PROBES:]
-    flip_plane = mirror_ref[0]
-    flip_row = mirror_ref[1] * (ROWS - 1)
-    for cell in range(CELLS):
-        plane, row = divmod(cell, ROWS)
-        target = (flip_plane ^ plane) * ROWS + (flip_row ^ row)
-        next_ref[pl.ds(target, PROBES, stride=CELLS), :] = result[:, cell * LANES : (cell + 1) * LANES]
-    row32 = lax.broadcasted_iota(jnp.int32, (PROBES, PROBES), 0)
-    lane32 = lax.broadcasted_iota(jnp.int32, (PROBES, PROBES), 1)
-    beta = None
-    for block in range(3):
-        inverse = jnp.where(block_of == block, solved[block], 0.0)
-        alpha = nt_dot(moved(solved[block], -1), inverse, exact)
-        if block > 0:
-            alpha = alpha - jnp.dot(
-                beta, nt_dot(solved[block - 1], inverse, exact), precision=exact, preferred_element_type=F32
-            )
-        alpha_ref[block] = alpha + jnp.where(row32 == lane32, SHIFT, 0.0)
-        beta = nt_dot(moved(uppers[block + 1], -1), inverse, exact)
-        beta_ref[block] = jnp.where(row32 <= lane32, beta, 0.0)
-
-
-def finish(mirror, gram, split):
+    position = mirrored()
+    view = next_ref.reshape(PROBES, CELLS, LANES)
+    copies = []
+    for group in range(CELLS // 8):
+        columns = pl.ds(group * 8 * LANES, 8 * LANES)
+        result = jnp.dot(weights, split_ref[:, columns], preferred_element_type=F32)
+        result = result[:PROBES] + result[PROBES:]
+        for place in range(8):
+            plane, row = divmod(group * 8 + place, ROWS)
+            target = pl.ds(position(plane, row), PROBES, stride=CELLS)
+            next_ref[target, :] = result[:, place * LANES : (place + 1) * LANES]
+        plane, half = divmod(group, 2)
+        core, pair = lax.axis_index(CORE), lax.axis_index(PAIR)
+        first = (plane + core * (1 - 2 * plane)) * ROWS + (half + pair * (1 - 2 * half)) * 8
+        part = pl.ds(pl.multiple_of(first, 8), 8)
+        copy = pltpu.make_async_copy(view.at[:, part, :], next_hbm.at[:, part, :], left.at[group])
+        copy.start()
+        copies.append(copy)
+    for copy in copies:
+        copy.wait()
+
+
+def finish(gram, split):
     return pl.pallas_call(
         finish_kernel,
         out_shape=(
             jax.ShapeDtypeStruct((3, PROBES, PROBES), F32),
             jax.ShapeDtypeStruct((3, PROBES, PROBES), F32),
-            jax.ShapeDtypeStruct((PROBES * CELLS, LANES), F32),
+            jax.ShapeDtypeStruct((PROBES, CELLS, LANES), F32),
         ),
-        in_specs=[pl.BlockSpec(memory_space=pltpu.SMEM)] + vmem_specs(2),
-        out_specs=tuple(vmem_specs(3)),
+        in_specs=vmem_specs(2),
+        out_specs=tuple(vmem_specs(2)) + (pl.BlockSpec(memory_space=pltpu.HBM),),
+        scratch_shapes=[
+            pltpu.VMEM((PROBES * CELLS, LANES), F32),
+            pltpu.SemaphoreType.DMA((CELLS // 8,)),
+        ],
         compiler_params=pltpu.CompilerParams(vmem_limit_bytes=VMEM_LIMIT),
         interpret=INTERPRET,
         name="finish",
-    )(mirror, *held(gram, split))
+    )(*held(gram, split))
 
 
 def off_chip(x):
@@ -449,8 +480,7 @@
 def per_device(probe_signs, diagonal):
     signs = probe_signs.reshape(PROBES * CELLS, LANES)
     diag = diagonal.reshape(CELLS, LANES)
-    mirror = jnp.stack([lax.axis_index(CORE), lax.axis_index("gy_1")]).astype(jnp.int32)
-    own, outer, top, bottom = prepare(mirror, signs, diag)
+    own, outer, top, bottom = prepare(signs, diag)
     near = off_chip(own)
     high = row_pair(top, 0)
     low = row_pair(bottom, 1)
@@ -460,7 +490,7 @@
     corner = off_chip(corner_message)
     cross = on_chip(cross_message)
     split, gram = basis(own, high, low, near, beside, far, corner, cross)
-    alphas, betas, following = finish(mirror, reduced(gram), split)
+    alphas, betas, following = finish(reduced(gram), split)
     return (alphas, betas, following.reshape(PROBES, PLANES, ROWS, LANES))
 
 

time: 91.9 us -> 90.6 us (0.986)
  Pallas kernels: 10.3 us -> 9.13 us
where the time goes in v5:
time: 90.6 us; the launch traced here: 90.2 us
  blocking collectives  40.8 us (45%)
  starting transfers between devices  32.1 us (35%)
  Pallas kernels  9.13 us (10%)
  waiting for transfers between devices  7.29 us (8%)
    all_to_all x3, blocking collectives, exchanged(): return lax.all_to_all(x, axes, 0, 0, tiled=True)  40.8 us
    ppermute x2, starting transfers between devices, row_pair(): return lax.ppermute(x, GY, [(i, step(i) % count) for i in range(count)])  13.7 us
    ppermute x2, starting transfers between devices, on_chip(): return lax.ppermute(x, CORE, [(i, count - 1 - i) for i in range(count)])  8.86 us
    ppermute x2, starting transfers between devices, off_chip(): lax.ppermute(x, GX, [(i, (i - 1 if i % 2 == 0 else i + 1) % count) for i...  6.5 us
    pallas_call x1, Pallas kernels, finish(): pl.pallas_call(finish_kernel, out_shape=(jax.ShapeDtypeStruct((3, PROBES,...  5.21 us
    ppermute x1, starting transfers between devices, same_core(): lax.ppermute(x, GX, [(i, (i + 2 if i % 2 == 0 else i - 2) % count) for i...  2.98 us
    ppermute x2, waiting for transfers between devices, row_pair(): return lax.ppermute(x, GY, [(i, step(i) % count) for i in range(count)])  2.94 us
    pallas_call x1, Pallas kernels, basis(): pl.pallas_call(basis_kernel, out_shape=(shaped(8 * PROBES, width, dtype=B...  2.54 us
  transfers between devices with their start and end apart: 7, of which 3 were waited for; matrix products, arithmetic and copies ran while one was open for 0% of the time, Pallas kernels for 0%

profile of v5, /device:TPU:1, one launch (start us, length us, event | category | flops | bytes accessed | tf_op | source)
XLA Modules:
  0.0 90.2 jit_solution(2473014925165076779)
XLA Ops:
  0.6 1.4 %prepare.1 = (f32[1056,128]{1,0:T(8,128)S(1)}, f32[512,128]{1,0:T(8,128)S(1)}, f32[200,128]{1,0:T(8,128)S(1)}, f32[200,128]{1,0:T(8,128)S(1)}) custom-call(s32[1024,128]{1,0:T(8,128)} %bitcast.7, f32[32,128]{1,0:T(8,128)} %bitcast.8), custom_call_target="tpu_custom_call" | custom-call | tf_op jit(solution)/shard_map/prepare/pallas_call | solution.py:108
  2.0 4.6 %collective-permute-start.2 = (f32[1056,128]{1,0:T(8,128)S(1)}, f32[1056,128]{1,0:T(8,128)S(1)}, u32[]{:S(2)}, u32[]{:S(2)}) collective-permute-start(f32[1056,128]{1,0:T(8,128)S(1)} %get-tuple-element.14.own_ref), channel_id=1, source_target_pairs={{0,496},{16,32},{32,16},{48,64},{64,48},{80,96},{96,80},{112,128},... | collective-permute-start | bytes 1622024 | tf_op jit(solution)/shard_map/ppermute | solution.py:446
  6.6 6.1 %collective-permute-start.3 = (f32[1056,128]{1,0:T(8,128)S(1)}, f32[1056,128]{1,0:T(8,128)S(1)}, u32[]{:S(2)}, u32[]{:S(2)}) collective-permute-start(f32[1056,128]{1,0:T(8,128)S(1)} %get-tuple-element.14.own_ref), channel_id=1, source_target_pairs={{0,16},{16,0},{1,17},{17,1},{2,18},{18,2},{3,19},{19,3},{4,20},{20... | collective-permute-start | bytes 1622024 | tf_op jit(solution)/shard_map/ppermute | solution.py:456
  12.7 2.8 %collective-permute-start = (f32[200,128]{1,0:T(8,128)S(1)}, f32[200,128]{1,0:T(8,128)S(1)}, u32[]{:S(2)}, u32[]{:S(2)}) collective-permute-start(f32[200,128]{1,0:T(8,128)S(1)} %get-tuple-element.15), channel_id=1, source_target_pairs={{0,1},{1,0},{2,3},{3,2},{4,5},{5,4},{6,7},{7,6},{8,9},{9,8},{10,11... | collective-permute-start | bytes 307208 | tf_op jit(solution)/shard_map/ppermute | solution.py:462
  15.5 10.9 %collective-permute-start.1 = (f32[200,128]{1,0:T(8,128)S(1)}, f32[200,128]{1,0:T(8,128)S(1)}, u32[]{:S(2)}, u32[]{:S(2)}) collective-permute-start(f32[200,128]{1,0:T(8,128)S(1)} %get-tuple-element.16), channel_id=1, source_target_pairs={{0,15},{1,2},{2,1},{3,4},{4,3},{5,6},{6,5},{7,8},{8,7},{9,10},{10,... | collective-permute-start | bytes 307208 | tf_op jit(solution)/shard_map/ppermute | solution.py:462
  26.4 0.0 collective-permute-done.high_ref
  26.4 2.9 %collective-permute-done.1.low_ref = f32[200,128]{1,0:T(8,128)S(1)} collective-permute-done((f32[200,128]{1,0:T(8,128)S(1)}, f32[200,128]{1,0:T(8,128)S(1)}, u32[]{:S(2)}, u32[]{:S(2)}) %collective-permute-start.1) | collective-permute-done | bytes 102432 | tf_op jit(solution)/shard_map/ppermute | solution.py:462
  29.4 0.0 collective-permute-done.2.near_ref
  29.4 2.8 %collective-permute-start.6 = (f32[712,128]{1,0:T(8,128)S(1)}, f32[712,128]{1,0:T(8,128)S(1)}, u32[]{:S(2)}, u32[]{:S(2)}) collective-permute-start(f32[712,128]{1,0:T(8,128)S(1)} %get-tuple-element.19), channel_id=1, source_target_pairs={{0,16},{16,0},{1,17},{17,1},{2,18},{18,2},{3,19},{19,3},{4,20},{20... | collective-permute-start | bytes 1093640 | tf_op jit(solution)/shard_map/ppermute | solution.py:456
  32.2 3.0 %collective-permute-start.4 = (f32[512,128]{1,0:T(8,128)S(1)}, f32[512,128]{1,0:T(8,128)S(1)}, u32[]{:S(2)}, u32[]{:S(2)}) collective-permute-start(f32[512,128]{1,0:T(8,128)S(1)} %get-tuple-element.17), channel_id=1, source_target_pairs={{0,32},{16,496},{32,64},{48,16},{64,96},{80,48},{96,128},{112,80},... | collective-permute-start | bytes 786440 | tf_op jit(solution)/shard_map/ppermute | solution.py:451
  35.2 1.9 %collective-permute-start.5 = (f32[200,128]{1,0:T(8,128)S(1)}, f32[200,128]{1,0:T(8,128)S(1)}, u32[]{:S(2)}, u32[]{:S(2)}) collective-permute-start(f32[200,128]{1,0:T(8,128)S(1)} %get-tuple-element.18), channel_id=1, source_target_pairs={{0,496},{16,32},{32,16},{48,64},{64,48},{80,96},{96,80},{112,128},... | collective-permute-start | bytes 307208 | tf_op jit(solution)/shard_map/ppermute | solution.py:446
  37.1 2.5 %collective-permute-done.4.far_ref = f32[512,128]{1,0:T(8,128)S(1)} collective-permute-done((f32[512,128]{1,0:T(8,128)S(1)}, f32[512,128]{1,0:T(8,128)S(1)}, u32[]{:S(2)}, u32[]{:S(2)}) %collective-permute-start.4) | collective-permute-done | bytes 262176 | tf_op jit(solution)/shard_map/ppermute | solution.py:451
  39.6 0.0 collective-permute-done.3.beside_ref
  39.6 1.8 %collective-permute-done.5.corner_ref = f32[200,128]{1,0:T(8,128)S(1)} collective-permute-done((f32[200,128]{1,0:T(8,128)S(1)}, f32[200,128]{1,0:T(8,128)S(1)}, u32[]{:S(2)}, u32[]{:S(2)}) %collective-permute-start.5) | collective-permute-done | bytes 102432 | tf_op jit(solution)/shard_map/ppermute | solution.py:446
  41.5 0.0 collective-permute-done.6.cross_ref
  41.5 2.5 %basis.1 = (bf16[256,4096]{1,0:T(8,128)(2,1)S(1)}, f32[64,128]{1,0:T(8,128)S(1)}) custom-call(f32[1056,128]{1,0:T(8,128)S(1)} %get-tuple-element.14.own_ref, f32[200,128]{1,0:T(8,128)S(1)} %collective-permute-done.high_ref, f32[200,128]{1,0:T(8,128)S(1)} %collective-permute-done.1.low_ref, f32[1056,128]{1,0:T(8,128)S(1)} %collective-permute-done.2.near_ref, ...), custom_call_target="tpu_custom_call" | custom-call | tf_op jit(solution)/shard_map/basis/pallas_call | solution.py:269
  44.0 9.5 %all_to_all.15 = f32[8,8,128]{2,1,0:T(8,128)S(1)} all-to-all(f32[8,8,128]{2,1,0:T(8,128)S(1)} %bitcast.6), channel_id=1, replica_groups=mesh['gx_0'=2,'gx_1'=8,'gx_2'=2,'gy_0'=8,'gy_1'=2] {'gx_0','gx_2','gy_1'}, dimensions={0} | all-to-all | bytes 65536 | tf_op jit(solution)/shard_map/all_to_all | solution.py:466
  53.6 21.2 %all_to_all.16 = f32[64,8,128]{2,1,0:T(8,128)S(1)} all-to-all(f32[64,8,128]{2,1,0:T(8,128)S(1)} %broadcast_in_dim.4), channel_id=1, replica_groups=mesh['gx_0'=2,'gx_1'=8,'gx_2'=2,'gy_0'=8,'gy_1'=2] {'gx_1','gy_0'}, dimensions={0} | all-to-all | bytes 524288 | tf_op jit(solution)/shard_map/all_to_all | solution.py:466
  74.8 0.1 reduce_sum.19
  74.9 10.1 %all_to_all.17 = f32[8,8,128]{2,1,0:T(8,128)S(1)} all-to-all(f32[8,8,128]{2,1,0:T(8,128)S(1)} %broadcast_in_dim.5), channel_id=1, replica_groups=mesh['gx_0'=2,'gx_1'=8,'gx_2'=2,'gy_0'=8,'gy_1'=2] {'gx_0','gx_2','gy_1'}, dimensions={0} | all-to-all | bytes 65536 | tf_op jit(solution)/shard_map/all_to_all | solution.py:466
  85.0 5.2 %finish.1 = (f32[3,32,32]{2,1,0:T(8,128)}, f32[3,32,32]{2,1,0:T(8,128)}, f32[32,32,128]{2,1,0:T(8,128)}) custom-call(f32[64,128]{1,0:T(8,128)S(1)} %bitcast.5, bf16[256,4096]{1,0:T(8,128)(2,1)S(1)} %get-tuple-element.21.split_ref), custom_call_target="tpu_custom_call" | custom-call | tf_op jit(solution)/shard_map/finish/pallas_call | solution.py:425
  (4 shorter events, 0.1 us)
Async XLA Ops:
  2.0 27.4 %collective-permute-start.2 = (f32[1056,128]{1,0:T(8,128)S(1)}, f32[1056,128]{1,0:T(8,128)S(1)}, u32[]{:S(2)}, u32[]{:S(2)}) collective-permute-start(f32[1056,128]{1,0:T(8,128)S(1)} %get-tuple-element.14.own_ref), channel_id=1, source_target_pairs={{0,496},{16,32},{32,16},{48,64},{64,48},{80,96},{96,80},{112,128},... | collective-permute-start | bytes 1622024 | tf_op jit(solution)/shard_map/ppermute | solution.py:446
  6.6 33.0 %collective-permute-start.3 = (f32[1056,128]{1,0:T(8,128)S(1)}, f32[1056,128]{1,0:T(8,128)S(1)}, u32[]{:S(2)}, u32[]{:S(2)}) collective-permute-start(f32[1056,128]{1,0:T(8,128)S(1)} %get-tuple-element.14.own_ref), channel_id=1, source_target_pairs={{0,16},{16,0},{1,17},{17,1},{2,18},{18,2},{3,19},{19,3},{4,20},{20... | collective-permute-start | bytes 1622024 | tf_op jit(solution)/shard_map/ppermute | solution.py:456
  12.7 13.8 %collective-permute-start = (f32[200,128]{1,0:T(8,128)S(1)}, f32[200,128]{1,0:T(8,128)S(1)}, u32[]{:S(2)}, u32[]{:S(2)}) collective-permute-start(f32[200,128]{1,0:T(8,128)S(1)} %get-tuple-element.15), channel_id=1, source_target_pairs={{0,1},{1,0},{2,3},{3,2},{4,5},{5,4},{6,7},{7,6},{8,9},{9,8},{10,11... | collective-permute-start | bytes 307208 | tf_op jit(solution)/shard_map/ppermute | solution.py:462
  15.5 13.9 %collective-permute-start.1 = (f32[200,128]{1,0:T(8,128)S(1)}, f32[200,128]{1,0:T(8,128)S(1)}, u32[]{:S(2)}, u32[]{:S(2)}) collective-permute-start(f32[200,128]{1,0:T(8,128)S(1)} %get-tuple-element.16), channel_id=1, source_target_pairs={{0,15},{1,2},{2,1},{3,4},{4,3},{5,6},{6,5},{7,8},{8,7},{9,10},{10,... | collective-permute-start | bytes 307208 | tf_op jit(solution)/shard_map/ppermute | solution.py:462
  29.4 12.1 %collective-permute-start.6 = (f32[712,128]{1,0:T(8,128)S(1)}, f32[712,128]{1,0:T(8,128)S(1)}, u32[]{:S(2)}, u32[]{:S(2)}) collective-permute-start(f32[712,128]{1,0:T(8,128)S(1)} %get-tuple-element.19), channel_id=1, source_target_pairs={{0,16},{16,0},{1,17},{17,1},{2,18},{18,2},{3,19},{19,3},{4,20},{20... | collective-permute-start | bytes 1093640 | tf_op jit(solution)/shard_map/ppermute | solution.py:456
  32.2 7.4 %collective-permute-start.4 = (f32[512,128]{1,0:T(8,128)S(1)}, f32[512,128]{1,0:T(8,128)S(1)}, u32[]{:S(2)}, u32[]{:S(2)}) collective-permute-start(f32[512,128]{1,0:T(8,128)S(1)} %get-tuple-element.17), channel_id=1, source_target_pairs={{0,32},{16,496},{32,64},{48,16},{64,96},{80,48},{96,128},{112,80},... | collective-permute-start | bytes 786440 | tf_op jit(solution)/shard_map/ppermute | solution.py:451
  35.2 6.3 %collective-permute-start.5 = (f32[200,128]{1,0:T(8,128)S(1)}, f32[200,128]{1,0:T(8,128)S(1)}, u32[]{:S(2)}, u32[]{:S(2)}) collective-permute-start(f32[200,128]{1,0:T(8,128)S(1)} %get-tuple-element.18), channel_id=1, source_target_pairs={{0,496},{16,32},{32,16},{48,64},{64,48},{80,96},{96,80},{112,128},... | collective-permute-start | bytes 307208 | tf_op jit(solution)/shard_map/ppermute | solution.py:446

commit v6 on v5

--- a/solution.py
+++ b/solution.py
@@ -165,6 +165,40 @@
     return lax.dot_general(left, right, (((1,), (1,)), ((), ())), preferred_element_type=F32)
 
 
+def moved(value, blocks):
+    return pltpu.roll(value, (blocks * PROBES) % LANES, 1)
+
+
+def places():
+    row = lax.broadcasted_iota(jnp.int32, (PROBES, LANES), 0)
+    lane = lax.broadcasted_iota(jnp.int32, (PROBES, LANES), 1)
+    return row, lane, lane % PROBES
+
+
+def packed(first, last):
+    row, lane, column = places()
+    other = moved(last, -1)
+    diagonals = jnp.sum(jnp.where(row == column, other, 0.0), axis=0, keepdims=True)
+    slanted = pltpu.roll(jnp.broadcast_to(diagonals, (8, LANES)), 0, 1, stride=16, stride_axis=0)
+    slanted = jnp.concatenate([slanted] * (PROBES // 8), 0)
+    held_here = (row >= 17) & (row < 23) & (lane >= 96) & (lane < 112)
+    return jnp.where(row <= column, first, jnp.where(held_here, slanted, other))
+
+
+def unpacked(value):
+    row, lane, column = places()
+    turned = value.T
+    turned = jnp.concatenate([turned[block * PROBES : (block + 1) * PROBES, :] for block in range(4)], 1)
+    slanted = jnp.zeros((8, LANES), F32)
+    for step in range(1, 7):
+        mine = (row[:8] == step) & (lane[:8] // 16 == 6 - step)
+        slanted = jnp.where(mine, pltpu.roll(value[16:24, :], LANES - 16 * step, 1), slanted)
+    diagonals = jnp.sum(slanted, axis=0, keepdims=True)
+    first = jnp.where(row <= column, value, turned)
+    other = jnp.where(row == column, diagonals, jnp.where(row > column, value, turned))
+    return first, moved(other, 1)
+
+
 def basis_kernel(
     own_ref, high_ref, low_ref, near_ref, beside_ref, far_ref, corner_ref, cross_ref,
     split_out, gram_ref, first_ref, second_ref,
@@ -260,15 +294,14 @@
     left = jnp.concatenate([split[:PROBES], split[3 * PROBES : 4 * PROBES], split[7 * PROBES :]], 0)
     product = nt_dot(left, split)
     product = product[:, :LANES] + product[:, LANES:]
-    gram_ref[:PROBES, :] = product[:PROBES]
-    gram_ref[PROBES:, :] = product[PROBES : 2 * PROBES] + product[2 * PROBES :]
+    gram_ref[...] = packed(product[:PROBES], product[PROBES : 2 * PROBES] + product[2 * PROBES :])
 
 
 def basis(*operands):
     width = CELLS * LANES
     return pl.pallas_call(
         basis_kernel,
-        out_shape=(shaped(8 * PROBES, width, dtype=BF16), shaped(2 * PROBES, LANES)),
+        out_shape=(shaped(8 * PROBES, width, dtype=BF16), shaped(PROBES, LANES)),
         in_specs=vmem_specs(len(operands)),
         out_specs=tuple(vmem_specs(2)),
         scratch_shapes=[pltpu.VMEM((108 * PROBES, LANES), F32), pltpu.VMEM((68 * PROBES, LANES), F32)],
@@ -356,15 +389,12 @@
     return result + nt_dot(both, jnp.concatenate([right_lower, right_lower], 1))
 
 
-def finish_kernel(gram_ref, split_ref, alpha_ref, beta_ref, next_hbm, next_ref, left):
+def finish_kernel(
+    gram_ref, split_ref, alpha_hbm, beta_hbm, next_hbm, next_ref, alpha_ref, beta_ref, left, sent
+):
     lane = lax.broadcasted_iota(jnp.int32, (PROBES, LANES), 1)
     block_of = lane // PROBES
-    first = gram_ref[:PROBES, :]
-    last = gram_ref[PROBES:, :]
-
-    def moved(value, blocks):
-        return pltpu.roll(value, (blocks * PROBES) % LANES, 1)
-
+    first, last = unpacked(gram_ref[...])
     second = moved(first, -1) + jnp.where(block_of == 1, B0, B1) * moved(first, 1)
     second = jnp.where(block_of == 3, moved(last, 2), jnp.where(block_of == 0, 0.0, second))
     third = moved(last, 1) + jnp.where(block_of == 2, B1 * moved(second, 1) - B0 * first, 0.0)
@@ -401,7 +431,12 @@
     )
     position = mirrored()
     view = next_ref.reshape(PROBES, CELLS, LANES)
-    copies = []
+    copies = [
+        pltpu.make_async_copy(alpha_ref, alpha_hbm, sent.at[0]),
+        pltpu.make_async_copy(beta_ref, beta_hbm, sent.at[1]),
+    ]
+    for copy in copies:
+        copy.start()
     for group in range(CELLS // 8):
         columns = pl.ds(group * 8 * LANES, 8 * LANES)
         result = jnp.dot(weights, split_ref[:, columns], preferred_element_type=F32)
@@ -430,10 +465,13 @@
             jax.ShapeDtypeStruct((PROBES, CELLS, LANES), F32),
         ),
         in_specs=vmem_specs(2),
-        out_specs=tuple(vmem_specs(2)) + (pl.BlockSpec(memory_space=pltpu.HBM),),
+        out_specs=(pl.BlockSpec(memory_space=pltpu.HBM),) * 3,
         scratch_shapes=[
             pltpu.VMEM((PROBES * CELLS, LANES), F32),
+            pltpu.VMEM((3, PROBES, PROBES), F32),
+            pltpu.VMEM((3, PROBES, PROBES), F32),
             pltpu.SemaphoreType.DMA((CELLS // 8,)),
+            pltpu.SemaphoreType.DMA((2,)),
         ],
         compiler_params=pltpu.CompilerParams(vmem_limit_bytes=VMEM_LIMIT),
         interpret=INTERPRET,

time: 90.6 us -> 88 us (0.971)
  blocking collectives: 40.8 us -> 38.4 us
    all_to_all x3, blocking collectives: 40.8 us -> 38.4 us  [exchanged(): return lax.all_to_all(x, axes, 0, 0, tiled=True)]
where the time goes in v6:
time: 88 us; the launch traced here: 87.6 us
  blocking collectives  38.4 us (44%)
  starting transfers between devices  32.1 us (36%)
  Pallas kernels  8.92 us (10%)
  waiting for transfers between devices  7.29 us (8%)
    all_to_all x3, blocking collectives, exchanged(): return lax.all_to_all(x, axes, 0, 0, tiled=True)  38.4 us
    ppermute x2, starting transfers between devices, row_pair(): return lax.ppermute(x, GY, [(i, step(i) % count) for i in range(count)])  13.7 us
    ppermute x2, starting transfers between devices, on_chip(): return lax.ppermute(x, CORE, [(i, count - 1 - i) for i in range(count)])  8.86 us
    ppermute x2, starting transfers between devices, off_chip(): lax.ppermute(x, GX, [(i, (i - 1 if i % 2 == 0 else i + 1) % count) for i...  6.5 us
    pallas_call x1, Pallas kernels, finish(): pl.pallas_call(finish_kernel, out_shape=(jax.ShapeDtypeStruct((3, PROBES,...  4.89 us
    ppermute x1, starting transfers between devices, same_core(): lax.ppermute(x, GX, [(i, (i + 2 if i % 2 == 0 else i - 2) % count) for i...  2.98 us
    ppermute x2, waiting for transfers between devices, row_pair(): return lax.ppermute(x, GY, [(i, step(i) % count) for i in range(count)])  2.94 us
    pallas_call x1, Pallas kernels, basis(): pl.pallas_call(basis_kernel, out_shape=(shaped(8 * PROBES, width, dtype=B...  2.65 us
  transfers between devices with their start and end apart: 7, of which 3 were waited for; matrix products, arithmetic and copies ran while one was open for 0% of the time, Pallas kernels for 0%

profile of v6, /device:TPU:1, one launch (start us, length us, event | category | flops | bytes accessed | tf_op | source)
XLA Modules:
  0.0 87.6 jit_solution(8246789943201671478)
XLA Ops:
  0.6 1.4 %prepare.1 = (f32[1056,128]{1,0:T(8,128)S(1)}, f32[512,128]{1,0:T(8,128)S(1)}, f32[200,128]{1,0:T(8,128)S(1)}, f32[200,128]{1,0:T(8,128)S(1)}) custom-call(s32[1024,128]{1,0:T(8,128)} %bitcast.7, f32[32,128]{1,0:T(8,128)} %bitcast.8), custom_call_target="tpu_custom_call" | custom-call | tf_op jit(solution)/shard_map/prepare/pallas_call | solution.py:108
  2.0 4.6 %collective-permute-start.2 = (f32[1056,128]{1,0:T(8,128)S(1)}, f32[1056,128]{1,0:T(8,128)S(1)}, u32[]{:S(2)}, u32[]{:S(2)}) collective-permute-start(f32[1056,128]{1,0:T(8,128)S(1)} %get-tuple-element.14.own_ref), channel_id=1, source_target_pairs={{0,496},{16,32},{32,16},{48,64},{64,48},{80,96},{96,80},{112,128},... | collective-permute-start | bytes 1622024 | tf_op jit(solution)/shard_map/ppermute | solution.py:484
  6.6 6.1 %collective-permute-start.3 = (f32[1056,128]{1,0:T(8,128)S(1)}, f32[1056,128]{1,0:T(8,128)S(1)}, u32[]{:S(2)}, u32[]{:S(2)}) collective-permute-start(f32[1056,128]{1,0:T(8,128)S(1)} %get-tuple-element.14.own_ref), channel_id=1, source_target_pairs={{0,16},{16,0},{1,17},{17,1},{2,18},{18,2},{3,19},{19,3},{4,20},{20... | collective-permute-start | bytes 1622024 | tf_op jit(solution)/shard_map/ppermute | solution.py:494
  12.7 2.8 %collective-permute-start = (f32[200,128]{1,0:T(8,128)S(1)}, f32[200,128]{1,0:T(8,128)S(1)}, u32[]{:S(2)}, u32[]{:S(2)}) collective-permute-start(f32[200,128]{1,0:T(8,128)S(1)} %get-tuple-element.15), channel_id=1, source_target_pairs={{0,1},{1,0},{2,3},{3,2},{4,5},{5,4},{6,7},{7,6},{8,9},{9,8},{10,11... | collective-permute-start | bytes 307208 | tf_op jit(solution)/shard_map/ppermute | solution.py:500
  15.5 10.9 %collective-permute-start.1 = (f32[200,128]{1,0:T(8,128)S(1)}, f32[200,128]{1,0:T(8,128)S(1)}, u32[]{:S(2)}, u32[]{:S(2)}) collective-permute-start(f32[200,128]{1,0:T(8,128)S(1)} %get-tuple-element.16), channel_id=1, source_target_pairs={{0,15},{1,2},{2,1},{3,4},{4,3},{5,6},{6,5},{7,8},{8,7},{9,10},{10,... | collective-permute-start | bytes 307208 | tf_op jit(solution)/shard_map/ppermute | solution.py:500
  26.4 0.0 collective-permute-done.high_ref
  26.4 2.9 %collective-permute-done.1.low_ref = f32[200,128]{1,0:T(8,128)S(1)} collective-permute-done((f32[200,128]{1,0:T(8,128)S(1)}, f32[200,128]{1,0:T(8,128)S(1)}, u32[]{:S(2)}, u32[]{:S(2)}) %collective-permute-start.1) | collective-permute-done | bytes 102432 | tf_op jit(solution)/shard_map/ppermute | solution.py:500
  29.4 0.0 collective-permute-done.2.near_ref
  29.4 2.8 %collective-permute-start.6 = (f32[712,128]{1,0:T(8,128)S(1)}, f32[712,128]{1,0:T(8,128)S(1)}, u32[]{:S(2)}, u32[]{:S(2)}) collective-permute-start(f32[712,128]{1,0:T(8,128)S(1)} %get-tuple-element.19), channel_id=1, source_target_pairs={{0,16},{16,0},{1,17},{17,1},{2,18},{18,2},{3,19},{19,3},{4,20},{20... | collective-permute-start | bytes 1093640 | tf_op jit(solution)/shard_map/ppermute | solution.py:494
  32.2 3.0 %collective-permute-start.4 = (f32[512,128]{1,0:T(8,128)S(1)}, f32[512,128]{1,0:T(8,128)S(1)}, u32[]{:S(2)}, u32[]{:S(2)}) collective-permute-start(f32[512,128]{1,0:T(8,128)S(1)} %get-tuple-element.17), channel_id=1, source_target_pairs={{0,32},{16,496},{32,64},{48,16},{64,96},{80,48},{96,128},{112,80},... | collective-permute-start | bytes 786440 | tf_op jit(solution)/shard_map/ppermute | solution.py:489
  35.2 1.9 %collective-permute-start.5 = (f32[200,128]{1,0:T(8,128)S(1)}, f32[200,128]{1,0:T(8,128)S(1)}, u32[]{:S(2)}, u32[]{:S(2)}) collective-permute-start(f32[200,128]{1,0:T(8,128)S(1)} %get-tuple-element.18), channel_id=1, source_target_pairs={{0,496},{16,32},{32,16},{48,64},{64,48},{80,96},{96,80},{112,128},... | collective-permute-start | bytes 307208 | tf_op jit(solution)/shard_map/ppermute | solution.py:484
  37.1 2.5 %collective-permute-done.4.far_ref = f32[512,128]{1,0:T(8,128)S(1)} collective-permute-done((f32[512,128]{1,0:T(8,128)S(1)}, f32[512,128]{1,0:T(8,128)S(1)}, u32[]{:S(2)}, u32[]{:S(2)}) %collective-permute-start.4) | collective-permute-done | bytes 262176 | tf_op jit(solution)/shard_map/ppermute | solution.py:489
  39.6 0.0 collective-permute-done.3.beside_ref
  39.6 1.8 %collective-permute-done.5.corner_ref = f32[200,128]{1,0:T(8,128)S(1)} collective-permute-done((f32[200,128]{1,0:T(8,128)S(1)}, f32[200,128]{1,0:T(8,128)S(1)}, u32[]{:S(2)}, u32[]{:S(2)}) %collective-permute-start.5) | collective-permute-done | bytes 102432 | tf_op jit(solution)/shard_map/ppermute | solution.py:484
  41.5 0.0 collective-permute-done.6.cross_ref
  41.5 2.6 %basis.1 = (bf16[256,4096]{1,0:T(8,128)(2,1)S(1)}, f32[32,128]{1,0:T(8,128)S(1)}) custom-call(f32[1056,128]{1,0:T(8,128)S(1)} %get-tuple-element.14.own_ref, f32[200,128]{1,0:T(8,128)S(1)} %collective-permute-done.high_ref, f32[200,128]{1,0:T(8,128)S(1)} %collective-permute-done.1.low_ref, f32[1056,128]{1,0:T(8,128)S(1)} %collective-permute-done.2.near_ref, ...), custom_call_target="tpu_custom_call" | custom-call | tf_op jit(solution)/shard_map/basis/pallas_call | solution.py:302
  44.1 9.5 %all_to_all.15 = f32[8,4,128]{2,1,0:T(4,128)S(1)} all-to-all(f32[8,4,128]{2,1,0:T(4,128)S(1)} %bitcast.6), channel_id=1, replica_groups=mesh['gx_0'=2,'gx_1'=8,'gx_2'=2,'gy_0'=8,'gy_1'=2] {'gx_0','gx_2','gy_1'}, dimensions={0} | all-to-all | bytes 32768 | tf_op jit(solution)/shard_map/all_to_all | solution.py:504
  53.6 19.6 %all_to_all.16 = f32[64,4,128]{2,1,0:T(4,128)S(1)} all-to-all(f32[64,4,128]{2,1,0:T(4,128)S(1)} %broadcast_in_dim.4), channel_id=1, replica_groups=mesh['gx_0'=2,'gx_1'=8,'gx_2'=2,'gy_0'=8,'gy_1'=2] {'gx_1','gy_0'}, dimensions={0} | all-to-all | bytes 262144 | tf_op jit(solution)/shard_map/all_to_all | solution.py:504
  73.3 0.1 reduce_sum.19
  73.4 9.3 %all_to_all.17 = f32[8,4,128]{2,1,0:T(4,128)S(1)} all-to-all(f32[8,4,128]{2,1,0:T(4,128)S(1)} %broadcast_in_dim.5), channel_id=1, replica_groups=mesh['gx_0'=2,'gx_1'=8,'gx_2'=2,'gy_0'=8,'gy_1'=2] {'gx_0','gx_2','gy_1'}, dimensions={0} | all-to-all | bytes 32768 | tf_op jit(solution)/shard_map/all_to_all | solution.py:504
  82.7 4.9 %finish.1 = (f32[3,32,32]{2,1,0:T(8,128)}, f32[3,32,32]{2,1,0:T(8,128)}, f32[32,32,128]{2,1,0:T(8,128)}) custom-call(f32[32,128]{1,0:T(8,128)S(1)} %bitcast.5, bf16[256,4096]{1,0:T(8,128)(2,1)S(1)} %get-tuple-element.21.split_ref), custom_call_target="tpu_custom_call" | custom-call | tf_op jit(solution)/shard_map/finish/pallas_call | solution.py:460
  (4 shorter events, 0.1 us)
Async XLA Ops:
  2.0 27.4 %collective-permute-start.2 = (f32[1056,128]{1,0:T(8,128)S(1)}, f32[1056,128]{1,0:T(8,128)S(1)}, u32[]{:S(2)}, u32[]{:S(2)}) collective-permute-start(f32[1056,128]{1,0:T(8,128)S(1)} %get-tuple-element.14.own_ref), channel_id=1, source_target_pairs={{0,496},{16,32},{32,16},{48,64},{64,48},{80,96},{96,80},{112,128},... | collective-permute-start | bytes 1622024 | tf_op jit(solution)/shard_map/ppermute | solution.py:484
  6.6 33.0 %collective-permute-start.3 = (f32[1056,128]{1,0:T(8,128)S(1)}, f32[1056,128]{1,0:T(8,128)S(1)}, u32[]{:S(2)}, u32[]{:S(2)}) collective-permute-start(f32[1056,128]{1,0:T(8,128)S(1)} %get-tuple-element.14.own_ref), channel_id=1, source_target_pairs={{0,16},{16,0},{1,17},{17,1},{2,18},{18,2},{3,19},{19,3},{4,20},{20... | collective-permute-start | bytes 1622024 | tf_op jit(solution)/shard_map/ppermute | solution.py:494
  12.7 13.8 %collective-permute-start = (f32[200,128]{1,0:T(8,128)S(1)}, f32[200,128]{1,0:T(8,128)S(1)}, u32[]{:S(2)}, u32[]{:S(2)}) collective-permute-start(f32[200,128]{1,0:T(8,128)S(1)} %get-tuple-element.15), channel_id=1, source_target_pairs={{0,1},{1,0},{2,3},{3,2},{4,5},{5,4},{6,7},{7,6},{8,9},{9,8},{10,11... | collective-permute-start | bytes 307208 | tf_op jit(solution)/shard_map/ppermute | solution.py:500
  15.5 13.9 %collective-permute-start.1 = (f32[200,128]{1,0:T(8,128)S(1)}, f32[200,128]{1,0:T(8,128)S(1)}, u32[]{:S(2)}, u32[]{:S(2)}) collective-permute-start(f32[200,128]{1,0:T(8,128)S(1)} %get-tuple-element.16), channel_id=1, source_target_pairs={{0,15},{1,2},{2,1},{3,4},{4,3},{5,6},{6,5},{7,8},{8,7},{9,10},{10,... | collective-permute-start | bytes 307208 | tf_op jit(solution)/shard_map/ppermute | solution.py:500
  29.4 12.1 %collective-permute-start.6 = (f32[712,128]{1,0:T(8,128)S(1)}, f32[712,128]{1,0:T(8,128)S(1)}, u32[]{:S(2)}, u32[]{:S(2)}) collective-permute-start(f32[712,128]{1,0:T(8,128)S(1)} %get-tuple-element.19), channel_id=1, source_target_pairs={{0,16},{16,0},{1,17},{17,1},{2,18},{18,2},{3,19},{19,3},{4,20},{20... | collective-permute-start | bytes 1093640 | tf_op jit(solution)/shard_map/ppermute | solution.py:494
  32.2 7.4 %collective-permute-start.4 = (f32[512,128]{1,0:T(8,128)S(1)}, f32[512,128]{1,0:T(8,128)S(1)}, u32[]{:S(2)}, u32[]{:S(2)}) collective-permute-start(f32[512,128]{1,0:T(8,128)S(1)} %get-tuple-element.17), channel_id=1, source_target_pairs={{0,32},{16,496},{32,64},{48,16},{64,96},{80,48},{96,128},{112,80},... | collective-permute-start | bytes 786440 | tf_op jit(solution)/shard_map/ppermute | solution.py:489
  35.2 6.3 %collective-permute-start.5 = (f32[200,128]{1,0:T(8,128)S(1)}, f32[200,128]{1,0:T(8,128)S(1)}, u32[]{:S(2)}, u32[]{:S(2)}) collective-permute-start(f32[200,128]{1,0:T(8,128)S(1)} %get-tuple-element.18), channel_id=1, source_target_pairs={{0,496},{16,32},{32,16},{48,64},{64,48},{80,96},{96,80},{112,128},... | collective-permute-start | bytes 307208 | tf_op jit(solution)/shard_map/ppermute | solution.py:484

commit v7 on v6

--- a/solution.py
+++ b/solution.py
@@ -1,3 +1,5 @@
+import functools
+
 import jax
 import jax.numpy as jnp
 from jax import lax
@@ -30,8 +32,7 @@
 
 OWN_ROWS = CELLS * PROBES + CELLS
 EDGE_ROWS = 2 * 3 * PROBES + 8
-CORNER_ROWS = 6 * PROBES + 8
-CROSS_ROWS = ROWS * PROBES + CORNER_ROWS
+MESSAGE_ROWS = (ROWS + 6) * PROBES + 8
 
 
 def vmem_specs(count):
@@ -61,7 +62,7 @@
 
 
 def prepare_kernel(
-    signs_hbm, diag_hbm, own_ref, far_ref, high_ref, low_ref, signs_ref, diag_ref, arrived
+    signs_hbm, diag_hbm, own_ref, high_ref, low_ref, signs_ref, diag_ref, arrived
 ):
     rows = 8 * CELLS
     copies = []
@@ -96,8 +97,6 @@
                 ref[pl.ds(index * PROBES + group * 8, 8), :] = probes
 
             put(own_ref, cell)
-            if plane == 1:
-                put(far_ref, row)
             for ref, step in ((low_ref, row), (high_ref, ROWS - 1 - row)):
                 if step < 3:
                     put(ref, plane * 3 + step)
@@ -109,12 +108,11 @@
         prepare_kernel,
         out_shape=(
             shaped(OWN_ROWS, LANES),
-            shaped(ROWS * PROBES, LANES),
             shaped(EDGE_ROWS, LANES),
             shaped(EDGE_ROWS, LANES),
         ),
         in_specs=[hbm, hbm],
-        out_specs=tuple(vmem_specs(4)),
+        out_specs=tuple(vmem_specs(3)),
         scratch_shapes=[
             pltpu.VMEM((PROBES * CELLS, LANES), jnp.int32),
             pltpu.VMEM((CELLS, LANES), F32),
@@ -126,39 +124,34 @@
     )(*(pltpu.with_memory_space_constraint(x, pltpu.HBM) for x in (signs, diagonal)))
 
 
-def pack_kernel(high_ref, low_ref, near_ref, corner_ref, cross_ref):
+def pack_kernel(plane, first_row, high_ref, low_ref, across_ref, message_ref):
     def edge(plane, row):
         if row < 0:
             return low_ref[row_of(plane * 3 - row - 1), :]
         return high_ref[row_of(plane * 3 + row - ROWS), :]
 
-    def edge_line(plane, row):
-        ref = low_ref if row < 0 else high_ref
-        start = 6 * PROBES + plane * 2
-        return ref[start : start + 1, :]
-
     for row in range(ROWS):
-        cross_ref[row_of(row), :] = near_ref[row_of(row), :]
-    for ref, plane, first in ((corner_ref, 0, 0), (cross_ref, 1, ROWS)):
-        for place, row in enumerate((-2, -1, ROWS, ROWS + 1)):
-            ref[row_of(first + place), :] = edge(plane, row)
-        for place, row in enumerate((-1, ROWS)):
-            ref[row_of(first + 4 + place), :] = edge(1 - plane, row)
-            start = (first + 6) * PROBES + place
-            ref[start : start + 1, :] = edge_line(plane, row)
-        ref[(first + 6) * PROBES + 2 :, :] = jnp.zeros((6, LANES), F32)
-
-
-def pack(high, low, near):
+        message_ref[row_of(row), :] = across_ref[row_of(first_row + row), :]
+    for place, row in enumerate((-2, -1, ROWS, ROWS + 1)):
+        message_ref[row_of(ROWS + place), :] = edge(plane, row)
+    for place, row in enumerate((-1, ROWS)):
+        message_ref[row_of(ROWS + 4 + place), :] = edge(1 - plane, row)
+        start = (ROWS + 6) * PROBES + place
+        source = low_ref if row < 0 else high_ref
+        line = 6 * PROBES + plane * 2
+        message_ref[start : start + 1, :] = source[line : line + 1, :]
+    message_ref[(ROWS + 6) * PROBES + 2 :, :] = jnp.zeros((6, LANES), F32)
+
+
+def pack(plane, first_row, *operands):
     return pl.pallas_call(
-        pack_kernel,
-        out_shape=(shaped(CORNER_ROWS, LANES), shaped(CROSS_ROWS, LANES)),
-        in_specs=vmem_specs(3),
-        out_specs=tuple(vmem_specs(2)),
+        functools.partial(pack_kernel, plane, first_row),
+        out_shape=shaped(MESSAGE_ROWS, LANES),
+        in_specs=vmem_specs(len(operands)),
+        out_specs=vmem_specs(1)[0],
         compiler_params=pltpu.CompilerParams(vmem_limit_bytes=VMEM_LIMIT),
         interpret=INTERPRET,
-        name="pack",
-    )(*held(high, low, near))
+    )(*held(*operands))
 
 
 def nt_dot(left, right):
@@ -200,7 +193,7 @@
 
 
 def basis_kernel(
-    own_ref, high_ref, low_ref, near_ref, beside_ref, far_ref, corner_ref, cross_ref,
+    own_ref, high_ref, low_ref, near_ref, beside_ref, corner_ref, cross_ref,
     split_out, gram_ref, first_ref, second_ref,
 ):
     def distance(plane):
@@ -215,14 +208,14 @@
                 return high_ref[row_of(plane * 3 + row - ROWS), :]
             return own_ref[row_of(plane * ROWS + row), :]
         if away == 3:
-            return (far_ref if plane < 0 else cross_ref)[row_of(row), :]
+            return (corner_ref if plane < 0 else cross_ref)[row_of(row), :]
         if 0 <= row < ROWS:
             if plane < 0:
                 return near_ref[row_of((away - 1) * ROWS + row), :]
             return beside_ref[row_of((2 - away) * ROWS + row), :]
-        ref, first = (corner_ref, 0) if plane < 0 else (cross_ref, ROWS)
+        ref = corner_ref if plane < 0 else cross_ref
         places = (-2, -1, ROWS, ROWS + 1) if away == 1 else (-1, ROWS)
-        return ref[row_of(first + 4 * (away - 1) + places.index(row)), :]
+        return ref[row_of(ROWS + 4 * (away - 1) + places.index(row)), :]
 
     def factor(plane, row):
         away = distance(plane)
@@ -239,8 +232,8 @@
             else:
                 ref, start = beside_ref, CELLS * PROBES + (2 - away) * ROWS + row
         else:
-            ref, first = (corner_ref, 0) if plane < 0 else (cross_ref, ROWS)
-            start = (first + 6) * PROBES + (0 if row < 0 else 1)
+            ref = corner_ref if plane < 0 else cross_ref
+            start = (ROWS + 6) * PROBES + (0 if row < 0 else 1)
         return ref[start : start + 1, :] + (6.0 - SHIFT)
 
     def cells(width):
@@ -484,11 +477,6 @@
     return lax.ppermute(x, GX, [(i, (i - 1 if i % 2 == 0 else i + 1) % count) for i in range(count)])
 
 
-def same_core(x):
-    count = lax.axis_size(GX)
-    return lax.ppermute(x, GX, [(i, (i + 2 if i % 2 == 0 else i - 2) % count) for i in range(count)])
-
-
 def on_chip(x):
     count = lax.axis_size(CORE)
     return lax.ppermute(x, CORE, [(i, count - 1 - i) for i in range(count)])
@@ -518,16 +506,16 @@
 def per_device(probe_signs, diagonal):
     signs = probe_signs.reshape(PROBES * CELLS, LANES)
     diag = diagonal.reshape(CELLS, LANES)
-    own, outer, top, bottom = prepare(signs, diag)
-    near = off_chip(own)
+    own, top, bottom = prepare(signs, diag)
     high = row_pair(top, 0)
     low = row_pair(bottom, 1)
-    far = same_core(outer)
+    near = off_chip(own)
     beside = on_chip(own)
-    corner_message, cross_message = pack(high, low, near)
+    corner_message = pack(0, ROWS, high, low, beside)
     corner = off_chip(corner_message)
+    cross_message = pack(1, 0, high, low, near)
     cross = on_chip(cross_message)
-    split, gram = basis(own, high, low, near, beside, far, corner, cross)
+    split, gram = basis(own, high, low, near, beside, corner, cross)
     alphas, betas, following = finish(reduced(gram), split)
     return (alphas, betas, following.reshape(PROBES, PLANES, ROWS, LANES))
 

time: 88 us -> 85.4 us (0.970)
  waiting for transfers between devices: 7.29 us -> 3.36 us
  blocking collectives: 38.4 us -> 41.8 us
  starting transfers between devices: 32.1 us -> 30.1 us
    ppermute x2, starting transfers between devices: 8.86 us -> 12.5 us  [on_chip(): return lax.ppermute(x, CORE, [(i, count - 1 - i) for i in range(count)])]
    all_to_all x3, blocking collectives: 38.4 us -> 41.8 us  [exchanged(): return lax.all_to_all(x, axes, 0, 0, tiled=True)]
    ppermute x1 -> x0, starting transfers between devices: 2.98 us -> none  [same_core(): lax.ppermute(x, GX, [(i, (i + 2 if i % 2 == 0 else i - 2) % count) for i...]
    ppermute x2, starting transfers between devices: 13.7 us -> 11.1 us  [row_pair(): return lax.ppermute(x, GY, [(i, step(i) % count) for i in range(count)])]
    ppermute x1 -> x0, waiting for transfers between devices: 2.5 us -> none  [same_core(): lax.ppermute(x, GX, [(i, (i + 2 if i % 2 == 0 else i - 2) % count) for i...]
    ppermute x2, waiting for transfers between devices: 2.94 us -> 2.03 us  [row_pair(): return lax.ppermute(x, GY, [(i, step(i) % count) for i in range(count)])]
  transfers between devices with their start and end apart: 7 -> 6, of which waited for: 3 -> 2; matrix products, arithmetic and copies ran while one was open for 0% -> 0% of each run, Pallas kernels for 0% -> 0%
where the time goes in v7:
time: 85.4 us; the launch traced here: 85 us
  blocking collectives  41.8 us (49%)
  starting transfers between devices  30.1 us (35%)
  Pallas kernels  8.92 us (10%)
  waiting for transfers between devices  3.36 us (4%)
    all_to_all x3, blocking collectives, exchanged(): return lax.all_to_all(x, axes, 0, 0, tiled=True)  41.8 us
    ppermute x2, starting transfers between devices, on_chip(): return lax.ppermute(x, CORE, [(i, count - 1 - i) for i in range(count)])  12.5 us
    ppermute x2, starting transfers between devices, row_pair(): return lax.ppermute(x, GY, [(i, step(i) % count) for i in range(count)])  11.1 us
    ppermute x2, starting transfers between devices, off_chip(): lax.ppermute(x, GX, [(i, (i - 1 if i % 2 == 0 else i + 1) % count) for i...  6.46 us
    pallas_call x1, Pallas kernels, finish(): pl.pallas_call(finish_kernel, out_shape=(jax.ShapeDtypeStruct((3, PROBES,...  4.89 us
    pallas_call x1, Pallas kernels, basis(): pl.pallas_call(basis_kernel, out_shape=(shaped(8 * PROBES, width, dtype=B...  2.63 us
    ppermute x2, waiting for transfers between devices, row_pair(): return lax.ppermute(x, GY, [(i, step(i) % count) for i in range(count)])  2.03 us
  transfers between devices with their start and end apart: 6, of which 2 were waited for; matrix products, arithmetic and copies ran while one was open for 0% of the time, Pallas kernels for 0%

profile of v7, /device:TPU:1, one launch (start us, length us, event | category | flops | bytes accessed | tf_op | source)
XLA Modules:
  0.0 85.0 jit_solution(16259379788593193878)
XLA Ops:
  0.6 1.4 %prepare.1 = (f32[1056,128]{1,0:T(8,128)S(1)}, f32[200,128]{1,0:T(8,128)S(1)}, f32[200,128]{1,0:T(8,128)S(1)}) custom-call(s32[1024,128]{1,0:T(8,128)} %bitcast.7, f32[32,128]{1,0:T(8,128)} %bitcast.8), custom_call_target="tpu_custom_call" | custom-call | tf_op jit(solution)/shard_map/prepare/pallas_call | solution.py:107
  2.0 8.7 %collective-permute-start.3 = (f32[1056,128]{1,0:T(8,128)S(1)}, f32[1056,128]{1,0:T(8,128)S(1)}, u32[]{:S(2)}, u32[]{:S(2)}) collective-permute-start(f32[1056,128]{1,0:T(8,128)S(1)} %get-tuple-element.11.own_ref), channel_id=1, source_target_pairs={{0,16},{16,0},{1,17},{17,1},{2,18},{18,2},{3,19},{19,3},{4,20},{20... | collective-permute-start | bytes 1622024 | tf_op jit(solution)/shard_map/ppermute | solution.py:482
  10.7 1.9 %collective-permute-start.2 = (f32[1056,128]{1,0:T(8,128)S(1)}, f32[1056,128]{1,0:T(8,128)S(1)}, u32[]{:S(2)}, u32[]{:S(2)}) collective-permute-start(f32[1056,128]{1,0:T(8,128)S(1)} %get-tuple-element.11.own_ref), channel_id=1, source_target_pairs={{0,496},{16,32},{32,16},{48,64},{64,48},{80,96},{96,80},{112,128},... | collective-permute-start | bytes 1622024 | tf_op jit(solution)/shard_map/ppermute | solution.py:477
  12.7 1.9 %collective-permute-start = (f32[200,128]{1,0:T(8,128)S(1)}, f32[200,128]{1,0:T(8,128)S(1)}, u32[]{:S(2)}, u32[]{:S(2)}) collective-permute-start(f32[200,128]{1,0:T(8,128)S(1)} %get-tuple-element.12), channel_id=1, source_target_pairs={{0,1},{1,0},{2,3},{3,2},{4,5},{5,4},{6,7},{7,6},{8,9},{9,8},{10,11... | collective-permute-start | bytes 307208 | tf_op jit(solution)/shard_map/ppermute | solution.py:488
  14.6 9.2 %collective-permute-start.1 = (f32[200,128]{1,0:T(8,128)S(1)}, f32[200,128]{1,0:T(8,128)S(1)}, u32[]{:S(2)}, u32[]{:S(2)}) collective-permute-start(f32[200,128]{1,0:T(8,128)S(1)} %get-tuple-element.13), channel_id=1, source_target_pairs={{0,15},{1,2},{2,1},{3,4},{4,3},{5,6},{6,5},{7,8},{8,7},{9,10},{10,... | collective-permute-start | bytes 307208 | tf_op jit(solution)/shard_map/ppermute | solution.py:488
  23.8 0.0 collective-permute-done.high_ref
  23.8 2.0 %collective-permute-done.1.low_ref = f32[200,128]{1,0:T(8,128)S(1)} collective-permute-done((f32[200,128]{1,0:T(8,128)S(1)}, f32[200,128]{1,0:T(8,128)S(1)}, u32[]{:S(2)}, u32[]{:S(2)}) %collective-permute-start.1) | collective-permute-done | bytes 102432 | tf_op jit(solution)/shard_map/ppermute | solution.py:488
  25.8 0.0 collective-permute-done.3.across_ref.beside_ref
  25.9 4.5 %collective-permute-start.4 = (f32[712,128]{1,0:T(8,128)S(1)}, f32[712,128]{1,0:T(8,128)S(1)}, u32[]{:S(2)}, u32[]{:S(2)}) collective-permute-start(f32[712,128]{1,0:T(8,128)S(1)} %shard_map.49), channel_id=1, source_target_pairs={{0,496},{16,32},{32,16},{48,64},{64,48},{80,96},{96,80},{112,128},... | collective-permute-start | bytes 1093640 | tf_op jit(solution)/shard_map/ppermute | solution.py:477
  30.4 0.0 collective-permute-done.2.across_ref.near_ref
  30.4 3.8 %collective-permute-start.5 = (f32[712,128]{1,0:T(8,128)S(1)}, f32[712,128]{1,0:T(8,128)S(1)}, u32[]{:S(2)}, u32[]{:S(2)}) collective-permute-start(f32[712,128]{1,0:T(8,128)S(1)} %shard_map.50), channel_id=1, source_target_pairs={{0,16},{16,0},{1,17},{17,1},{2,18},{18,2},{3,19},{19,3},{4,20},{20... | collective-permute-start | bytes 1093640 | tf_op jit(solution)/shard_map/ppermute | solution.py:482
  34.2 1.3 %collective-permute-done.4.corner_ref = f32[712,128]{1,0:T(8,128)S(1)} collective-permute-done((f32[712,128]{1,0:T(8,128)S(1)}, f32[712,128]{1,0:T(8,128)S(1)}, u32[]{:S(2)}, u32[]{:S(2)}) %collective-permute-start.4) | collective-permute-done | bytes 364576 | tf_op jit(solution)/shard_map/ppermute | solution.py:477
  35.5 0.0 collective-permute-done.5.cross_ref
  35.5 2.6 %basis.1 = (bf16[256,4096]{1,0:T(8,128)(2,1)S(1)}, f32[32,128]{1,0:T(8,128)S(1)}) custom-call(f32[1056,128]{1,0:T(8,128)S(1)} %get-tuple-element.11.own_ref, f32[200,128]{1,0:T(8,128)S(1)} %collective-permute-done.high_ref, f32[200,128]{1,0:T(8,128)S(1)} %collective-permute-done.1.low_ref, f32[1056,128]{1,0:T(8,128)S(1)} %collective-permute-done.2.across_ref.near_ref, ...), custom_call_target="tpu_custom_call" | custom-call | tf_op jit(solution)/shard_map/basis/pallas_call | solution.py:295
  38.2 12.9 %all_to_all.15 = f32[8,4,128]{2,1,0:T(4,128)S(1)} all-to-all(f32[8,4,128]{2,1,0:T(4,128)S(1)} %bitcast.6), channel_id=1, replica_groups=mesh['gx_0'=2,'gx_1'=8,'gx_2'=2,'gy_0'=8,'gy_1'=2] {'gx_0','gx_2','gy_1'}, dimensions={0} | all-to-all | bytes 32768 | tf_op jit(solution)/shard_map/all_to_all | solution.py:492
  51.1 19.6 %all_to_all.16 = f32[64,4,128]{2,1,0:T(4,128)S(1)} all-to-all(f32[64,4,128]{2,1,0:T(4,128)S(1)} %broadcast_in_dim.4), channel_id=1, replica_groups=mesh['gx_0'=2,'gx_1'=8,'gx_2'=2,'gy_0'=8,'gy_1'=2] {'gx_1','gy_0'}, dimensions={0} | all-to-all | bytes 262144 | tf_op jit(solution)/shard_map/all_to_all | solution.py:492
  70.7 0.1 reduce_sum.19
  70.8 9.3 %all_to_all.17 = f32[8,4,128]{2,1,0:T(4,128)S(1)} all-to-all(f32[8,4,128]{2,1,0:T(4,128)S(1)} %broadcast_in_dim.5), channel_id=1, replica_groups=mesh['gx_0'=2,'gx_1'=8,'gx_2'=2,'gy_0'=8,'gy_1'=2] {'gx_0','gx_2','gy_1'}, dimensions={0} | all-to-all | bytes 32768 | tf_op jit(solution)/shard_map/all_to_all | solution.py:492
  80.1 4.9 %finish.1 = (f32[3,32,32]{2,1,0:T(8,128)}, f32[3,32,32]{2,1,0:T(8,128)}, f32[32,32,128]{2,1,0:T(8,128)}) custom-call(f32[32,128]{1,0:T(8,128)S(1)} %bitcast.5, bf16[256,4096]{1,0:T(8,128)(2,1)S(1)} %get-tuple-element.15.split_ref), custom_call_target="tpu_custom_call" | custom-call | tf_op jit(solution)/shard_map/finish/pallas_call | solution.py:453
  (5 shorter events, 0.1 us)
Async XLA Ops:
  2.0 23.8 %collective-permute-start.3 = (f32[1056,128]{1,0:T(8,128)S(1)}, f32[1056,128]{1,0:T(8,128)S(1)}, u32[]{:S(2)}, u32[]{:S(2)}) collective-permute-start(f32[1056,128]{1,0:T(8,128)S(1)} %get-tuple-element.11.own_ref), channel_id=1, source_target_pairs={{0,16},{16,0},{1,17},{17,1},{2,18},{18,2},{3,19},{19,3},{4,20},{20... | collective-permute-start | bytes 1622024 | tf_op jit(solution)/shard_map/ppermute | solution.py:482
  10.7 19.7 %collective-permute-start.2 = (f32[1056,128]{1,0:T(8,128)S(1)}, f32[1056,128]{1,0:T(8,128)S(1)}, u32[]{:S(2)}, u32[]{:S(2)}) collective-permute-start(f32[1056,128]{1,0:T(8,128)S(1)} %get-tuple-element.11.own_ref), channel_id=1, source_target_pairs={{0,496},{16,32},{32,16},{48,64},{64,48},{80,96},{96,80},{112,128},... | collective-permute-start | bytes 1622024 | tf_op jit(solution)/shard_map/ppermute | solution.py:477
  12.7 11.1 %collective-permute-start = (f32[200,128]{1,0:T(8,128)S(1)}, f32[200,128]{1,0:T(8,128)S(1)}, u32[]{:S(2)}, u32[]{:S(2)}) collective-permute-start(f32[200,128]{1,0:T(8,128)S(1)} %get-tuple-element.12), channel_id=1, source_target_pairs={{0,1},{1,0},{2,3},{3,2},{4,5},{5,4},{6,7},{7,6},{8,9},{9,8},{10,11... | collective-permute-start | bytes 307208 | tf_op jit(solution)/shard_map/ppermute | solution.py:488
  14.6 11.2 %collective-permute-start.1 = (f32[200,128]{1,0:T(8,128)S(1)}, f32[200,128]{1,0:T(8,128)S(1)}, u32[]{:S(2)}, u32[]{:S(2)}) collective-permute-start(f32[200,128]{1,0:T(8,128)S(1)} %get-tuple-element.13), channel_id=1, source_target_pairs={{0,15},{1,2},{2,1},{3,4},{4,3},{5,6},{6,5},{7,8},{8,7},{9,10},{10,... | collective-permute-start | bytes 307208 | tf_op jit(solution)/shard_map/ppermute | solution.py:488
  25.9 9.7 %collective-permute-start.4 = (f32[712,128]{1,0:T(8,128)S(1)}, f32[712,128]{1,0:T(8,128)S(1)}, u32[]{:S(2)}, u32[]{:S(2)}) collective-permute-start(f32[712,128]{1,0:T(8,128)S(1)} %shard_map.49), channel_id=1, source_target_pairs={{0,496},{16,32},{32,16},{48,64},{64,48},{80,96},{96,80},{112,128},... | collective-permute-start | bytes 1093640 | tf_op jit(solution)/shard_map/ppermute | solution.py:477
  30.4 5.1 %collective-permute-start.5 = (f32[712,128]{1,0:T(8,128)S(1)}, f32[712,128]{1,0:T(8,128)S(1)}, u32[]{:S(2)}, u32[]{:S(2)}) collective-permute-start(f32[712,128]{1,0:T(8,128)S(1)} %shard_map.50), channel_id=1, source_target_pairs={{0,16},{16,0},{1,17},{17,1},{2,18},{18,2},{3,19},{19,3},{4,20},{20... | collective-permute-start | bytes 1093640 | tf_op jit(solution)/shard_map/ppermute | solution.py:482

commit v8 on v7

--- a/solution.py
+++ b/solution.py
@@ -192,115 +192,175 @@
     return first, moved(other, 1)
 
 
-def basis_kernel(
-    own_ref, high_ref, low_ref, near_ref, beside_ref, corner_ref, cross_ref,
-    split_out, gram_ref, first_ref, second_ref,
-):
-    def distance(plane):
-        return -plane if plane < 0 else max(plane - (PLANES - 1), 0)
-
-    def k0(plane, row):
+def distance(plane):
+    return -plane if plane < 0 else max(plane - (PLANES - 1), 0)
+
+
+def cells(width):
+    found = []
+    for plane in range(-width, PLANES + width):
+        extra = width - distance(plane)
+        for row in range(-extra, ROWS + extra):
+            found.append((plane, row))
+    return found
+
+
+def known_early(order, plane, row):
+    if order == 0:
+        return distance(plane) == 0 or (distance(plane) < 3 and 0 <= row < ROWS)
+    around = [(plane, row), (plane - 1, row), (plane + 1, row), (plane, row - 1), (plane, row + 1)]
+    return all(known_early(order - 1, *cell) for cell in around)
+
+
+def slots(order, width, early):
+    chosen = [cell for cell in cells(width) if known_early(order, *cell) == early]
+    return {cell: slot for slot, cell in enumerate(chosen)}
+
+
+FIRST_EARLY, FIRST_LATE = slots(1, 2, True), slots(1, 2, False)
+SECOND_EARLY, SECOND_LATE = slots(2, 1, True), slots(2, 1, False)
+
+
+class Fields:
+    def __init__(self, own, high, low, near, beside, corner, cross, first, second, split):
+        self.own, self.high, self.low, self.near, self.beside = own, high, low, near, beside
+        self.corner, self.cross = corner, cross
+        self.first, self.second, self.split = first, second, split
+
+    def k0(self, plane, row):
         away = distance(plane)
         if away == 0:
             if row < 0:
-                return low_ref[row_of(plane * 3 - row - 1), :]
+                return self.low[row_of(plane * 3 - row - 1), :]
             if row >= ROWS:
-                return high_ref[row_of(plane * 3 + row - ROWS), :]
-            return own_ref[row_of(plane * ROWS + row), :]
+                return self.high[row_of(plane * 3 + row - ROWS), :]
+            return self.own[row_of(plane * ROWS + row), :]
         if away == 3:
-            return (corner_ref if plane < 0 else cross_ref)[row_of(row), :]
+            return (self.corner if plane < 0 else self.cross)[row_of(row), :]
         if 0 <= row < ROWS:
             if plane < 0:
-                return near_ref[row_of((away - 1) * ROWS + row), :]
-            return beside_ref[row_of((2 - away) * ROWS + row), :]
-        ref = corner_ref if plane < 0 else cross_ref
-        places = (-2, -1, ROWS, ROWS + 1) if away == 1 else (-1, ROWS)
-        return ref[row_of(ROWS + 4 * (away - 1) + places.index(row)), :]
-
-    def factor(plane, row):
+                return self.near[row_of((away - 1) * ROWS + row), :]
+            return self.beside[row_of((2 - away) * ROWS + row), :]
+        ref = self.corner if plane < 0 else self.cross
+        known = (-2, -1, ROWS, ROWS + 1) if away == 1 else (-1, ROWS)
+        return ref[row_of(ROWS + 4 * (away - 1) + known.index(row)), :]
+
+    def factor(self, plane, row):
         away = distance(plane)
         if away == 0:
             if row < 0:
-                ref, start = low_ref, 6 * PROBES + plane * 2 - row - 1
+                ref, start = self.low, 6 * PROBES + plane * 2 - row - 1
             elif row >= ROWS:
-                ref, start = high_ref, 6 * PROBES + plane * 2 + row - ROWS
+                ref, start = self.high, 6 * PROBES + plane * 2 + row - ROWS
             else:
-                ref, start = own_ref, CELLS * PROBES + plane * ROWS + row
+                ref, start = self.own, CELLS * PROBES + plane * ROWS + row
         elif 0 <= row < ROWS:
             if plane < 0:
-                ref, start = near_ref, CELLS * PROBES + (away - 1) * ROWS + row
+                ref, start = self.near, CELLS * PROBES + (away - 1) * ROWS + row
             else:
-                ref, start = beside_ref, CELLS * PROBES + (2 - away) * ROWS + row
+                ref, start = self.beside, CELLS * PROBES + (2 - away) * ROWS + row
         else:
-            ref = corner_ref if plane < 0 else cross_ref
+            ref = self.corner if plane < 0 else self.cross
             start = (ROWS + 6) * PROBES + (0 if row < 0 else 1)
         return ref[start : start + 1, :] + (6.0 - SHIFT)
 
-    def cells(width):
-        found = []
-        for plane in range(-width, PLANES + width):
-            extra = width - distance(plane)
-            for row in range(-extra, ROWS + extra):
-                found.append((plane, row))
-        return found
-
-    first_slot = {key: slot for slot, key in enumerate(cells(2))}
-    second_slot = {key: slot for slot, key in enumerate(cells(1))}
-
-    def k1(plane, row):
-        return first_ref[row_of(first_slot[(plane, row)]), :]
-
-    def k2(plane, row):
-        return second_ref[row_of(second_slot[(plane, row)]), :]
-
-    def apply(field, plane, row):
+    def k1(self, plane, row):
+        early = (plane, row) in FIRST_EARLY
+        slot = (FIRST_EARLY if early else FIRST_LATE)[(plane, row)]
+        return self.first[0 if early else 1][row_of(slot), :]
+
+    def k2(self, plane, row):
+        early = (plane, row) in SECOND_EARLY
+        slot = (SECOND_EARLY if early else SECOND_LATE)[(plane, row)]
+        return self.second[0 if early else 1][row_of(slot), :]
+
+    def apply(self, field, plane, row):
         center = field(plane, row)
         beside = field(plane - 1, row) + field(plane + 1, row)
         beside = beside + (field(plane, row - 1) + field(plane, row + 1))
         beside = beside + (pltpu.roll(center, 1, 1) + pltpu.roll(center, LANES - 1, 1))
-        return factor(plane, row) * center - beside
-
-    def keep(order, plane, row, value):
+        return self.factor(plane, row) * center - beside
+
+    def keep(self, order, plane, row, value):
+        if distance(plane) > 0 or not 0 <= row < ROWS:
+            return
         columns = pl.ds((plane * ROWS + row) * LANES, LANES)
         upper = value.astype(BF16)
-        split_out[row_of(order), columns] = upper
+        self.split[row_of(order), columns] = upper
         if order == 0:
-            split_out[row_of(4), columns] = jnp.zeros_like(upper)
+            self.split[row_of(4), columns] = jnp.zeros_like(upper)
         else:
-            split_out[row_of(order + 4), columns] = (value - upper.astype(F32)).astype(BF16)
-
+            self.split[row_of(order + 4), columns] = (value - upper.astype(F32)).astype(BF16)
+
+    def fill(self, early):
+        side = 0 if early else 1
+        for (plane, row), slot in (FIRST_EARLY if early else FIRST_LATE).items():
+            value = self.apply(self.k0, plane, row)
+            self.first[side][row_of(slot), :] = value
+            self.keep(1, plane, row, value)
+        for (plane, row), slot in (SECOND_EARLY if early else SECOND_LATE).items():
+            value = self.apply(self.k1, plane, row) - B0 * self.k0(plane, row)
+            self.second[side][row_of(slot), :] = value
+            self.keep(2, plane, row, value)
+
+
+def early_kernel(own_ref, high_ref, low_ref, near_ref, beside_ref, split_ref, first_ref, second_ref):
+    fields = Fields(
+        own_ref, high_ref, low_ref, near_ref, beside_ref, None, None, (first_ref, None), (second_ref, None), split_ref
+    )
     for plane, row in cells(0):
-        keep(0, plane, row, k0(plane, row))
-    for plane, row in cells(2):
-        value = apply(k0, plane, row)
-        first_ref[row_of(first_slot[(plane, row)]), :] = value
-        if distance(plane) == 0 and 0 <= row < ROWS:
-            keep(1, plane, row, value)
-    for plane, row in cells(1):
-        value = apply(k1, plane, row) - B0 * k0(plane, row)
-        second_ref[row_of(second_slot[(plane, row)]), :] = value
-        if distance(plane) == 0 and 0 <= row < ROWS:
-            keep(2, plane, row, value)
+        fields.keep(0, plane, row, fields.k0(plane, row))
+    fields.fill(True)
+
+
+def late_kernel(
+    own_ref, high_ref, low_ref, near_ref, beside_ref, corner_ref, cross_ref, first_ref, second_ref, split_in,
+    split_ref, gram_ref, first_late, second_late,
+):
+    fields = Fields(
+        own_ref, high_ref, low_ref, near_ref, beside_ref, corner_ref, cross_ref,
+        (first_ref, first_late), (second_ref, second_late), split_ref,
+    )
+    fields.fill(False)
     for plane, row in cells(0):
-        keep(3, plane, row, apply(k2, plane, row) - B1 * k1(plane, row))
-    split = split_out[...]
+        fields.keep(3, plane, row, fields.apply(fields.k2, plane, row) - B1 * fields.k1(plane, row))
+    split = split_ref[...]
     left = jnp.concatenate([split[:PROBES], split[3 * PROBES : 4 * PROBES], split[7 * PROBES :]], 0)
     product = nt_dot(left, split)
     product = product[:, :LANES] + product[:, LANES:]
     gram_ref[...] = packed(product[:PROBES], product[PROBES : 2 * PROBES] + product[2 * PROBES :])
 
 
-def basis(*operands):
-    width = CELLS * LANES
+def basis_early(*operands):
     return pl.pallas_call(
-        basis_kernel,
-        out_shape=(shaped(8 * PROBES, width, dtype=BF16), shaped(PROBES, LANES)),
+        early_kernel,
+        out_shape=(
+            shaped(8 * PROBES, CELLS * LANES, dtype=BF16),
+            shaped(len(FIRST_EARLY) * PROBES, LANES),
+            shaped(len(SECOND_EARLY) * PROBES, LANES),
+        ),
+        in_specs=vmem_specs(len(operands)),
+        out_specs=tuple(vmem_specs(3)),
+        compiler_params=pltpu.CompilerParams(vmem_limit_bytes=VMEM_LIMIT),
+        interpret=INTERPRET,
+        name="basis_early",
+    )(*held(*operands))
+
+
+def basis_late(*operands):
+    return pl.pallas_call(
+        late_kernel,
+        out_shape=(shaped(8 * PROBES, CELLS * LANES, dtype=BF16), shaped(PROBES, LANES)),
         in_specs=vmem_specs(len(operands)),
         out_specs=tuple(vmem_specs(2)),
-        scratch_shapes=[pltpu.VMEM((108 * PROBES, LANES), F32), pltpu.VMEM((68 * PROBES, LANES), F32)],
+        scratch_shapes=[
+            pltpu.VMEM((len(FIRST_LATE) * PROBES, LANES), F32),
+            pltpu.VMEM((len(SECOND_LATE) * PROBES, LANES), F32),
+        ],
+        input_output_aliases={len(operands) - 1: 0},
         compiler_params=pltpu.CompilerParams(vmem_limit_bytes=VMEM_LIMIT),
         interpret=INTERPRET,
-        name="basis",
+        name="basis_late",
     )(*held(*operands))
 
 
@@ -515,7 +575,8 @@
     corner = off_chip(corner_message)
     cross_message = pack(1, 0, high, low, near)
     cross = on_chip(cross_message)
-    split, gram = basis(own, high, low, near, beside, corner, cross)
+    split, first, second = basis_early(own, high, low, near, beside)
+    split, gram = basis_late(own, high, low, near, beside, corner, cross, first, second, split)
     alphas, betas, following = finish(reduced(gram), split)
     return (alphas, betas, following.reshape(PROBES, PLANES, ROWS, LANES))
 

time: 85.4 us -> 84.7 us (level)
  waiting for transfers between devices: 3.36 us -> 2.43 us
    ppermute x2, waiting for transfers between devices: 1.33 us -> 0.4 us  [off_chip(): lax.ppermute(x, GX, [(i, (i - 1 if i % 2 == 0 else i + 1) % count) for i...]
    pallas_call x1 -> x2, Pallas kernels: 2.63 us -> 2.78 us  [the longest x1 1.86 us: basis_late(): pl.pallas_call(late_kernel, out_shape=(shaped(8 * PROBES, CELLS * LANES,...]
  transfers between devices with their start and end apart: 6 -> 6, of which waited for: 2 -> 2; matrix products, arithmetic and copies ran while one was open for 0% -> 0% of each run, Pallas kernels for 0% -> 1%
where the time goes in v8:
time: 84.7 us; the launch traced here: 84.2 us
  blocking collectives  41.8 us (49%)
  starting transfers between devices  30.1 us (36%)
  Pallas kernels  9.07 us (11%)
  waiting for transfers between devices  2.43 us (3%)
    all_to_all x3, blocking collectives, exchanged(): return lax.all_to_all(x, axes, 0, 0, tiled=True)  41.8 us
    ppermute x2, starting transfers between devices, on_chip(): return lax.ppermute(x, CORE, [(i, count - 1 - i) for i in range(count)])  12.5 us
    ppermute x2, starting transfers between devices, row_pair(): return lax.ppermute(x, GY, [(i, step(i) % count) for i in range(count)])  11.1 us
    ppermute x2, starting transfers between devices, off_chip(): lax.ppermute(x, GX, [(i, (i - 1 if i % 2 == 0 else i + 1) % count) for i...  6.46 us
    pallas_call x1, Pallas kernels, finish(): pl.pallas_call(finish_kernel, out_shape=(jax.ShapeDtypeStruct((3, PROBES,...  4.89 us
    ppermute x2, waiting for transfers between devices, row_pair(): return lax.ppermute(x, GY, [(i, step(i) % count) for i in range(count)])  2.03 us
    pallas_call x1, Pallas kernels, basis_late(): pl.pallas_call(late_kernel, out_shape=(shaped(8 * PROBES, CELLS * LANES,...  1.86 us
  transfers between devices with their start and end apart: 6, of which 2 were waited for; matrix products, arithmetic and copies ran while one was open for 0% of the time, Pallas kernels for 1%

profile of v8, /device:TPU:1, one launch (start us, length us, event | category | flops | bytes accessed | tf_op | source)
XLA Modules:
  0.0 84.2 jit_solution(3133875373797886738)
XLA Ops:
  0.6 1.4 %prepare.1 = (f32[1056,128]{1,0:T(8,128)S(1)}, f32[200,128]{1,0:T(8,128)S(1)}, f32[200,128]{1,0:T(8,128)S(1)}) custom-call(s32[1024,128]{1,0:T(8,128)} %bitcast.7, f32[32,128]{1,0:T(8,128)} %bitcast.8), custom_call_target="tpu_custom_call" | custom-call | tf_op jit(solution)/shard_map/prepare/pallas_call | solution.py:107
  2.0 8.7 %collective-permute-start.3 = (f32[1056,128]{1,0:T(8,128)S(1)}, f32[1056,128]{1,0:T(8,128)S(1)}, u32[]{:S(2)}, u32[]{:S(2)}) collective-permute-start(f32[1056,128]{1,0:T(8,128)S(1)} %get-tuple-element.14.own_ref), channel_id=1, source_target_pairs={{0,16},{16,0},{1,17},{17,1},{2,18},{18,2},{3,19},{19,3},{4,20},{20... | collective-permute-start | bytes 1622024 | tf_op jit(solution)/shard_map/ppermute | solution.py:542
  10.7 1.9 %collective-permute-start.2 = (f32[1056,128]{1,0:T(8,128)S(1)}, f32[1056,128]{1,0:T(8,128)S(1)}, u32[]{:S(2)}, u32[]{:S(2)}) collective-permute-start(f32[1056,128]{1,0:T(8,128)S(1)} %get-tuple-element.14.own_ref), channel_id=1, source_target_pairs={{0,496},{16,32},{32,16},{48,64},{64,48},{80,96},{96,80},{112,128},... | collective-permute-start | bytes 1622024 | tf_op jit(solution)/shard_map/ppermute | solution.py:537
  12.7 1.9 %collective-permute-start = (f32[200,128]{1,0:T(8,128)S(1)}, f32[200,128]{1,0:T(8,128)S(1)}, u32[]{:S(2)}, u32[]{:S(2)}) collective-permute-start(f32[200,128]{1,0:T(8,128)S(1)} %get-tuple-element.15), channel_id=1, source_target_pairs={{0,1},{1,0},{2,3},{3,2},{4,5},{5,4},{6,7},{7,6},{8,9},{9,8},{10,11... | collective-permute-start | bytes 307208 | tf_op jit(solution)/shard_map/ppermute | solution.py:548
  14.6 9.2 %collective-permute-start.1 = (f32[200,128]{1,0:T(8,128)S(1)}, f32[200,128]{1,0:T(8,128)S(1)}, u32[]{:S(2)}, u32[]{:S(2)}) collective-permute-start(f32[200,128]{1,0:T(8,128)S(1)} %get-tuple-element.16), channel_id=1, source_target_pairs={{0,15},{1,2},{2,1},{3,4},{4,3},{5,6},{6,5},{7,8},{8,7},{9,10},{10,... | collective-permute-start | bytes 307208 | tf_op jit(solution)/shard_map/ppermute | solution.py:548
  23.8 0.0 collective-permute-done.high_ref
  23.8 2.0 %collective-permute-done.1.low_ref = f32[200,128]{1,0:T(8,128)S(1)} collective-permute-done((f32[200,128]{1,0:T(8,128)S(1)}, f32[200,128]{1,0:T(8,128)S(1)}, u32[]{:S(2)}, u32[]{:S(2)}) %collective-permute-start.1) | collective-permute-done | bytes 102432 | tf_op jit(solution)/shard_map/ppermute | solution.py:548
  25.8 0.0 collective-permute-done.3.across_ref.beside_ref
  25.9 4.5 %collective-permute-start.4 = (f32[712,128]{1,0:T(8,128)S(1)}, f32[712,128]{1,0:T(8,128)S(1)}, u32[]{:S(2)}, u32[]{:S(2)}) collective-permute-start(f32[712,128]{1,0:T(8,128)S(1)} %shard_map.49), channel_id=1, source_target_pairs={{0,496},{16,32},{32,16},{48,64},{64,48},{80,96},{96,80},{112,128},... | collective-permute-start | bytes 1093640 | tf_op jit(solution)/shard_map/ppermute | solution.py:537
  30.4 0.0 collective-permute-done.2.across_ref.near_ref
  30.4 3.8 %collective-permute-start.5 = (f32[712,128]{1,0:T(8,128)S(1)}, f32[712,128]{1,0:T(8,128)S(1)}, u32[]{:S(2)}, u32[]{:S(2)}) collective-permute-start(f32[712,128]{1,0:T(8,128)S(1)} %shard_map.50), channel_id=1, source_target_pairs={{0,16},{16,0},{1,17},{17,1},{2,18},{18,2},{3,19},{19,3},{4,20},{20... | collective-permute-start | bytes 1093640 | tf_op jit(solution)/shard_map/ppermute | solution.py:542
  34.2 0.9 %basis_early.1 = (bf16[256,4096]{1,0:T(8,128)(2,1)S(1)}, f32[1920,128]{1,0:T(8,128)S(1)}, f32[896,128]{1,0:T(8,128)S(1)}) custom-call(f32[1056,128]{1,0:T(8,128)S(1)} %get-tuple-element.14.own_ref, f32[200,128]{1,0:T(8,128)S(1)} %collective-permute-done.high_ref, f32[200,128]{1,0:T(8,128)S(1)} %collective-permute-done.1.low_ref, ...), custom_call_target="tpu_custom_call" | custom-call | tf_op jit(solution)/shard_map/basis_early/pallas_call | solution.py:335
  35.1 0.4 collective-permute-done.4.corner_ref
  35.5 0.0 collective-permute-done.5.cross_ref
  35.5 1.9 %basis_late.1 = (bf16[256,4096]{1,0:T(8,128)(2,1)S(1)}, f32[32,128]{1,0:T(8,128)S(1)}) custom-call(f32[1056,128]{1,0:T(8,128)S(1)} %get-tuple-element.14.own_ref, f32[200,128]{1,0:T(8,128)S(1)} %collective-permute-done.high_ref, f32[200,128]{1,0:T(8,128)S(1)} %collective-permute-done.1.low_ref, ...), custom_call_target="tpu_custom_call", output_to_operand_aliasing={{0}: (9, {})} | custom-call | tf_op jit(solution)/shard_map/basis_late/pallas_call | solution.py:351
  37.4 12.9 %all_to_all.15 = f32[8,4,128]{2,1,0:T(4,128)S(1)} all-to-all(f32[8,4,128]{2,1,0:T(4,128)S(1)} %bitcast.6), channel_id=1, replica_groups=mesh['gx_0'=2,'gx_1'=8,'gx_2'=2,'gy_0'=8,'gy_1'=2] {'gx_0','gx_2','gy_1'}, dimensions={0} | all-to-all | bytes 32768 | tf_op jit(solution)/shard_map/all_to_all | solution.py:552
  50.4 19.6 %all_to_all.16 = f32[64,4,128]{2,1,0:T(4,128)S(1)} all-to-all(f32[64,4,128]{2,1,0:T(4,128)S(1)} %broadcast_in_dim.4), channel_id=1, replica_groups=mesh['gx_0'=2,'gx_1'=8,'gx_2'=2,'gy_0'=8,'gy_1'=2] {'gx_1','gy_0'}, dimensions={0} | all-to-all | bytes 262144 | tf_op jit(solution)/shard_map/all_to_all | solution.py:552
  69.9 0.1 reduce_sum.19
  70.0 9.3 %all_to_all.17 = f32[8,4,128]{2,1,0:T(4,128)S(1)} all-to-all(f32[8,4,128]{2,1,0:T(4,128)S(1)} %broadcast_in_dim.5), channel_id=1, replica_groups=mesh['gx_0'=2,'gx_1'=8,'gx_2'=2,'gy_0'=8,'gy_1'=2] {'gx_0','gx_2','gy_1'}, dimensions={0} | all-to-all | bytes 32768 | tf_op jit(solution)/shard_map/all_to_all | solution.py:552
  79.3 4.9 %finish.1 = (f32[3,32,32]{2,1,0:T(8,128)}, f32[3,32,32]{2,1,0:T(8,128)}, f32[32,32,128]{2,1,0:T(8,128)}) custom-call(f32[32,128]{1,0:T(8,128)S(1)} %bitcast.5, bf16[256,4096]{1,0:T(8,128)(2,1)S(1)} %get-tuple-element.21.split_ref), custom_call_target="tpu_custom_call" | custom-call | tf_op jit(solution)/shard_map/finish/pallas_call | solution.py:513
  (5 shorter events, 0.1 us)
Async XLA Ops:
  2.0 23.8 %collective-permute-start.3 = (f32[1056,128]{1,0:T(8,128)S(1)}, f32[1056,128]{1,0:T(8,128)S(1)}, u32[]{:S(2)}, u32[]{:S(2)}) collective-permute-start(f32[1056,128]{1,0:T(8,128)S(1)} %get-tuple-element.14.own_ref), channel_id=1, source_target_pairs={{0,16},{16,0},{1,17},{17,1},{2,18},{18,2},{3,19},{19,3},{4,20},{20... | collective-permute-start | bytes 1622024 | tf_op jit(solution)/shard_map/ppermute | solution.py:542
  10.7 19.7 %collective-permute-start.2 = (f32[1056,128]{1,0:T(8,128)S(1)}, f32[1056,128]{1,0:T(8,128)S(1)}, u32[]{:S(2)}, u32[]{:S(2)}) collective-permute-start(f32[1056,128]{1,0:T(8,128)S(1)} %get-tuple-element.14.own_ref), channel_id=1, source_target_pairs={{0,496},{16,32},{32,16},{48,64},{64,48},{80,96},{96,80},{112,128},... | collective-permute-start | bytes 1622024 | tf_op jit(solution)/shard_map/ppermute | solution.py:537
  12.7 11.1 %collective-permute-start = (f32[200,128]{1,0:T(8,128)S(1)}, f32[200,128]{1,0:T(8,128)S(1)}, u32[]{:S(2)}, u32[]{:S(2)}) collective-permute-start(f32[200,128]{1,0:T(8,128)S(1)} %get-tuple-element.15), channel_id=1, source_target_pairs={{0,1},{1,0},{2,3},{3,2},{4,5},{5,4},{6,7},{7,6},{8,9},{9,8},{10,11... | collective-permute-start | bytes 307208 | tf_op jit(solution)/shard_map/ppermute | solution.py:548
  14.6 11.2 %collective-permute-start.1 = (f32[200,128]{1,0:T(8,128)S(1)}, f32[200,128]{1,0:T(8,128)S(1)}, u32[]{:S(2)}, u32[]{:S(2)}) collective-permute-start(f32[200,128]{1,0:T(8,128)S(1)} %get-tuple-element.16), channel_id=1, source_target_pairs={{0,15},{1,2},{2,1},{3,4},{4,3},{5,6},{6,5},{7,8},{8,7},{9,10},{10,... | collective-permute-start | bytes 307208 | tf_op jit(solution)/shard_map/ppermute | solution.py:548
  25.9 9.7 %collective-permute-start.4 = (f32[712,128]{1,0:T(8,128)S(1)}, f32[712,128]{1,0:T(8,128)S(1)}, u32[]{:S(2)}, u32[]{:S(2)}) collective-permute-start(f32[712,128]{1,0:T(8,128)S(1)} %shard_map.49), channel_id=1, source_target_pairs={{0,496},{16,32},{32,16},{48,64},{64,48},{80,96},{96,80},{112,128},... | collective-permute-start | bytes 1093640 | tf_op jit(solution)/shard_map/ppermute | solution.py:537
  30.4 5.1 %collective-permute-start.5 = (f32[712,128]{1,0:T(8,128)S(1)}, f32[712,128]{1,0:T(8,128)S(1)}, u32[]{:S(2)}, u32[]{:S(2)}) collective-permute-start(f32[712,128]{1,0:T(8,128)S(1)} %shard_map.50), channel_id=1, source_target_pairs={{0,16},{16,0},{1,17},{17,1},{2,18},{18,2},{3,19},{19,3},{4,20},{20... | collective-permute-start | bytes 1093640 | tf_op jit(solution)/shard_map/ppermute | solution.py:542

commit v9 on v8

--- a/solution.py
+++ b/solution.py
@@ -304,12 +304,28 @@
             self.keep(2, plane, row, value)
 
 
-def early_kernel(own_ref, high_ref, low_ref, near_ref, beside_ref, split_ref, first_ref, second_ref):
+def start_kernel(own_ref, split_ref):
+    fields = Fields(own_ref, None, None, None, None, None, None, None, None, split_ref)
+    for plane, row in cells(0):
+        fields.keep(0, plane, row, fields.k0(plane, row))
+
+
+def basis_start(own):
+    return pl.pallas_call(
+        start_kernel,
+        out_shape=shaped(8 * PROBES, CELLS * LANES, dtype=BF16),
+        in_specs=vmem_specs(1),
+        out_specs=vmem_specs(1)[0],
+        compiler_params=pltpu.CompilerParams(vmem_limit_bytes=VMEM_LIMIT),
+        interpret=INTERPRET,
+        name="basis_start",
+    )(*held(own))
+
+
+def early_kernel(own_ref, high_ref, low_ref, near_ref, beside_ref, split_in, split_ref, first_ref, second_ref):
     fields = Fields(
         own_ref, high_ref, low_ref, near_ref, beside_ref, None, None, (first_ref, None), (second_ref, None), split_ref
     )
-    for plane, row in cells(0):
-        fields.keep(0, plane, row, fields.k0(plane, row))
     fields.fill(True)
 
 
@@ -341,6 +357,7 @@
         ),
         in_specs=vmem_specs(len(operands)),
         out_specs=tuple(vmem_specs(3)),
+        input_output_aliases={len(operands) - 1: 0},
         compiler_params=pltpu.CompilerParams(vmem_limit_bytes=VMEM_LIMIT),
         interpret=INTERPRET,
         name="basis_early",
@@ -571,11 +588,12 @@
     low = row_pair(bottom, 1)
     near = off_chip(own)
     beside = on_chip(own)
+    split = basis_start(own)
     corner_message = pack(0, ROWS, high, low, beside)
     corner = off_chip(corner_message)
     cross_message = pack(1, 0, high, low, near)
     cross = on_chip(cross_message)
-    split, first, second = basis_early(own, high, low, near, beside)
+    split, first, second = basis_early(own, high, low, near, beside, split)
     split, gram = basis_late(own, high, low, near, beside, corner, cross, first, second, split)
     alphas, betas, following = finish(reduced(gram), split)
     return (alphas, betas, following.reshape(PROBES, PLANES, ROWS, LANES))

time: 84.7 us -> 84.6 us (level)
  no operation moved by 1% of the time
where the time goes in v9:
time: 84.6 us; the launch traced here: 84.2 us
  blocking collectives  41.8 us (49%)
  starting transfers between devices  30.1 us (36%)
  Pallas kernels  9 us (11%)
  waiting for transfers between devices  2.46 us (3%)
    all_to_all x3, blocking collectives, exchanged(): return lax.all_to_all(x, axes, 0, 0, tiled=True)  41.8 us
    ppermute x2, starting transfers between devices, on_chip(): return lax.ppermute(x, CORE, [(i, count - 1 - i) for i in range(count)])  12.5 us
    ppermute x2, starting transfers between devices, row_pair(): return lax.ppermute(x, GY, [(i, step(i) % count) for i in range(count)])  11.1 us
    ppermute x2, starting transfers between devices, off_chip(): lax.ppermute(x, GX, [(i, (i - 1 if i % 2 == 0 else i + 1) % count) for i...  6.46 us
    pallas_call x1, Pallas kernels, finish(): pl.pallas_call(finish_kernel, out_shape=(jax.ShapeDtypeStruct((3, PROBES,...  4.89 us
    ppermute x2, waiting for transfers between devices, row_pair(): return lax.ppermute(x, GY, [(i, step(i) % count) for i in range(count)])  2.03 us
    pallas_call x1, Pallas kernels, basis_late(): pl.pallas_call(late_kernel, out_shape=(shaped(8 * PROBES, CELLS * LANES,...  1.82 us
  transfers between devices with their start and end apart: 6, of which 2 were waited for; matrix products, arithmetic and copies ran while one was open for 0% of the time, Pallas kernels for 1%

profile of v9, /device:TPU:1, one launch (start us, length us, event | category | flops | bytes accessed | tf_op | source)
XLA Modules:
  0.0 84.2 jit_solution(7600031252861513910)
XLA Ops:
  0.6 1.4 %prepare.1 = (f32[1056,128]{1,0:T(8,128)S(1)}, f32[200,128]{1,0:T(8,128)S(1)}, f32[200,128]{1,0:T(8,128)S(1)}) custom-call(s32[1024,128]{1,0:T(8,128)} %bitcast.7, f32[32,128]{1,0:T(8,128)} %bitcast.8), custom_call_target="tpu_custom_call" | custom-call | tf_op jit(solution)/shard_map/prepare/pallas_call | solution.py:107
  2.0 8.7 %collective-permute-start.3 = (f32[1056,128]{1,0:T(8,128)S(1)}, f32[1056,128]{1,0:T(8,128)S(1)}, u32[]{:S(2)}, u32[]{:S(2)}) collective-permute-start(f32[1056,128]{1,0:T(8,128)S(1)} %get-tuple-element.14.own_ref), channel_id=1, source_target_pairs={{0,16},{16,0},{1,17},{17,1},{2,18},{18,2},{3,19},{19,3},{4,20},{20... | collective-permute-start | bytes 1622024 | tf_op jit(solution)/shard_map/ppermute | solution.py:559
  10.7 1.9 %collective-permute-start.2 = (f32[1056,128]{1,0:T(8,128)S(1)}, f32[1056,128]{1,0:T(8,128)S(1)}, u32[]{:S(2)}, u32[]{:S(2)}) collective-permute-start(f32[1056,128]{1,0:T(8,128)S(1)} %get-tuple-element.14.own_ref), channel_id=1, source_target_pairs={{0,496},{16,32},{32,16},{48,64},{64,48},{80,96},{96,80},{112,128},... | collective-permute-start | bytes 1622024 | tf_op jit(solution)/shard_map/ppermute | solution.py:554
  12.7 1.9 %collective-permute-start = (f32[200,128]{1,0:T(8,128)S(1)}, f32[200,128]{1,0:T(8,128)S(1)}, u32[]{:S(2)}, u32[]{:S(2)}) collective-permute-start(f32[200,128]{1,0:T(8,128)S(1)} %get-tuple-element.15), channel_id=1, source_target_pairs={{0,1},{1,0},{2,3},{3,2},{4,5},{5,4},{6,7},{7,6},{8,9},{9,8},{10,11... | collective-permute-start | bytes 307208 | tf_op jit(solution)/shard_map/ppermute | solution.py:565
  14.6 9.2 %collective-permute-start.1 = (f32[200,128]{1,0:T(8,128)S(1)}, f32[200,128]{1,0:T(8,128)S(1)}, u32[]{:S(2)}, u32[]{:S(2)}) collective-permute-start(f32[200,128]{1,0:T(8,128)S(1)} %get-tuple-element.16), channel_id=1, source_target_pairs={{0,15},{1,2},{2,1},{3,4},{4,3},{5,6},{6,5},{7,8},{8,7},{9,10},{10,... | collective-permute-start | bytes 307208 | tf_op jit(solution)/shard_map/ppermute | solution.py:565
  23.8 0.0 collective-permute-done.high_ref
  23.8 2.0 %collective-permute-done.1.low_ref = f32[200,128]{1,0:T(8,128)S(1)} collective-permute-done((f32[200,128]{1,0:T(8,128)S(1)}, f32[200,128]{1,0:T(8,128)S(1)}, u32[]{:S(2)}, u32[]{:S(2)}) %collective-permute-start.1) | collective-permute-done | bytes 102432 | tf_op jit(solution)/shard_map/ppermute | solution.py:565
  25.8 0.0 collective-permute-done.3.across_ref.beside_ref
  25.9 4.5 %collective-permute-start.4 = (f32[712,128]{1,0:T(8,128)S(1)}, f32[712,128]{1,0:T(8,128)S(1)}, u32[]{:S(2)}, u32[]{:S(2)}) collective-permute-start(f32[712,128]{1,0:T(8,128)S(1)} %shard_map.49), channel_id=1, source_target_pairs={{0,496},{16,32},{32,16},{48,64},{64,48},{80,96},{96,80},{112,128},... | collective-permute-start | bytes 1093640 | tf_op jit(solution)/shard_map/ppermute | solution.py:554
  30.4 0.0 collective-permute-done.2.across_ref.near_ref
  30.4 3.8 %collective-permute-start.5 = (f32[712,128]{1,0:T(8,128)S(1)}, f32[712,128]{1,0:T(8,128)S(1)}, u32[]{:S(2)}, u32[]{:S(2)}) collective-permute-start(f32[712,128]{1,0:T(8,128)S(1)} %shard_map.50), channel_id=1, source_target_pairs={{0,16},{16,0},{1,17},{17,1},{2,18},{18,2},{3,19},{19,3},{4,20},{20... | collective-permute-start | bytes 1093640 | tf_op jit(solution)/shard_map/ppermute | solution.py:559
  34.2 0.1 basis_start.1.split_in
  34.3 0.8 basis_early.1
  35.1 0.4 collective-permute-done.4.corner_ref
  35.5 0.0 collective-permute-done.5.cross_ref
  35.5 1.8 %basis_late.1 = (bf16[256,4096]{1,0:T(8,128)(2,1)S(1)}, f32[32,128]{1,0:T(8,128)S(1)}) custom-call(f32[1056,128]{1,0:T(8,128)S(1)} %get-tuple-element.14.own_ref, f32[200,128]{1,0:T(8,128)S(1)} %collective-permute-done.high_ref, f32[200,128]{1,0:T(8,128)S(1)} %collective-permute-done.1.low_ref, ...), custom_call_target="tpu_custom_call", output_to_operand_aliasing={{0}: (9, {})} | custom-call | tf_op jit(solution)/shard_map/basis_late/pallas_call | solution.py:368
  37.4 12.9 %all_to_all.15 = f32[8,4,128]{2,1,0:T(4,128)S(1)} all-to-all(f32[8,4,128]{2,1,0:T(4,128)S(1)} %bitcast.6), channel_id=1, replica_groups=mesh['gx_0'=2,'gx_1'=8,'gx_2'=2,'gy_0'=8,'gy_1'=2] {'gx_0','gx_2','gy_1'}, dimensions={0} | all-to-all | bytes 32768 | tf_op jit(solution)/shard_map/all_to_all | solution.py:569
  50.3 19.6 %all_to_all.16 = f32[64,4,128]{2,1,0:T(4,128)S(1)} all-to-all(f32[64,4,128]{2,1,0:T(4,128)S(1)} %broadcast_in_dim.4), channel_id=1, replica_groups=mesh['gx_0'=2,'gx_1'=8,'gx_2'=2,'gy_0'=8,'gy_1'=2] {'gx_1','gy_0'}, dimensions={0} | all-to-all | bytes 262144 | tf_op jit(solution)/shard_map/all_to_all | solution.py:569
  69.9 0.1 reduce_sum.19
  70.0 9.3 %all_to_all.17 = f32[8,4,128]{2,1,0:T(4,128)S(1)} all-to-all(f32[8,4,128]{2,1,0:T(4,128)S(1)} %broadcast_in_dim.5), channel_id=1, replica_groups=mesh['gx_0'=2,'gx_1'=8,'gx_2'=2,'gy_0'=8,'gy_1'=2] {'gx_0','gx_2','gy_1'}, dimensions={0} | all-to-all | bytes 32768 | tf_op jit(solution)/shard_map/all_to_all | solution.py:569
  79.3 4.9 %finish.1 = (f32[3,32,32]{2,1,0:T(8,128)}, f32[3,32,32]{2,1,0:T(8,128)}, f32[32,32,128]{2,1,0:T(8,128)}) custom-call(f32[32,128]{1,0:T(8,128)S(1)} %bitcast.5, bf16[256,4096]{1,0:T(8,128)(2,1)S(1)} %get-tuple-element.21.split_ref), custom_call_target="tpu_custom_call" | custom-call | tf_op jit(solution)/shard_map/finish/pallas_call | solution.py:530
  (5 shorter events, 0.1 us)
Async XLA Ops:
  2.0 23.8 %collective-permute-start.3 = (f32[1056,128]{1,0:T(8,128)S(1)}, f32[1056,128]{1,0:T(8,128)S(1)}, u32[]{:S(2)}, u32[]{:S(2)}) collective-permute-start(f32[1056,128]{1,0:T(8,128)S(1)} %get-tuple-element.14.own_ref), channel_id=1, source_target_pairs={{0,16},{16,0},{1,17},{17,1},{2,18},{18,2},{3,19},{19,3},{4,20},{20... | collective-permute-start | bytes 1622024 | tf_op jit(solution)/shard_map/ppermute | solution.py:559
  10.7 19.7 %collective-permute-start.2 = (f32[1056,128]{1,0:T(8,128)S(1)}, f32[1056,128]{1,0:T(8,128)S(1)}, u32[]{:S(2)}, u32[]{:S(2)}) collective-permute-start(f32[1056,128]{1,0:T(8,128)S(1)} %get-tuple-element.14.own_ref), channel_id=1, source_target_pairs={{0,496},{16,32},{32,16},{48,64},{64,48},{80,96},{96,80},{112,128},... | collective-permute-start | bytes 1622024 | tf_op jit(solution)/shard_map/ppermute | solution.py:554
  12.7 11.1 %collective-permute-start = (f32[200,128]{1,0:T(8,128)S(1)}, f32[200,128]{1,0:T(8,128)S(1)}, u32[]{:S(2)}, u32[]{:S(2)}) collective-permute-start(f32[200,128]{1,0:T(8,128)S(1)} %get-tuple-element.15), channel_id=1, source_target_pairs={{0,1},{1,0},{2,3},{3,2},{4,5},{5,4},{6,7},{7,6},{8,9},{9,8},{10,11... | collective-permute-start | bytes 307208 | tf_op jit(solution)/shard_map/ppermute | solution.py:565
  14.6 11.2 %collective-permute-start.1 = (f32[200,128]{1,0:T(8,128)S(1)}, f32[200,128]{1,0:T(8,128)S(1)}, u32[]{:S(2)}, u32[]{:S(2)}) collective-permute-start(f32[200,128]{1,0:T(8,128)S(1)} %get-tuple-element.16), channel_id=1, source_target_pairs={{0,15},{1,2},{2,1},{3,4},{4,3},{5,6},{6,5},{7,8},{8,7},{9,10},{10,... | collective-permute-start | bytes 307208 | tf_op jit(solution)/shard_map/ppermute | solution.py:565
  25.9 9.7 %collective-permute-start.4 = (f32[712,128]{1,0:T(8,128)S(1)}, f32[712,128]{1,0:T(8,128)S(1)}, u32[]{:S(2)}, u32[]{:S(2)}) collective-permute-start(f32[712,128]{1,0:T(8,128)S(1)} %shard_map.49), channel_id=1, source_target_pairs={{0,496},{16,32},{32,16},{48,64},{64,48},{80,96},{96,80},{112,128},... | collective-permute-start | bytes 1093640 | tf_op jit(solution)/shard_map/ppermute | solution.py:554
  30.4 5.1 %collective-permute-start.5 = (f32[712,128]{1,0:T(8,128)S(1)}, f32[712,128]{1,0:T(8,128)S(1)}, u32[]{:S(2)}, u32[]{:S(2)}) collective-permute-start(f32[712,128]{1,0:T(8,128)S(1)} %shard_map.50), channel_id=1, source_target_pairs={{0,16},{16,0},{1,17},{17,1},{2,18},{18,2},{3,19},{19,3},{4,20},{20... | collective-permute-start | bytes 1093640 | tf_op jit(solution)/shard_map/ppermute | solution.py:559
